TPU v7x, 32 devices: a whole 2x2x4 slice. The times are simulated.
32 devices in a mesh: rep: 2 (over x), shard: 16 (over z, y, core).
Axes of the slice: x: 2, y: 2, z: 4, core: 2. Of those that a mesh axis runs over, the one named last changes fastest.
Arguments:
- tokens: bfloat16 [4096, 2048], P(('rep', 'shard')), may hold values from -6 to 6
- segment_ids: int32 [4096], P(('rep', 'shard')), may hold values from -1 to 31, as said below
- cotangent: bfloat16 [4096, 2048], P(('rep', 'shard')), may hold values from -6 to 6
- w_qkv: bfloat16 [2048, 6144], P('shard'), may hold values from -0.125 to 0.125
- w_out: bfloat16 [2048, 2048], P('shard'), may hold values from -0.125 to 0.125
- w_gate_up: bfloat16 [2048, 16384], P('shard'), may hold values from -0.125 to 0.125
- w_down: bfloat16 [8192, 2048], P('shard'), may hold values from -0.0625 to 0.0625
- q_gain: bfloat16 [2048], P('shard'), may hold values from 0.5 to 1.5
- k_gain: bfloat16 [2048], P('shard'), may hold values from 0.5 to 1.5
- attn_gain: bfloat16 [2048], P('shard'), may hold values from 0.5 to 1.5
- mlp_gain: bfloat16 [2048], P('shard'), may hold values from 0.5 to 1.5
Outputs:
- output: bfloat16 [4096, 2048], P(('rep', 'shard'))
- grad_tokens: float32 [4096, 2048], P(('rep', 'shard'))
- grad_qkv: float32 [2048, 6144], P('shard')
- grad_out: float32 [2048, 2048], P('shard')
- grad_gate_up: float32 [2048, 16384], P('shard')
- grad_down: float32 [8192, 2048], P('shard')
- grad_q_gain: float32 [2048], P('shard')
- grad_k_gain: float32 [2048], P('shard')
- grad_attn_gain: float32 [2048], P('shard')
- grad_mlp_gain: float32 [2048], P('shard')
Inputs may be any that keep to these rules, and one draw needn't show every extreme that they name: `segment_ids`: within each block of 128 slots, live slots come first in runs of equal ids numbered upwards from 0 (one packed sequence each), each run starting at a slot whose index within the block is a multiple of 4, then padding slots with id -1; at least one block has no padding and starts a run at every multiple of 4.
All inputs are finite; a program needn't handle non-finite values.
Results may differ from a plain program's by a relative error of at most 0.02.
Values may be sent and summed in bfloat16 or wider, within the bound.
A program may use at most 384 MiB of HBM per device.

v0:
```python
import jax
import jax.numpy as jnp
from jax import lax
from jax.sharding import PartitionSpec as P

H = 16


EPSILON = 1e-06
THETA = 500000.0


def positions(seg_row):
    count = seg_row.shape[0]
    slots = jnp.arange(count, dtype=jnp.int32)
    starts = jnp.concatenate([jnp.ones((1,), jnp.bool_), seg_row[1:] != seg_row[:-1]])
    first = lax.cummax(jnp.where(starts, slots, 0), axis=0)
    return slots - first


def rope_tables(seg_row, head_width):
    half_width = head_width // 2
    spots = positions(seg_row).astype(jnp.float32)
    inverse = THETA ** (-(2.0 * jnp.arange(half_width, dtype=jnp.float32)) / head_width)
    angle = spots[:, None] * inverse[None, :]
    return (jnp.cos(angle), jnp.sin(angle))


def rotate(matrix, cosine, sine, num_heads):
    count, width = matrix.shape
    shaped = matrix.reshape(count, num_heads, width // num_heads)
    half_width = shaped.shape[2] // 2
    first_half = shaped[..., :half_width]
    second_half = shaped[..., half_width:]
    cos_head = cosine[:, None, :]
    sin_head = sine[:, None, :]
    joined = jnp.concatenate(
        [
            first_half * cos_head - second_half * sin_head,
            second_half * cos_head + first_half * sin_head,
        ],
        axis=-1,
    )
    return joined.reshape(count, width)


def allowed(seg_row):
    count = seg_row.shape[0]
    slots = jnp.arange(count)
    return (seg_row[:, None] == seg_row[None, :]) & (slots[None, :] <= slots[:, None])


def norm_forward(vector, gain):
    rscale = lax.rsqrt(jnp.mean(vector * vector, axis=-1, keepdims=True) + EPSILON)
    normed = vector * rscale
    return (normed * gain, normed, rscale)


def norm_backward(upstream, normed, rscale, gain):
    scaled = upstream * gain
    inner = jnp.mean(scaled * normed, axis=-1, keepdims=True)
    return (rscale * (scaled - normed * inner), jnp.sum(upstream * normed, axis=0))


def contract_last(left, right):
    return lax.dot_general(
        left, right, (((1,), (1,)), ((), ())), preferred_element_type=jnp.float32
    )


def contract_first(left, right):
    return lax.dot_general(
        left, right, (((0,), (0,)), ((), ())), preferred_element_type=jnp.float32
    )


def head_split(matrix, num_heads):
    return matrix.reshape(matrix.shape[0], num_heads, -1)


def attention_scores(query_rot, keys_rot, seg_row, num_heads):
    head_width = query_rot.shape[1] // num_heads
    scores = jnp.einsum(
        "thd,shd->hts",
        head_split(query_rot, num_heads),
        head_split(keys_rot, num_heads),
        preferred_element_type=jnp.float32,
    ) * head_width ** (-0.5)
    return jnp.where(allowed(seg_row)[None], scores, -1e30)


def attention_forward(query_rot, keys_rot, values_b, seg_row, num_heads):
    scores = attention_scores(query_rot, keys_rot, seg_row, num_heads)
    top = jnp.max(scores, axis=-1, keepdims=True)
    log_total = top[..., 0] + jnp.log(jnp.sum(jnp.exp(scores - top), axis=-1))
    probs_b = jnp.exp(scores - log_total[..., None]).astype(jnp.bfloat16)
    context = jnp.einsum(
        "hts,shd->thd", probs_b, head_split(values_b, num_heads), preferred_element_type=jnp.float32
    )
    return (context.reshape(query_rot.shape), log_total)


def attention_backward(
    query_rot, keys_rot, values_b, seg_row, log_total, context, d_context_b, num_heads
):
    count, width = query_rot.shape
    head_width = width // num_heads
    scores = attention_scores(query_rot, keys_rot, seg_row, num_heads)
    probs = jnp.exp(scores - log_total[..., None])
    probs_b = probs.astype(jnp.bfloat16)
    d_heads = head_split(d_context_b, num_heads)
    d_values = jnp.einsum("hts,thd->shd", probs_b, d_heads, preferred_element_type=jnp.float32)
    d_probs = jnp.einsum(
        "thd,shd->hts", d_heads, head_split(values_b, num_heads), preferred_element_type=jnp.float32
    )
    delta = jnp.sum(
        d_heads.astype(jnp.float32) * context.reshape(count, num_heads, head_width), axis=-1
    ).T
    d_scores_b = (probs * (d_probs - delta[..., None]) * head_width ** (-0.5)).astype(jnp.bfloat16)
    d_query = jnp.einsum(
        "hts,shd->thd",
        d_scores_b,
        head_split(keys_rot, num_heads),
        preferred_element_type=jnp.float32,
    )
    d_keys = jnp.einsum(
        "hts,thd->shd",
        d_scores_b,
        head_split(query_rot, num_heads),
        preferred_element_type=jnp.float32,
    )
    return (
        d_query.reshape(count, width),
        d_keys.reshape(count, width),
        d_values.reshape(count, width),
    )


def add_block(left, weight_rows):
    return jnp.dot(left, weight_rows, preferred_element_type=jnp.float32)


def fold_gain(left, pieces):
    weight_rows, gain_piece = pieces
    return (add_block(left, weight_rows), gain_piece)


def fold_two_gains(left, pieces):
    weight_rows, first_piece, second_piece = pieces
    return (add_block(left, weight_rows), first_piece, second_piece)


def back_rows(upstream, piece):
    return contract_last(upstream, piece)


def fold_owned(left_rows, upstream_piece):
    return contract_first(left_rows, upstream_piece)


def fold_all_owned(lefts, pieces):
    return tuple((fold_owned(left_rows, piece) for left_rows, piece in zip(lefts, pieces)))


def shards(
    tokens,
    segment_ids,
    cotangent,
    w_qkv,
    w_out,
    w_gate_up,
    w_down,
    q_gain,
    k_gain,
    attn_gain,
    mlp_gain,
):
    count, width = tokens.shape
    ff_width = w_gate_up.shape[1] // 2
    num_heads = H
    cosine, sine = rope_tables(segment_ids, width // num_heads)
    qkv, query_gain_full, keys_gain_full = fold_two_gains(
        tokens,
        (
            lax.all_gather(w_qkv, "shard", axis=0, tiled=True),
            lax.all_gather(q_gain, "shard", axis=0, tiled=True),
            lax.all_gather(k_gain, "shard", axis=0, tiled=True),
        ),
    )
    gain_query = query_gain_full.astype(jnp.float32)
    gain_keys = keys_gain_full.astype(jnp.float32)
    query_norm, query_hat, query_scale = norm_forward(qkv[:, :width], gain_query)
    keys_norm, keys_hat, keys_scale = norm_forward(qkv[:, width : 2 * width], gain_keys)
    query_rot = rotate(query_norm, cosine, sine, num_heads).astype(jnp.bfloat16)
    keys_rot = rotate(keys_norm, cosine, sine, num_heads).astype(jnp.bfloat16)
    values_b = qkv[:, 2 * width :].astype(jnp.bfloat16)
    context, log_total = attention_forward(query_rot, keys_rot, values_b, segment_ids, num_heads)
    context_b = context.astype(jnp.bfloat16)
    attn_raw, attn_gain_full = fold_gain(
        context_b,
        (
            lax.all_gather(w_out, "shard", axis=0, tiled=True),
            lax.all_gather(attn_gain, "shard", axis=0, tiled=True),
        ),
    )
    gain_attn = attn_gain_full.astype(jnp.float32)
    attn_norm, attn_hat, attn_scale = norm_forward(attn_raw, gain_attn)
    resid = tokens.astype(jnp.float32) + attn_norm
    resid_b = resid.astype(jnp.bfloat16)
    gate_up, mlp_gain_full = fold_gain(
        resid_b,
        (
            lax.all_gather(w_gate_up, "shard", axis=0, tiled=True),
            lax.all_gather(mlp_gain, "shard", axis=0, tiled=True),
        ),
    )
    gain_mlp = mlp_gain_full.astype(jnp.float32)
    gate_raw = gate_up[:, :ff_width]
    up_raw = gate_up[:, ff_width:]
    sigma = jax.nn.sigmoid(gate_raw)
    activated = gate_raw * sigma
    mixed_b = (activated * up_raw).astype(jnp.bfloat16)
    down_raw = add_block(mixed_b, lax.all_gather(w_down, "shard", axis=0, tiled=True))
    down_norm, down_hat, down_scale = norm_forward(down_raw, gain_mlp)
    output = (resid + down_norm).astype(jnp.bfloat16)
    valid = (segment_ids >= 0).astype(jnp.float32)[:, None]
    d_out = cotangent.astype(jnp.float32) * valid
    d_down, grad_mlp = norm_backward(d_out, down_hat, down_scale, gain_mlp)
    d_down_b = d_down.astype(jnp.bfloat16)
    d_mixed = back_rows(d_down_b, lax.all_gather(w_down, "shard", axis=0, tiled=True))
    d_gate = d_mixed * up_raw * sigma * (1.0 + gate_raw * (1.0 - sigma))
    d_up = d_mixed * activated
    d_gu_b = jnp.concatenate([d_gate, d_up], axis=1).astype(jnp.bfloat16)
    d_resid = d_out + back_rows(d_gu_b, lax.all_gather(w_gate_up, "shard", axis=0, tiled=True))
    d_attn, grad_attn = norm_backward(d_resid, attn_hat, attn_scale, gain_attn)
    d_attn_b = d_attn.astype(jnp.bfloat16)
    out_full, qkv_full = (
        lax.all_gather(w_out, "shard", axis=0, tiled=True),
        lax.all_gather(w_qkv, "shard", axis=0, tiled=True),
    )
    d_context_b = contract_last(d_attn_b, out_full).astype(jnp.bfloat16)
    d_query_rot, d_keys_rot, d_values = attention_backward(
        query_rot, keys_rot, values_b, segment_ids, log_total, context, d_context_b, num_heads
    )
    d_query_norm = rotate(d_query_rot, cosine, -sine, num_heads)
    d_keys_norm = rotate(d_keys_rot, cosine, -sine, num_heads)
    d_query, grad_query = norm_backward(d_query_norm, query_hat, query_scale, gain_query)
    d_keys, grad_keys = norm_backward(d_keys_norm, keys_hat, keys_scale, gain_keys)
    d_qkv_b = jnp.concatenate([d_query, d_keys, d_values], axis=1).astype(jnp.bfloat16)
    grad_tokens = d_resid + contract_last(d_qkv_b, qkv_full)
    mixed_rows, resid_rows, token_rows, context_rows = (
        lax.all_to_all(mixed_b, "shard", split_axis=1, concat_axis=0, tiled=True),
        lax.all_to_all(resid_b, "shard", split_axis=1, concat_axis=0, tiled=True),
        lax.all_to_all(tokens, "shard", split_axis=1, concat_axis=0, tiled=True),
        lax.all_to_all(context_b, "shard", split_axis=1, concat_axis=0, tiled=True),
    )
    grad_down, grad_gate_up, grad_qkv_own, grad_out_own = fold_all_owned(
        (mixed_rows, resid_rows, token_rows, context_rows),
        (
            lax.all_gather(d_down_b, "shard", axis=0, tiled=True),
            lax.all_gather(d_gu_b, "shard", axis=0, tiled=True),
            lax.all_gather(d_qkv_b, "shard", axis=0, tiled=True),
            lax.all_gather(d_attn_b, "shard", axis=0, tiled=True),
        ),
    )
    gains_own = (
        lax.psum_scatter(
            grad_query.astype(jnp.bfloat16), "shard", scatter_dimension=0, tiled=True
        ).astype(jnp.float32),
        lax.psum_scatter(
            grad_keys.astype(jnp.bfloat16), "shard", scatter_dimension=0, tiled=True
        ).astype(jnp.float32),
        lax.psum_scatter(
            grad_attn.astype(jnp.bfloat16), "shard", scatter_dimension=0, tiled=True
        ).astype(jnp.float32),
        lax.psum_scatter(
            grad_mlp.astype(jnp.bfloat16), "shard", scatter_dimension=0, tiled=True
        ).astype(jnp.float32),
    )
    summed = (
        lax.psum(grad_qkv_own.astype(jnp.bfloat16), "rep").astype(jnp.float32),
        lax.psum(grad_out_own.astype(jnp.bfloat16), "rep").astype(jnp.float32),
        lax.psum(grad_gate_up.astype(jnp.bfloat16), "rep").astype(jnp.float32),
        lax.psum(grad_down.astype(jnp.bfloat16), "rep").astype(jnp.float32),
        lax.psum(gains_own[0].astype(jnp.bfloat16), "rep").astype(jnp.float32),
        lax.psum(gains_own[1].astype(jnp.bfloat16), "rep").astype(jnp.float32),
        lax.psum(gains_own[2].astype(jnp.bfloat16), "rep").astype(jnp.float32),
        lax.psum(gains_own[3].astype(jnp.bfloat16), "rep").astype(jnp.float32),
    )
    grad_qkv, grad_out, grad_gu, grad_dn, grad_q, grad_k, grad_a, grad_m = summed
    return (
        output,
        grad_tokens,
        grad_qkv,
        grad_out,
        grad_gu,
        grad_dn,
        grad_q,
        grad_k,
        grad_a,
        grad_m,
    )


def solution(mesh):
    return jax.shard_map(
        shards,
        mesh=mesh,
        in_specs=(
            P(("rep", "shard"), None),
            P(("rep", "shard")),
            P(("rep", "shard"), None),
            P("shard", None),
            P("shard", None),
            P("shard", None),
            P("shard", None),
            P("shard"),
            P("shard"),
            P("shard"),
            P("shard"),
        ),
        out_specs=(
            P(("rep", "shard"), None),
            P(("rep", "shard"), None),
            P("shard", None),
            P("shard", None),
            P("shard", None),
            P("shard", None),
            P("shard"),
            P("shard"),
            P("shard"),
            P("shard"),
        ),
        check_vma=False,
    )
```

profile of v0, /device:TPU:0, one launch (start us, length us, event | category | flops | bytes accessed | tf_op | source)
XLA Modules:
  0.0 1692.9 jit_solution(17944830758551619071)
XLA Ops:
  10.1 23.4 %all-gather = bf16[16,1,128]{2,1,0:T(2,128)(2,1)S(1)} all-gather(bf16[1,1,128]{2,1,0:T(2,128)(2,1)S(1)} %bitcast.143), channel_id=1, replica_groups=mesh['rep'=2,'shard'=16] {'shard'}, dimensions={0}, use_global_device_ids=true | all-gather | bytes 4352 | tf_op jit(solution)/shard_map/all_gather | solution.py:186
  33.5 18.0 %all-gather.1 = bf16[16,1,128]{2,1,0:T(2,128)(2,1)S(1)} all-gather(bf16[1,1,128]{2,1,0:T(2,128)(2,1)S(1)} %bitcast.144), channel_id=1, replica_groups=mesh['rep'=2,'shard'=16] {'shard'}, dimensions={0}, use_global_device_ids=true | all-gather | bytes 4352 | tf_op jit(solution)/shard_map/all_gather | solution.py:187
  51.8 19.3 %all-gather.2 = bf16[16,1,128]{2,1,0:T(2,128)(2,1)S(1)} all-gather(bf16[1,1,128]{2,1,0:T(2,128)(2,1)S(1)} %bitcast.145), channel_id=1, replica_groups=mesh['rep'=2,'shard'=16] {'shard'}, dimensions={0}, use_global_device_ids=true | all-gather | bytes 4352 | tf_op jit(solution)/shard_map/all_gather | solution.py:203
  71.2 18.0 %all-gather.3 = bf16[16,1,128]{2,1,0:T(2,128)(2,1)S(1)} all-gather(bf16[1,1,128]{2,1,0:T(2,128)(2,1)S(1)} %bitcast.146), channel_id=1, replica_groups=mesh['rep'=2,'shard'=16] {'shard'}, dimensions={0}, use_global_device_ids=true | all-gather | bytes 4352 | tf_op jit(solution)/shard_map/all_gather | solution.py:214
  89.9 51.1 %all-gather.13.cloned.1.call-done = bf16[2048,6144]{1,0:T(8,128)(2,1)} async-done(((bf16[128,6144]{1,0:T(8,128)(2,1)}), bf16[2048,6144]{1,0:T(8,128)(2,1)}) %all-gather.13.cloned.1.call-update) | async-done | bytes 25165840 | tf_op jit(solution)/shard_map/all_gather | solution.py:185
  141.0 10.1 fusion.27
  158.2 59.4 %all-gather.15.cloned.1.call-done = bf16[2048,2048]{1,0:T(8,128)(2,1)} async-done(((bf16[128,2048]{1,0:T(8,128)(2,1)}), bf16[2048,2048]{1,0:T(8,128)(2,1)}) %all-gather.15.cloned.1.call-update) | async-done | bytes 8388624 | tf_op jit(solution)/shard_map/all_gather | solution.py:202
  224.6 319.3 %all-gather.17.cloned.1.call-done = bf16[2048,16384]{1,0:T(8,128)(2,1)} async-done(((bf16[128,16384]{1,0:T(8,128)(2,1)}), bf16[2048,16384]{1,0:T(8,128)(2,1)}) %all-gather.17.cloned.1.call-update) | async-done | bytes 67108880 | tf_op jit(solution)/shard_map/all_gather | solution.py:213
  544.0 29.7 %fusion.28 = f32[128,16384]{1,0:T(8,128)} fusion(bf16[128,2048]{1,0:T(8,128)(2,1)} %fusion.10, bf16[2048,16384]{1,0:T(8,128)(2,1)} %all-gather.17.cloned.1.call-done), kind=kOutput, calls=%fused_computation.105 | convolution fusion | flops 8589934592 | bytes 76021760 | tf_op jit(solution)/shard_map/dot_general | solution.py:140
  573.6 6.0 multiply_convert_fusion.2
  579.6 133.9 %all-gather.19.cloned.1.call-done = bf16[8192,2048]{1,0:T(8,128)(2,1)} async-done(((bf16[512,2048]{1,0:T(8,128)(2,1)}), bf16[8192,2048]{1,0:T(8,128)(2,1)}) %all-gather.19.cloned.1.call-update) | async-done | bytes 33554448 | tf_op jit(solution)/shard_map/all_gather | solution.py:223
  713.5 13.6 multiply_reduce_fusion.7
  729.3 20.1 %multiply_convert_fusion.1 = (bf16[128,8192]{1,0:T(8,128)(2,1)}, bf16[128,8192]{1,0:T(8,128)(2,1)}) fusion(f32[128,16384]{1,0:T(8,128)} %fusion.28, bf16[128,2048]{1,0:T(8,128)(2,1)} %multiply_convert_fusion.6, bf16[8192,2048]{1,0:T(8,128)(2,1)} %all-gather.19.cloned.1.call-done), kind=kOutput, calls=%fused_computation.5 | convolution fusion | flops 4308598784 | bytes 46661632 | tf_op jit(solution)/shard_map/dot_general | solution.py:66
  749.4 30.4 %multiply_reduce_fusion.1 = (bf16[2048]{0:T(1024)(128)(2,1)S(1)}, f32[128]{0:T(128)S(1)}, f32[128,2048]{1,0:T(8,128)}) fusion(f32[128,2048]{1,0:T(8,128)} %copy-done.2, f32[128]{0:T(128)S(1)} %add_rsqrt_fusion.1, f32[2048]{0:T(1024)S(1)} %bitcast.131, bf16[2048,16384]{1,0:T(8,128)(2,1)} %all-gather.17.cloned.1.call-done, ...), kind=kOutput, calls=%fused_computation.36 | convolution fusion | flops 8600680448 | bytes 73938432 | tf_op jit(solution)/shard_map/dot_general | solution.py:66
  784.0 7.3 convolution_convert_fusion.4
  812.9 27.7 %all_to_all.73 = bf16[128,16,128]{0,2,1:T(8,128)(2,1)} all-to-all(bf16[128,16,128]{0,2,1:T(8,128)(2,1)S(1)} %bitcast.127), channel_id=1, replica_groups=mesh['rep'=2,'shard'=16] {'shard'}, dimensions={1} | all-to-all | bytes 1048576 | tf_op jit(solution)/shard_map/all_to_all | solution.py:254
  840.6 9.8 all-to-all-start.1
  852.0 20.5 %all-to-all-done.1 = bf16[128,16,128]{0,2,1:T(8,128)(2,1)S(1)} async-done(((bf16[128,16,128]{0,2,1:T(8,128)(2,1)}), bf16[128,16,128]{0,2,1:T(8,128)(2,1)S(1)}, u32[]{:S(2)}, u32[]{:S(2)}) %all-to-all-start.1) | async-done | bytes 524320 | tf_op jit(solution)/shard_map/all_to_all | solution.py:255
  872.5 6.0 all-to-all-start.3
  880.1 5.5 convolution_convert_fusion.3
  885.5 50.8 %all-to-all-done.3 = bf16[128,16,512]{2,0,1:T(8,128)(2,1)} async-done(((bf16[128,16,512]{2,0,1:T(8,128)(2,1)}), bf16[128,16,512]{2,0,1:T(8,128)(2,1)}, u32[]{:S(2)}, u32[]{:S(2)}) %all-to-all-start.3) | async-done | bytes 2097184 | tf_op jit(solution)/shard_map/all_to_all | solution.py:252
  936.3 18.1 %all-to-all-start.2 = ((bf16[128,16,128]{2,0,1:T(8,128)(2,1)}), bf16[128,16,128]{2,0,1:T(8,128)(2,1)S(1)}, u32[]{:S(2)}, u32[]{:S(2)}) async-start(bf16[128,16,128]{2,0,1:T(8,128)(2,1)} %copy_bitcast_fusion.1), calls=%async_computation.2 | async-start | bytes 1048576 | tf_op jit(solution)/shard_map/all_to_all | solution.py:253
  954.7 36.5 %all-gather.27.cloned.1.call-done = bf16[2048,2048]{1,0:T(8,128)(2,1)} async-done(((bf16[128,2048]{1,0:T(8,128)(2,1)}), bf16[2048,2048]{1,0:T(8,128)(2,1)}) %all-gather.27.cloned.1.call-update) | async-done | bytes 8388624 | tf_op jit(solution)/shard_map/all_gather | solution.py:260
  991.2 9.9 convolution_convert_fusion.2
  1001.1 119.8 %all-gather.21.cloned.1.call-done = bf16[2048,6144]{1,0:T(8,128)(2,1)} async-done(((bf16[128,6144]{1,0:T(8,128)(2,1)}), bf16[2048,6144]{1,0:T(8,128)(2,1)}) %all-gather.21.cloned.1.call-update) | async-done | bytes 25165840 | tf_op jit(solution)/shard_map/all_gather | solution.py:262
  1120.9 12.9 fusion
  1133.8 315.4 %all-gather.25.cloned.1.call-done = bf16[2048,16384]{1,0:T(8,128)(2,1)} async-done(((bf16[128,16384]{1,0:T(8,128)(2,1)}), bf16[2048,16384]{1,0:T(8,128)(2,1)}) %all-gather.25.cloned.1.call-update) | async-done | bytes 67108880 | tf_op jit(solution)/shard_map/all_gather | solution.py:261
  1449.1 26.2 %convolution_convert_fusion = bf16[128,16384]{1,0:T(8,128)(2,1)} fusion(bf16[2048,128]{1,0:T(8,128)(2,1)S(1)} %bitcast.124, bf16[2048,16384]{1,0:T(8,128)(2,1)} %all-gather.25.cloned.1.call-done), kind=kOutput, calls=%fused_computation | convolution fusion | flops 8592031744 | bytes 71827456 | tf_op jit(solution)/shard_map/dot_general | solution.py:72
  1477.2 60.7 %all-reduce.4 = (bf16[2048]{0:T(1024)(128)(2,1)S(1)}, bf16[2048]{0:T(1024)(128)(2,1)S(1)}, bf16[2048]{0:T(1024)(128)(2,1)S(1)}, bf16[2048]{0:T(1024)(128)(2,1)S(1)}) all-reduce(bf16[2048]{0:T(1024)(128)(2,1)S(1)} %get-tuple-element.55, ...), channel_id=2, replica_groups=mesh['rep'=2,'shard'=16] {'shard'}, use_global_device_ids=true, to_apply=%region_17.18.clone | all-reduce | flops 8192 | bytes 32768
  1545.6 14.4 convolution_add_fusion
  1560.0 113.7 %all-reduce.9.cloned.1.call-done = (bf16[128,6144]{0,1:T(8,128)(2,1)}, bf16[128,2048]{1,0:T(8,128)(2,1)}, bf16[128,16384]{1,0:T(8,128)(2,1)}, bf16[512,2048]{1,0:T(8,128)(2,1)}) async-done(((bf16[128,6144]{0,1:T(8,128)(2,1)}, bf16[128,2048]{1,0:T(8,128)(2,1)}, bf16[128,16384]{1,0:T(8,128)(2,1)}, bf16[512,2048]{1,0:T(8,128)(2,1)}), (bf16[128,6144]{0,1:T(8,128)(2,1)}, bf16[128,2048]{1,0:T(8,128)(2,1)}, ...) | async-done | bytes 8388624 | tf_op jit(solution)/shard_map/psum | solution.py:281
  1673.7 6.6 convert_element_type.154
  (155 shorter events, 63.6 us)
Async XLA Ops:
  7.2 2.9 copy-start.29
  7.2 26.3 %copy-start.30 = (bf16[128]{0:T(256)(128)(2,1)S(1)}, bf16[128]{0:T(256)(128)(2,1)}, u32[]{:S(2)}) copy-start(bf16[128]{0:T(256)(128)(2,1)} %param.19) | copy-start | bytes 772
  7.2 44.3 %copy-start.28 = (s32[128]{0:T(128)S(1)}, s32[128]{0:T(128)}, u32[]{:S(2)}) copy-start(s32[128]{0:T(128)} %param.12) | copy-start | bytes 1540
  7.2 44.6 %copy-start.31 = (bf16[128]{0:T(256)(128)(2,1)S(1)}, bf16[128]{0:T(256)(128)(2,1)}, u32[]{:S(2)}) copy-start(bf16[128]{0:T(256)(128)(2,1)} %param.20) | copy-start | bytes 772
  7.2 63.9 %copy-start.32 = (bf16[128]{0:T(256)(128)(2,1)S(1)}, bf16[128]{0:T(256)(128)(2,1)}, u32[]{:S(2)}) copy-start(bf16[128]{0:T(256)(128)(2,1)} %param.21) | copy-start | bytes 772
  7.2 133.8 %all-gather.13.cloned.1.call-start = ((), (), s32[]{:S(2)}) async-start(), calls=%async_computation.4 | async-start | bytes 26738688 | tf_op jit(solution)/shard_map/all_gather | solution.py:185
  8.0 209.7 %all-gather.15.cloned.1.call-start = ((), (), s32[]{:S(2)}) async-start(), calls=%async_computation.5 | async-start | bytes 8912896 | tf_op jit(solution)/shard_map/all_gather | solution.py:202
  8.7 535.2 %all-gather.17.cloned.1.call-start = ((), (), s32[]{:S(2)}) async-start(), calls=%async_computation.6 | async-start | bytes 71303168 | tf_op jit(solution)/shard_map/all_gather | solution.py:213
  9.4 704.0 %all-gather.19.cloned.1.call-start = ((), (), s32[]{:S(2)}) async-start(), calls=%async_computation.7 | async-start | bytes 35651584 | tf_op jit(solution)/shard_map/all_gather | solution.py:223
  10.0 870.0 %all-gather.23.cloned.1.call-start = ((), (), s32[]{:S(2)}) async-start(), calls=%async_computation.9 | async-start | bytes 8912896 | tf_op jit(solution)/shard_map/all_gather | solution.py:263
  217.7 6.0 copy-start.4
  713.5 13.7 copy-start.8
  783.2 208.0 %all-gather.27.cloned.1.call-start = ((), (), s32[]{:S(2)}) async-start(), calls=%async_computation.11 | async-start | bytes 8912896 | tf_op jit(solution)/shard_map/all_gather | solution.py:260
  783.8 337.1 %all-gather.21.cloned.1.call-start = ((), (), s32[]{:S(2)}) async-start(), calls=%async_computation.8 | async-start | bytes 26738688 | tf_op jit(solution)/shard_map/all_gather | solution.py:262
  798.0 3.4 copy-start.14
  798.1 3.4 copy-start.16
  798.1 3.9 copy-start.10
  798.1 3.9 copy-start.12
  807.6 641.5 %all-gather.25.cloned.1.call-start = ((), (), s32[]{:S(2)}) async-start(), calls=%async_computation.10 | async-start | bytes 71303168 | tf_op jit(solution)/shard_map/all_gather | solution.py:261
  811.6 38.8 %copy-start.1 = (bf16[128,8192]{1,0:T(8,128)(2,1)S(1)}, bf16[128,8192]{1,0:T(8,128)(2,1)}, u32[]{:S(2)}) copy-start(bf16[128,8192]{1,0:T(8,128)(2,1)} %multiply_convert_fusion.2) | copy-start | bytes 6291460
  840.6 31.9 %all-to-all-start.1 = ((bf16[128,16,128]{0,2,1:T(8,128)(2,1)}), bf16[128,16,128]{0,2,1:T(8,128)(2,1)S(1)}, u32[]{:S(2)}, u32[]{:S(2)}) async-start(bf16[128,16,128]{0,2,1:T(8,128)(2,1)} %get-tuple-element.103), calls=%async_computation.1 | async-start | bytes 1048576 | tf_op jit(solution)/shard_map/all_to_all | solution.py:255
  850.4 28.4 %copy-start.7 = (bf16[128,2048]{1,0:T(8,128)(2,1)S(1)}, bf16[128,2048]{1,0:T(8,128)(2,1)}, u32[]{:S(2)}) copy-start(bf16[128,2048]{1,0:T(8,128)(2,1)} %fusion.10) | copy-start | bytes 1572868
  852.0 26.5 %copy-start.19 = (bf16[128,16,128]{0,2,1:T(8,128)(2,1)S(1)}, bf16[128,16,128]{0,2,1:T(8,128)(2,1)}, u32[]{:S(2)}) copy-start(bf16[128,16,128]{0,2,1:T(8,128)(2,1)} %all_to_all.73) | copy-start | bytes 1572868
  872.5 63.9 %all-to-all-start.3 = ((bf16[128,16,512]{2,0,1:T(8,128)(2,1)}), bf16[128,16,512]{2,0,1:T(8,128)(2,1)}, u32[]{:S(2)}, u32[]{:S(2)}) async-start(bf16[128,16,512]{2,0,1:T(8,128)(2,1)} %bitcast.120), calls=%async_computation.3 | async-start | bytes 4194304 | tf_op jit(solution)/shard_map/all_to_all | solution.py:252
  936.3 197.5 %all-to-all-start.2 = ((bf16[128,16,128]{2,0,1:T(8,128)(2,1)}), bf16[128,16,128]{2,0,1:T(8,128)(2,1)S(1)}, u32[]{:S(2)}, u32[]{:S(2)}) async-start(bf16[128,16,128]{2,0,1:T(8,128)(2,1)} %copy_bitcast_fusion.1), calls=%async_computation.2 | async-start | bytes 1048576 | tf_op jit(solution)/shard_map/all_to_all | solution.py:253
  954.5 719.2 %all-reduce.9.cloned.1.call-start = ((), (), s32[]{:S(2)}) async-start(), calls=%async_computation.12 | async-start | bytes 16777216 | tf_op jit(solution)/shard_map/psum | solution.py:281
  1475.3 70.3 %copy-start.17 = (f32[128,2048]{1,0:T(8,128)S(1)}, f32[128,2048]{1,0:T(8,128)}, u32[]{:S(2)}) copy-start(f32[128,2048]{1,0:T(8,128)} %get-tuple-element.109) | copy-start | bytes 3145732
  1475.3 70.3 %copy-start.21 = (bf16[128,2048]{1,0:T(8,128)(2,1)S(1)}, bf16[128,2048]{1,0:T(8,128)(2,1)}, u32[]{:S(2)}) copy-start(bf16[128,2048]{1,0:T(8,128)(2,1)} %copy.132) | copy-start | bytes 1572868
  1475.3 70.3 %copy-start.23 = (bf16[128,2048]{1,0:T(8,128)(2,1)S(1)}, bf16[128,2048]{1,0:T(8,128)(2,1)}, u32[]{:S(2)}) copy-start(bf16[128,2048]{1,0:T(8,128)(2,1)} %copy-done.22) | copy-start | bytes 1572868
  1475.3 70.3 %copy-start.25 = (bf16[128,2048]{1,0:T(8,128)(2,1)S(1)}, bf16[128,2048]{1,0:T(8,128)(2,1)}, u32[]{:S(2)}) copy-start(bf16[128,2048]{1,0:T(8,128)(2,1)} %copy-done.24) | copy-start | bytes 1572868
  1673.7 6.6 copy-start.18
  1680.3 4.6 copy-start.27
  (14 other events, 18.7 us)
Sparse Core Ops, SparseCore 0:
  9.6 131.3 all-gather.12
  143.2 74.4 all-gather.14
  219.3 324.6 all-gather.16
  545.4 168.0 all-gather.18
  783.3 94.6 all-gather.22
  880.1 111.0 all-gather.26
  993.4 127.4 all-gather.20
  1123.0 326.0 all-gather.24
  1475.5 198.1 all-reduce.8
where the time goes:
time: 1700 us; the launch traced here: 1690 us
  waiting for transfers between devices  1220 us (72%)
  matrix products  193 us (11%)
  blocking collectives  172 us (10%)
  other arithmetic  36.9 us (2%)
  starting transfers between devices  34.6 us (2%)
  local copies, waits for them, and re-layouts  17.3 us (1%)
    all_gather x1, waiting for transfers between devices, shards(): lax.all_gather(w_gate_up, 'shard', axis=0, tiled=True)  319 us
    all_gather x1, waiting for transfers between devices, shards(): lax.all_gather(d_gu_b, 'shard', axis=0, tiled=True)  315 us
    all_gather x1, waiting for transfers between devices, shards(): lax.all_gather(w_down, 'shard', axis=0, tiled=True)  134 us
    all_gather x1, waiting for transfers between devices, shards(): lax.all_gather(d_qkv_b, 'shard', axis=0, tiled=True)  120 us
    psum x1, waiting for transfers between devices, shards(): lax.psum(grad_qkv_own.astype(jnp.bfloat16), 'rep').astype(jnp.float32)  114 us
    dot_general x4, matrix products, contract_last(): lax.dot_general(left, right, (((1,), (1,)), ((), ())), preferred_element_...  72.1 us
    unnamed x1, blocking collectives  60.7 us
    all_gather x1, waiting for transfers between devices, shards(): lax.all_gather(w_out, 'shard', axis=0, tiled=True)  59.4 us
  transfers between devices with their start and end apart: 12, of which 10 were waited for; matrix products, arithmetic and copies ran while one was open for 8% of the time, Pallas kernels for 0%

commit v1 on v0

v1 whole, which is shorter than its diff:
```python
import jax
import jax.numpy as jnp
from jax import lax
from jax.sharding import PartitionSpec as P

H = 16
EPSILON = 1e-06
THETA = 500000.0
BF = jnp.bfloat16
F32 = jnp.float32


def positions(seg):
    slots = lax.broadcasted_iota(jnp.int32, seg.shape, 1)
    starts = jnp.concatenate(
        [jnp.ones((seg.shape[0], 1), jnp.bool_), seg[:, 1:] != seg[:, :-1]], axis=1
    )
    first = lax.cummax(jnp.where(starts, slots, 0), axis=1)
    return slots - first


def rope_tables(seg, head_width):
    half_width = head_width // 2
    spots = positions(seg).astype(F32).reshape(-1)
    inverse = THETA ** (-(2.0 * jnp.arange(half_width, dtype=F32)) / head_width)
    angle = spots[:, None] * inverse[None, :]
    return jnp.cos(angle), jnp.sin(angle)


def rotate(matrix, cosine, sine):
    half = matrix.shape[-1] // 2
    a, b = matrix[..., :half], matrix[..., half:]
    return jnp.concatenate([a * cosine - b * sine, b * cosine + a * sine], axis=-1)


def mm(left, right):
    return jnp.dot(left, right, preferred_element_type=F32)


def mm_nt(left, right):
    return lax.dot_general(left, right, (((1,), (1,)), ((), ())), preferred_element_type=F32)


def mm_tn(left, right):
    return lax.dot_general(left, right, (((0,), (0,)), ((), ())), preferred_element_type=F32)


def norm_scale(vector):
    return lax.rsqrt(jnp.mean(vector * vector, axis=-1, keepdims=True) + EPSILON)


def norm_back(upstream, normed, rscale, gain):
    scaled = upstream * gain
    inner = jnp.mean(scaled * normed, axis=-1, keepdims=True)
    return rscale * (scaled - normed * inner), jnp.sum(upstream * normed, axis=0)


def gather(piece):
    return lax.all_gather(piece, "shard", axis=0, tiled=True)


def scatter(partial):
    return lax.psum_scatter(partial.astype(BF), "shard", scatter_dimension=0, tiled=True).astype(F32)


def make(n_rep, n_shard):
    def rep_scatter(x):
        if n_rep == 2:
            me = lax.axis_index("rep")
            mine = lax.dynamic_index_in_dim(x, me, 0, keepdims=False)
            other = lax.dynamic_index_in_dim(x, 1 - me, 0, keepdims=False)
            got = lax.ppermute(other.astype(BF), "rep", [(0, 1), (1, 0)])
            return (mine + got.astype(F32)).astype(BF)
        return lax.psum_scatter(x.astype(BF), "rep", scatter_dimension=0, tiled=False)

    def rep_gather(x):
        if n_rep == 2:
            me = lax.axis_index("rep")
            got = lax.ppermute(x, "rep", [(0, 1), (1, 0)])
            first = jnp.where(me == 0, x, got)
            second = jnp.where(me == 0, got, x)
            return jnp.stack([first, second])
        return lax.all_gather(x, "rep", axis=0, tiled=False)

    def rep_sum(x):
        rows = x.shape[0]
        part = rep_scatter(x.reshape(n_rep, rows // n_rep, x.shape[1]))
        return rep_gather(part).reshape(x.shape).astype(F32)

    def grad_back(x, groups):
        rows, cols = x.shape
        own = rows // n_shard
        width = cols // groups
        split = x.reshape(n_shard, n_rep, own // n_rep, cols).transpose(1, 0, 2, 3)
        part = rep_scatter(split)
        part = lax.all_to_all(part, "shard", split_axis=0, concat_axis=0, tiled=True)
        whole = rep_gather(part)
        whole = whole.reshape(n_rep, n_shard, own // n_rep, groups, width)
        return whole.transpose(0, 2, 3, 1, 4).reshape(own, groups * n_shard * width).astype(F32)

    def columns(w, groups):
        rows, cols = w.shape
        w = w.reshape(rows, groups, n_shard, cols // (groups * n_shard))
        w = lax.all_to_all(w, "shard", split_axis=2, concat_axis=0, tiled=True)
        return w.reshape(rows * n_shard, cols // n_shard)

    def shards(
        tokens, segment_ids, cotangent, w_qkv, w_out, w_gate_up, w_down,
        q_gain, k_gain, attn_gain, mlp_gain,
    ):
        count, width = tokens.shape
        heads = H // n_shard
        hw = width // H
        own = width // n_shard
        ff = w_down.shape[0]
        total = count * n_shard

        small = gather(jnp.stack([segment_ids.astype(BF), attn_gain, mlp_gain])[None])
        tokens_g = gather(tokens)
        wq = columns(w_qkv, 3)
        wg = columns(w_gate_up, 2)
        seg = small[:, 0].astype(jnp.int32)
        gain_attn = small[:, 1].reshape(-1).astype(F32)
        gain_mlp = small[:, 2].reshape(-1).astype(F32)
        gain_query = q_gain.astype(F32)
        gain_keys = k_gain.astype(F32)
        cosine, sine = rope_tables(seg, hw)
        cos3 = cosine[:, None, :]
        sin3 = sine[:, None, :]

        qkv = mm(tokens_g, wq)
        query, keys, values_b = qkv[:, :own], qkv[:, own : 2 * own], qkv[:, 2 * own :].astype(BF)
        squares = jnp.stack([jnp.sum(query * query, axis=-1), jnp.sum(keys * keys, axis=-1)])
        squares = lax.psum(squares, "shard")
        scales = lax.rsqrt(squares / width + EPSILON)
        query_scale, keys_scale = scales[0][:, None], scales[1][:, None]
        query_hat, keys_hat = query * query_scale, keys * keys_scale

        def rot(x, sign):
            return rotate(x.reshape(total, heads, hw), cos3, sign * sin3).reshape(total, own)

        query_rot = rot(query_hat * gain_query, 1.0).astype(BF)
        keys_rot = rot(keys_hat * gain_keys, 1.0).astype(BF)

        slots = jnp.arange(count)
        ok = (seg[:, :, None] == seg[:, None, :]) & (slots[None, :] <= slots[:, None])[None]
        ok = ok[:, None]

        def blocks(x):
            return x.reshape(n_shard, count, heads, hw)

        root = hw ** (-0.5)
        qb, kb, vb = blocks(query_rot), blocks(keys_rot), blocks(values_b)
        scores = jnp.einsum("bthd,bshd->bhts", qb, kb, preferred_element_type=F32) * root
        scores = jnp.where(ok, scores, -1e30)
        top = jnp.max(scores, axis=-1, keepdims=True)
        lse = top + jnp.log(jnp.sum(jnp.exp(scores - top), axis=-1, keepdims=True))
        probs = jnp.exp(scores - lse)
        probs_b = probs.astype(BF)
        context = jnp.einsum("bhts,bshd->bthd", probs_b, vb, preferred_element_type=F32)
        context_b = context.astype(BF).reshape(total, own)

        attn_raw = scatter(mm(context_b, w_out))
        attn_scale = norm_scale(attn_raw)
        attn_hat = attn_raw * attn_scale
        resid = tokens.astype(F32) + attn_hat * gain_attn
        resid_g = gather(resid.astype(BF))

        gate_up = mm(resid_g, wg)
        gate, up = gate_up[:, :ff], gate_up[:, ff:]
        sigma = jax.nn.sigmoid(gate)
        activated = gate * sigma
        mixed_b = (activated * up).astype(BF)
        down_raw = scatter(mm(mixed_b, w_down))
        down_scale = norm_scale(down_raw)
        down_hat = down_raw * down_scale
        output = (resid + down_hat * gain_mlp).astype(BF)

        valid = (segment_ids >= 0).astype(F32)[:, None]
        d_out = cotangent.astype(F32) * valid
        d_down, grad_mlp = norm_back(d_out, down_hat, down_scale, gain_mlp)
        d_down_g = gather(d_down.astype(BF))
        d_mixed = mm_nt(d_down_g, w_down)
        d_gate = d_mixed * up * sigma * (1.0 + gate * (1.0 - sigma))
        d_up = d_mixed * activated
        d_gu_b = jnp.concatenate([d_gate, d_up], axis=1).astype(BF)
        d_resid = d_out + scatter(mm_nt(d_gu_b, wg))
        grad_down = rep_sum(mm_tn(mixed_b, d_down_g))
        grad_gu = grad_back(mm_tn(resid_g, d_gu_b), 2)

        d_attn, grad_attn = norm_back(d_resid, attn_hat, attn_scale, gain_attn)
        d_attn_g = gather(d_attn.astype(BF))
        d_context_b = mm_nt(d_attn_g, w_out).astype(BF)
        grad_out = rep_sum(mm_tn(context_b, d_attn_g))

        db = blocks(d_context_b)
        d_values = jnp.einsum("bhts,bthd->bshd", probs_b, db, preferred_element_type=F32)
        d_probs = jnp.einsum("bthd,bshd->bhts", db, vb, preferred_element_type=F32)
        delta = jnp.sum(db.astype(F32) * context, axis=-1).transpose(0, 2, 1)[..., None]
        d_scores_b = (probs * (d_probs - delta) * root).astype(BF)
        d_query_rot = jnp.einsum("bhts,bshd->bthd", d_scores_b, kb, preferred_element_type=F32)
        d_keys_rot = jnp.einsum("bhts,bthd->bshd", d_scores_b, qb, preferred_element_type=F32)
        d_query_norm = rot(d_query_rot, -1.0)
        d_keys_norm = rot(d_keys_rot, -1.0)
        grad_query = jnp.sum(d_query_norm * query_hat, axis=0)
        grad_keys = jnp.sum(d_keys_norm * keys_hat, axis=0)
        query_up = d_query_norm * gain_query
        keys_up = d_keys_norm * gain_keys
        inner = jnp.stack(
            [jnp.sum(query_up * query_hat, axis=-1), jnp.sum(keys_up * keys_hat, axis=-1)]
        )
        inner = lax.psum(inner, "shard") / width
        d_query = query_scale * (query_up - query_hat * inner[0][:, None])
        d_keys = keys_scale * (keys_up - keys_hat * inner[1][:, None])
        d_qkv_b = jnp.concatenate(
            [d_query, d_keys, d_values.reshape(total, own)], axis=1
        ).astype(BF)
        grad_tokens = d_resid + scatter(mm_nt(d_qkv_b, wq))
        grad_qkv = grad_back(mm_tn(tokens_g, d_qkv_b), 3)

        gains_local = lax.psum_scatter(
            jnp.stack([grad_attn, grad_mlp]), "shard", scatter_dimension=1, tiled=True
        )
        gains = lax.psum(
            jnp.concatenate([gains_local, jnp.stack([grad_query, grad_keys])]), "rep"
        )
        return (
            output, grad_tokens, grad_qkv, grad_out, grad_gu, grad_down,
            gains[2], gains[3], gains[0], gains[1],
        )

    return shards


def solution(mesh):
    rows = P(("rep", "shard"), None)
    return jax.shard_map(
        make(mesh.shape["rep"], mesh.shape["shard"]),
        mesh=mesh,
        in_specs=(rows, P(("rep", "shard")), rows)
        + (P("shard", None),) * 4
        + (P("shard"),) * 4,
        out_specs=(rows, rows) + (P("shard", None),) * 4 + (P("shard"),) * 4,
        check_vma=False,
    )
```

time: 1700 us -> 1220 us (0.72)
  waiting for transfers between devices: 1220 us -> 548 us
  blocking collectives: 172 us -> 327 us
  matrix products: 193 us -> 110 us
  local copies, waits for them, and re-layouts: 17.3 us -> 96.9 us
  other arithmetic: 36.9 us -> 59.2 us
  starting transfers between devices: 34.6 us -> 56.4 us
    all_gather x8 -> x4, waiting for transfers between devices: 1040 us -> 157 us  [gather(): return lax.all_gather(piece, 'shard', axis=0, tiled=True)]
    reduce_scatter x0 -> x4, waiting for transfers between devices: none -> 307 us  [scatter(): lax.psum_scatter(partial.astype(BF), 'shard', scatter_dimension=0, tiled=...]
    psum x1 -> x3, blocking collectives: 5.37 us -> 126 us  [the longest x1 59.8 us: shards(): inner = lax.psum(inner, 'shard') / width]
    all_to_all x1, blocking collectives: 27.7 us -> 142 us  [columns(): w = lax.all_to_all(w, 'shard', split_axis=2, concat_axis=0, tiled=True)]
    psum x1 -> x0, waiting for transfers between devices: 114 us -> none  [shards(): lax.psum(grad_qkv_own.astype(jnp.bfloat16), 'rep').astype(jnp.float32)]
    dot_general x18, matrix products: 193 us -> 110 us  [the longest x4 37.9 us: mm_nt(): lax.dot_general(left, right, (((1,), (1,)), ((), ())), preferred_element_...]
    ppermute x0 -> x8, waiting for transfers between devices: none -> 63.9 us  [the longest x4 39.9 us: rep_gather(): got = lax.ppermute(x, 'rep', [(0, 1), (1, 0)])]
    unnamed x1 -> x0, blocking collectives: 60.7 us -> none
  transfers between devices with their start and end apart: 12 -> 20, of which waited for: 10 -> 11; matrix products, arithmetic and copies ran while one was open for 8% -> 14% of each run, Pallas kernels for 0% -> 0%
where the time goes in v1:
time: 1220 us; the launch traced here: 1210 us
  waiting for transfers between devices  548 us (45%)
  blocking collectives  327 us (27%)
  matrix products  110 us (9%)
  local copies, waits for them, and re-layouts  96.9 us (8%)
  other arithmetic  59.2 us (5%)
  starting transfers between devices  56.4 us (5%)
  between operations  15 us (1%)
    reduce_scatter x4, waiting for transfers between devices, scatter(): lax.psum_scatter(partial.astype(BF), 'shard', scatter_dimension=0, tiled=...  307 us
    all_gather x4, waiting for transfers between devices, gather(): return lax.all_gather(piece, 'shard', axis=0, tiled=True)  157 us
    all_to_all x1, blocking collectives, columns(): w = lax.all_to_all(w, 'shard', split_axis=2, concat_axis=0, tiled=True)  142 us
    psum x1, blocking collectives, shards(): inner = lax.psum(inner, 'shard') / width  59.8 us
    psum x1, blocking collectives, shards(): squares = lax.psum(squares, 'shard')  58.7 us
    all_gather x1, blocking collectives, gather(): return lax.all_gather(piece, 'shard', axis=0, tiled=True)  58.7 us
    ppermute x4, waiting for transfers between devices, rep_gather(): got = lax.ppermute(x, 'rep', [(0, 1), (1, 0)])  39.9 us
    dot_general x4, matrix products, mm_nt(): lax.dot_general(left, right, (((1,), (1,)), ((), ())), preferred_element_...  37.9 us
  transfers between devices with their start and end apart: 20, of which 11 were waited for; matrix products, arithmetic and copies ran while one was open for 14% of the time, Pallas kernels for 0%

profile of v1, /device:TPU:0, one launch (start us, length us, event | category | flops | bytes accessed | tf_op | source)
XLA Modules:
  0.0 1212.5 jit_solution(16660373175642401086)
XLA Ops:
  13.3 7.5 all-to-all-start
  20.9 58.7 %all-gather.1 = bf16[16,3,128]{2,1,0:T(4,128)(2,1)S(1)} all-gather(bf16[1,3,128]{2,1,0:T(4,128)(2,1)S(1)} %maximum_bitcast_fusion.2), channel_id=2, replica_groups=mesh['rep'=2,'shard'=16] {'shard'}, dimensions={0}, use_global_device_ids=true | all-gather | bytes 13056 | tf_op jit(solution)/shard_map/all_gather | solution.py:59
  83.7 29.8 %all-gather.7.cloned.1.call-done = bf16[2048,2048]{1,0:T(8,128)(2,1)} async-done(((bf16[128,2048]{1,0:T(8,128)(2,1)}), bf16[2048,2048]{1,0:T(8,128)(2,1)}) %all-gather.7.cloned.1.call-update) | async-done | bytes 8388624 | tf_op jit(solution)/shard_map/all_gather | solution.py:59
  113.5 6.4 fusion.13
  122.4 58.7 %psum.21 = f32[2,2048]{1,0:T(2,128)S(1)} all-reduce(f32[2,2048]{1,0:T(2,128)S(1)} %pad_maximum_fusion.10), channel_id=1, replica_groups=mesh['rep'=2,'shard'=16] {'shard'}, use_global_device_ids=true, to_apply=%region_2.3 | all-reduce | flops 4096 | bytes 32768 | tf_op jit(solution)/shard_map/psum | solution.py:134
  195.0 6.8 convolution_convert_fusion.3
  201.9 100.9 %reduce-scatter.8.cloned.1.call-done = bf16[128,2048]{1,0:T(8,128)(2,1)} async-done(((bf16[2048,2048]{1,0:T(8,128)(2,1)}), bf16[128,2048]{1,0:T(8,128)(2,1)}) %reduce-scatter.8.cloned.1.call-update) | async-done | bytes 524304 | tf_op jit(solution)/shard_map/reduce_scatter | solution.py:63
  306.4 6.4 copy.120
  315.5 141.9 %all_to_all.40 = bf16[128,2,16,512]{0,3,1,2:T(8,128)(2,1)S(1)} all-to-all(bf16[128,2,16,512]{0,3,1,2:T(8,128)(2,1)S(1)} %copy.121), channel_id=1, replica_groups=mesh['rep'=2,'shard'=16] {'shard'}, dimensions={2} | all-to-all | bytes 8388608 | tf_op jit(solution)/shard_map/all_to_all | solution.py:104
  462.1 12.6 %fusion.3 = f32[2048,1024]{0,1:T(8,128)S(1)} fusion(bf16[2048,2048]{1,0:T(8,128)(2,1)} %all-gather.9.cloned.1.call-done, bf16[128,8,16,128]{3,2,1,0:T(8,128)(2,1)} %bitcast.203), kind=kOutput, calls=%fused_computation.8 | convolution fusion | flops 8589934592 | bytes 20971520 | tf_op jit(solution)/shard_map/dot_general | solution.py:37
  479.4 6.8 convolution_convert_fusion.2
  486.3 103.6 %reduce-scatter.10.cloned.1.call-done = bf16[128,2048]{1,0:T(8,128)(2,1)} async-done(((bf16[2048,2048]{1,0:T(8,128)(2,1)}), bf16[128,2048]{1,0:T(8,128)(2,1)}) %reduce-scatter.10.cloned.1.call-update) | async-done | bytes 524304 | tf_op jit(solution)/shard_map/reduce_scatter | solution.py:63
  595.4 73.8 %all-gather.11.cloned.1.call-done = bf16[2048,2048]{1,0:T(8,128)(2,1)} async-done(((bf16[128,2048]{1,0:T(8,128)(2,1)}), bf16[2048,2048]{1,0:T(8,128)(2,1)}) %all-gather.11.cloned.1.call-update) | async-done | bytes 8388624 | tf_op jit(solution)/shard_map/all_gather | solution.py:59
  669.2 10.6 multiply_convert_fusion.1
  681.9 11.8 convolution_convert_fusion.1
  693.7 102.1 %reduce-scatter.12.cloned.1.call-done = bf16[128,2048]{1,0:T(8,128)(2,1)} async-done(((bf16[2048,2048]{1,0:T(8,128)(2,1)}), bf16[128,2048]{1,0:T(8,128)(2,1)}) %reduce-scatter.12.cloned.1.call-update) | async-done | bytes 524304 | tf_op jit(solution)/shard_map/reduce_scatter | solution.py:63
  800.6 12.6 %fusion.9 = f32[2048,1024]{1,0:T(8,128)S(1)} fusion(bf16[2048,2048]{1,0:T(8,128)(2,1)} %all-gather.9.cloned.1.call-done, bf16[2048,512]{0,1:T(8,128)(2,1)} %copy-done.35, bf16[2048,512]{0,1:T(8,128)(2,1)} %copy-done.34), kind=kOutput, calls=%fused_computation.23 | convolution fusion | flops 8598323200 | bytes 20971520 | tf_op jit(solution)/shard_map/dot_general | solution.py:45
  821.3 53.0 %all-gather.13.cloned.1.call-done = bf16[2048,2048]{1,0:T(8,128)(2,1)} async-done(((bf16[128,2048]{1,0:T(8,128)(2,1)}), bf16[2048,2048]{1,0:T(8,128)(2,1)}) %all-gather.13.cloned.1.call-update) | async-done | bytes 8388624 | tf_op jit(solution)/shard_map/all_gather | solution.py:59
  874.3 5.8 convolution_convert_fusion.4
  899.3 59.8 %psum.22 = f32[2,2048]{1,0:T(2,128)S(1)} all-reduce(f32[2,2048]{1,0:T(2,128)S(1)} %pad_maximum_fusion.11), channel_id=1, replica_groups=mesh['rep'=2,'shard'=16] {'shard'}, use_global_device_ids=true, to_apply=%region_16.17 | all-reduce | flops 4096 | bytes 32768 | tf_op jit(solution)/shard_map/psum | solution.py:212
  962.8 9.8 convolution_convert_fusion
  982.5 7.3 fusion.95
  991.6 24.0 %collective-permute-done.6 = bf16[256,2048]{1,0:T(8,128)(2,1)S(1)} collective-permute-done((bf16[256,2048]{1,0:T(8,128)(2,1)S(1)}, bf16[256,2048]{1,0:T(8,128)(2,1)S(1)}, u32[]{:S(2)}, u32[]{:S(2)}) %collective-permute-start.6) | collective-permute-done | bytes 1048608 | tf_op jit(solution)/shard_map/ppermute | solution.py:72
  1018.4 20.3 %all-to-all-done.3 = bf16[16,64,1024]{2,1,0:T(8,128)(2,1)} async-done(((bf16[16,64,1024]{2,1,0:T(8,128)(2,1)}), bf16[16,64,1024]{2,1,0:T(8,128)(2,1)}, u32[]{:S(2)}, u32[]{:S(2)}) %all-to-all-start.3) | async-done | bytes 2097184 | tf_op jit(solution)/shard_map/all_to_all | solution.py:96
  1043.5 8.6 convolution_bitcast_fusion
  1061.2 22.3 %collective-permute-done.5 = bf16[16,64,1024]{2,1,0:T(8,128)(2,1)} collective-permute-done((bf16[16,64,1024]{2,1,0:T(8,128)(2,1)}, bf16[16,64,1024]{2,1,0:T(8,128)(2,1)}, u32[]{:S(2)}, u32[]{:S(2)}) %collective-permute-start.5) | collective-permute-done | bytes 2097184 | tf_op jit(solution)/shard_map/ppermute | solution.py:79
  1092.5 5.2 copy.134
  1102.4 5.2 copy.135
  1109.8 32.8 %all-to-all-start.2 = ((bf16[16,64,384]{2,1,0:T(8,128)(2,1)}), bf16[16,64,384]{2,1,0:T(8,128)(2,1)}, u32[]{:S(2)}, u32[]{:S(2)}) async-start(bf16[16,64,384]{2,1,0:T(8,128)(2,1)} %fusion.15), calls=%async_computation.6 | async-start | bytes 1572864 | tf_op jit(solution)/shard_map/all_to_all | solution.py:96
  1153.0 9.4 reshape.428
  1164.9 7.9 psum.23
  1175.0 17.2 %collective-permute-done.1 = bf16[16,64,384]{2,1,0:T(8,128)(2,1)S(1)} collective-permute-done((bf16[16,64,384]{2,1,0:T(8,128)(2,1)}, bf16[16,64,384]{2,1,0:T(8,128)(2,1)S(1)}, u32[]{:S(2)}, u32[]{:S(2)}) %collective-permute-start.1) | collective-permute-done | bytes 786464 | tf_op jit(solution)/shard_map/ppermute | solution.py:79
  (204 shorter events, 158.2 us)
Async XLA Ops:
  7.2 472.2 %copy-start = (bf16[512,2048]{1,0:T(8,128)(2,1)S(1)}, bf16[512,2048]{1,0:T(8,128)(2,1)}, u32[]{:S(2)}) copy-start(bf16[512,2048]{1,0:T(8,128)(2,1)} %param.17) | copy-start | bytes 6291460
  7.2 106.3 %all-gather.7.cloned.1.call-start = ((), (), s32[]{:S(2)}) async-start(), calls=%async_computation.9 | async-start | bytes 8912896 | tf_op jit(solution)/shard_map/all_gather | solution.py:59
  8.0 12.9 %copy-start.29 = (bf16[128]{0:T(256)(128)(2,1)S(1)}, bf16[128]{0:T(256)(128)(2,1)}, u32[]{:S(2)}) copy-start(bf16[128]{0:T(256)(128)(2,1)} %param.21) | copy-start | bytes 772
  13.3 66.8 %all-to-all-start = ((bf16[128,3,16,128]{0,3,1,2:T(8,128)(2,1)}), bf16[128,3,16,128]{0,3,1,2:T(8,128)(2,1)}, u32[]{:S(2)}, u32[]{:S(2)}) async-start(bf16[128,3,16,128]{0,3,1,2:T(8,128)(2,1)} %copy.114), calls=%async_computation | async-start | bytes 3145728 | tf_op jit(solution)/shard_map/all_to_all | solution.py:104
  20.8 282.0 %reduce-scatter.8.cloned.1.call-start = ((), (), s32[]{:S(2)}) async-start(), calls=%async_computation.10 | async-start | bytes 8912896 | tf_op jit(solution)/shard_map/reduce_scatter | solution.py:63
  201.8 260.3 %all-gather.9.cloned.1.call-start = ((), (), s32[]{:S(2)}) async-start(), calls=%async_computation.11 | async-start | bytes 8912896 | tf_op jit(solution)/shard_map/all_gather | solution.py:59
  306.3 283.5 %reduce-scatter.10.cloned.1.call-start = ((), (), s32[]{:S(2)}) async-start(), calls=%async_computation.12 | async-start | bytes 8912896 | tf_op jit(solution)/shard_map/reduce_scatter | solution.py:63
  486.2 183.0 %all-gather.11.cloned.1.call-start = ((), (), s32[]{:S(2)}) async-start(), calls=%async_computation.13 | async-start | bytes 8912896 | tf_op jit(solution)/shard_map/all_gather | solution.py:59
  595.2 200.7 %reduce-scatter.12.cloned.1.call-start = ((), (), s32[]{:S(2)}) async-start(), calls=%async_computation.14 | async-start | bytes 8912896 | tf_op jit(solution)/shard_map/reduce_scatter | solution.py:63
  693.7 102.2 %copy-start.3 = (bf16[128,2048]{1,0:T(8,128)(2,1)S(1)}, bf16[128,2048]{1,0:T(8,128)(2,1)}, u32[]{:S(2)}) copy-start(bf16[128,2048]{1,0:T(8,128)(2,1)} %param.13) | copy-start | bytes 1572868
  693.7 102.2 %copy-start.6 = (bf16[128,2048]{1,0:T(8,128)(2,1)S(1)}, bf16[128,2048]{1,0:T(8,128)(2,1)}, u32[]{:S(2)}) copy-start(bf16[128,2048]{1,0:T(8,128)(2,1)} %reduce-scatter.8.cloned.1.call-done) | copy-start | bytes 1572868
  693.7 103.8 %copy-start.7 = (bf16[128,2048]{1,0:T(8,128)(2,1)S(1)}, bf16[128,2048]{1,0:T(8,128)(2,1)}, u32[]{:S(2)}) copy-start(bf16[128,2048]{1,0:T(8,128)(2,1)} %reduce-scatter.10.cloned.1.call-done) | copy-start | bytes 1572868
  693.7 103.8 %copy-start.12 = (bf16[128,2048]{1,0:T(8,128)(2,1)S(1)}, bf16[128,2048]{1,0:T(8,128)(2,1)}, u32[]{:S(2)}) copy-start(bf16[128,2048]{1,0:T(8,128)(2,1)} %param.11) | copy-start | bytes 1572868
  693.7 180.6 %all-gather.13.cloned.1.call-start = ((), (), s32[]{:S(2)}) async-start(), calls=%async_computation.15 | async-start | bytes 8912896 | tf_op jit(solution)/shard_map/all_gather | solution.py:59
  800.2 362.2 %reduce-scatter.16.cloned.1.call-start = ((), (), s32[]{:S(2)}) async-start(), calls=%async_computation.17 | async-start | bytes 1114112
  818.3 154.3 %collective-permute-start.4 = (bf16[16,64,1024]{2,1,0:T(8,128)(2,1)}, bf16[16,64,1024]{2,1,0:T(8,128)(2,1)}, u32[]{:S(2)}, u32[]{:S(2)}) collective-permute-start(bf16[16,64,1024]{2,1,0:T(8,128)(2,1)} %fusion.10), channel_id=1, source_target_pairs={{0,16},{16,0},{1,17},{17,1},{2,18},{18,2},{3,19},{19,3},{4,20},{20... | collective-permute-start | bytes 6291464 | tf_op jit(solution)/shard_map/ppermute | solution.py:72
  821.2 58.9 %copy-start.19 = (f32[16,128,1,128]{3,1,0,2:T(8,128)S(1)}, f32[16,128,1,128]{3,1,0,2:T(8,128)}, u32[]{:S(2)}) copy-start(f32[16,128,1,128]{3,1,0,2:T(8,128)} %get-tuple-element.68) | copy-start | bytes 3145732
  821.2 59.2 %copy-start.17 = (bf16[2048,128]{1,0:T(8,128)(2,1)S(1)}, bf16[2048,128]{1,0:T(8,128)(2,1)}, u32[]{:S(2)}) copy-start(bf16[2048,128]{1,0:T(8,128)(2,1)} %copy.144) | copy-start | bytes 1572868
  821.2 381.9 %reduce-scatter.14.cloned.1.call-start = ((), (), s32[]{:S(2)}) async-start(), calls=%async_computation.16 | async-start | bytes 8912896 | tf_op jit(solution)/shard_map/reduce_scatter | solution.py:63
  897.0 65.2 %copy-start.15 = (bf16[2048,128]{1,0:T(8,128)(2,1)S(1)}, bf16[2048,128]{1,0:T(8,128)(2,1)}, u32[]{:S(2)}) copy-start(bf16[2048,128]{1,0:T(8,128)(2,1)} %copy-done.14) | copy-start | bytes 1572868
  977.6 61.1 %all-to-all-start.3 = ((bf16[16,64,1024]{2,1,0:T(8,128)(2,1)}), bf16[16,64,1024]{2,1,0:T(8,128)(2,1)}, u32[]{:S(2)}, u32[]{:S(2)}) async-start(bf16[16,64,1024]{2,1,0:T(8,128)(2,1)} %fusion.5), calls=%async_computation.7 | async-start | bytes 4194304 | tf_op jit(solution)/shard_map/all_to_all | solution.py:96
  989.9 27.5 %copy-start.11 = (bf16[16,128,1,128]{3,1,0,2:T(8,128)(2,1)S(1)}, bf16[16,128,1,128]{3,1,0,2:T(8,128)(2,1)}, u32[]{:S(2)}) copy-start(bf16[16,128,1,128]{3,1,0,2:T(8,128)(2,1)} %copy-done.10) | copy-start | bytes 1572868
  990.0 25.5 %collective-permute-start.6 = (bf16[256,2048]{1,0:T(8,128)(2,1)S(1)}, bf16[256,2048]{1,0:T(8,128)(2,1)S(1)}, u32[]{:S(2)}, u32[]{:S(2)}) collective-permute-start(bf16[256,2048]{1,0:T(8,128)(2,1)S(1)} %fusion.45), channel_id=1, source_target_pairs={{0,16},{16,0},{1,17},{17,1},{2,18},{18,2},{3,19},{19,3},{4,20},{20... | collective-permute-start | bytes 3145736 | tf_op jit(solution)/shard_map/ppermute | solution.py:72
  1015.8 24.8 %collective-permute-start.7 = (bf16[256,2048]{1,0:T(8,128)(2,1)S(1)}, bf16[256,2048]{1,0:T(8,128)(2,1)}, u32[]{:S(2)}, u32[]{:S(2)}) collective-permute-start(bf16[256,2048]{1,0:T(8,128)(2,1)S(1)} %fusion.11), channel_id=1, source_target_pairs={{0,16},{16,0},{1,17},{17,1},{2,18},{18,2},{3,19},{19,3},{4,20},{20... | collective-permute-start | bytes 3145736 | tf_op jit(solution)/shard_map/ppermute | solution.py:79
  1018.4 25.1 %copy-start.25 = (bf16[2048,128]{0,1:T(8,128)(2,1)S(1)}, bf16[2048,128]{0,1:T(8,128)(2,1)}, u32[]{:S(2)}) copy-start(bf16[2048,128]{0,1:T(8,128)(2,1)} %get-tuple-element.26) | copy-start | bytes 1572868
  1018.4 25.1 %copy-start.26 = (bf16[2048,128]{0,1:T(8,128)(2,1)S(1)}, bf16[2048,128]{0,1:T(8,128)(2,1)}, u32[]{:S(2)}) copy-start(bf16[2048,128]{0,1:T(8,128)(2,1)} %get-tuple-element.27) | copy-start | bytes 1572868
  1038.7 44.8 %collective-permute-start.5 = (bf16[16,64,1024]{2,1,0:T(8,128)(2,1)}, bf16[16,64,1024]{2,1,0:T(8,128)(2,1)}, u32[]{:S(2)}, u32[]{:S(2)}) collective-permute-start(bf16[16,64,1024]{2,1,0:T(8,128)(2,1)} %all-to-all-done.3), channel_id=1, source_target_pairs={{0,16},{16,0},{1,17},{17,1},{2,18},{18,2},{3,19},{19,3},{4,20},{20... | collective-permute-start | bytes 6291464 | tf_op jit(solution)/shard_map/ppermute | solution.py:79
  1055.5 52.1 %collective-permute-start = (bf16[16,64,384]{2,1,0:T(8,128)(2,1)}, bf16[16,64,384]{2,1,0:T(8,128)(2,1)}, u32[]{:S(2)}, u32[]{:S(2)}) collective-permute-start(bf16[16,64,384]{2,1,0:T(8,128)(2,1)} %fusion.50), channel_id=1, source_target_pairs={{0,16},{16,0},{1,17},{17,1},{2,18},{18,2},{3,19},{19,3},{4,20},{20... | collective-permute-start | bytes 2359304 | tf_op jit(solution)/shard_map/ppermute | solution.py:72
  1109.8 63.5 %all-to-all-start.2 = ((bf16[16,64,384]{2,1,0:T(8,128)(2,1)}), bf16[16,64,384]{2,1,0:T(8,128)(2,1)}, u32[]{:S(2)}, u32[]{:S(2)}) async-start(bf16[16,64,384]{2,1,0:T(8,128)(2,1)} %fusion.15), calls=%async_computation.6 | async-start | bytes 1572864 | tf_op jit(solution)/shard_map/all_to_all | solution.py:96
  1147.6 15.7 %collective-permute-start.2 = (bf16[64,2048]{1,0:T(8,128)(2,1)S(1)}, bf16[64,2048]{1,0:T(8,128)(2,1)}, u32[]{:S(2)}, u32[]{:S(2)}) collective-permute-start(bf16[64,2048]{1,0:T(8,128)(2,1)S(1)} %fusion.81), channel_id=1, source_target_pairs={{0,16},{16,0},{1,17},{17,1},{2,18},{18,2},{3,19},{19,3},{4,20},{20... | collective-permute-start | bytes 786440 | tf_op jit(solution)/shard_map/ppermute | solution.py:72
  1164.3 9.5 collective-permute-start.3
  1173.3 18.9 %collective-permute-start.1 = (bf16[16,64,384]{2,1,0:T(8,128)(2,1)}, bf16[16,64,384]{2,1,0:T(8,128)(2,1)S(1)}, u32[]{:S(2)}, u32[]{:S(2)}) collective-permute-start(bf16[16,64,384]{2,1,0:T(8,128)(2,1)} %all-to-all-done.2), channel_id=1, source_target_pairs={{0,16},{16,0},{1,17},{17,1},{2,18},{18,2},{3,19},{19,3},{4,20},{20... | collective-permute-start | bytes 2359304 | tf_op jit(solution)/shard_map/ppermute | solution.py:79
  (24 other events, 134.1 us)
Sparse Core Ops, SparseCore 0:
  10.2 103.3 all-gather.6
  202.0 100.8 reduce-scatter.7
  306.4 133.9 all-gather.8
  486.3 103.4 reduce-scatter.9
  595.3 73.9 all-gather.10
  693.8 102.0 reduce-scatter.11
  800.3 73.9 all-gather.12
  877.9 56.2 reduce-scatter.15
  972.7 130.4 reduce-scatter.13

commit v2 on v1

--- a/solution.py
+++ b/solution.py
@@ -1,6 +1,10 @@
+import functools
+
 import jax
 import jax.numpy as jnp
 from jax import lax
+from jax.experimental import pallas as pl
+from jax.experimental.pallas import tpu as pltpu
 from jax.sharding import PartitionSpec as P
 
 H = 16
@@ -8,6 +12,733 @@
 THETA = 500000.0
 BF = jnp.bfloat16
 F32 = jnp.float32
+MESH = pl.DeviceIdType.MESH
+DMA = pltpu.SemaphoreType.DMA
+ANY = pl.BlockSpec(memory_space=pl.ANY)
+VM = pl.BlockSpec(memory_space=pltpu.VMEM)
+CHUNKS = 2
+VMEM_LIMIT = 62 << 20
+
+
+def position(n_shard):
+    s = lax.axis_index("shard")
+    return s // 4, (s // 2) % 2, s % 2, n_shard // 4
+
+
+def index(a, b, c):
+    return (a * 2 + b) * 2 + c
+
+
+def line_order(t, a, na):
+    m = jnp.minimum(a, na - 1 - a)
+    near = jnp.where(t % 2 == 1, a - (t + 1) // 2, a + (t + 1) // 2)
+    far = jnp.where(m == a, t, na - 1 - t)
+    return jnp.where(t <= 2 * m, near, far)
+
+
+def rows_of(i, size):
+    return pl.ds(pl.multiple_of(i * size, size), size)
+
+
+def send(src, dst, ssem, rsem, **target):
+    return pltpu.make_async_remote_copy(
+        src_ref=src, dst_ref=dst, send_sem=ssem, recv_sem=rsem,
+        device_id=target, device_id_type=MESH,
+    )
+
+
+def signal(sem, **target):
+    pl.semaphore_signal(sem, inc=1, device_id=target, device_id_type=MESH)
+
+
+def greet(pos):
+    barrier = pltpu.get_barrier_semaphore()
+    a, b, c, na = pos
+
+    @pl.when(a > 0)
+    def _():
+        signal(barrier, shard=index(a - 1, b, c))
+
+    @pl.when(a < na - 1)
+    def _():
+        signal(barrier, shard=index(a + 1, b, c))
+
+    signal(barrier, shard=index(a, 1 - b, c))
+    signal(barrier, shard=index(a, b, 1 - c))
+    pl.semaphore_wait(barrier, 2 + (a > 0).astype(jnp.int32) + (a < na - 1).astype(jnp.int32))
+
+
+def greet_all(n_shard, n_rep):
+    barrier = pltpu.get_barrier_semaphore()
+    s, r = lax.axis_index("shard"), lax.axis_index("rep")
+
+    def one(k, _):
+        signal(barrier, shard=lax.rem(s + k, n_shard))
+        return 0
+
+    lax.fori_loop(1, n_shard, one, 0)
+    for k in range(1, n_rep):
+        signal(barrier, rep=lax.rem(r + k, n_rep))
+    pl.semaphore_wait(barrier, n_shard - 1 + n_rep - 1)
+
+
+def gather_sems(n_shard):
+    na = n_shard // 4
+    return [
+        DMA((n_shard * CHUNKS,)), DMA((na * CHUNKS,)), DMA((na * CHUNKS,)),
+        DMA((na * CHUNKS,)), DMA((2 * na * CHUNKS,)),
+    ]
+
+
+def gather_loop(pos, count, buf, sems, on_chip, hook=None):
+    recv, up, down, ysend, csend = sems
+    a, b, c, na = pos
+    rows = count // CHUNKS
+
+    def desc(i, ch, ssem, target):
+        piece = buf.at[pl.ds(pl.multiple_of(i * count + ch * rows, rows), rows)]
+        return send(piece, piece, ssem, recv.at[i * CHUNKS + ch], shard=target)
+
+    def sends(j, ch):
+        i = index(j, b, c)
+
+        @pl.when((j <= a) & (a < na - 1))
+        def _():
+            desc(i, ch, up.at[j * CHUNKS + ch], index(a + 1, b, c)).start()
+
+        @pl.when((j >= a) & (a > 0))
+        def _():
+            desc(i, ch, down.at[j * CHUNKS + ch], index(a - 1, b, c)).start()
+
+        desc(i, ch, ysend.at[j * CHUNKS + ch], index(a, 1 - b, c)).start()
+        desc(i, ch, csend.at[(j * 2 + b) * CHUNKS + ch], index(a, b, 1 - c)).start()
+
+    def arrived(i, ch):
+        desc(i, ch, csend.at[0], index(a, b, 1 - c)).wait_recv()
+
+    def pair_step(j):
+        i = index(j, 1 - b, c)
+        for ch in range(CHUNKS):
+            arrived(i, ch)
+            desc(i, ch, csend.at[(j * 2 + 1 - b) * CHUNKS + ch], index(a, b, 1 - c)).start()
+        for ch in range(CHUNKS):
+            arrived(index(j, 1 - b, 1 - c), ch)
+        on_chip(j * 2 + 1 - b)
+
+    def step(t, _):
+        j = line_order(t, a, na)
+        for ch in range(CHUNKS):
+
+            @pl.when(t > 0)
+            def _():
+                arrived(index(j, b, c), ch)
+
+            sends(j, ch)
+        if hook is not None:
+            hook(t)
+        for ch in range(CHUNKS):
+            arrived(index(j, b, 1 - c), ch)
+        on_chip(j * 2 + b)
+
+        @pl.when(t > 0)
+        def _():
+            pair_step(line_order(t - 1, a, na))
+
+        return 0
+
+    lax.fori_loop(0, na, step, 0)
+    pair_step(line_order(na - 1, a, na))
+
+    def finish(j, _):
+        i = index(j, b, c)
+        for ch in range(CHUNKS):
+
+            @pl.when((j <= a) & (a < na - 1))
+            def _():
+                desc(i, ch, up.at[j * CHUNKS + ch], index(a, b, 1 - c)).wait_send()
+
+            @pl.when((j >= a) & (a > 0))
+            def _():
+                desc(i, ch, down.at[j * CHUNKS + ch], index(a, b, 1 - c)).wait_send()
+
+            desc(i, ch, ysend.at[j * CHUNKS + ch], index(a, 1 - b, c)).wait_send()
+            for bb in range(2):
+                slot = (j * 2 + bb) * CHUNKS + ch
+                desc(index(j, bb, c), ch, csend.at[slot], index(a, b, 1 - c)).wait_send()
+        return 0
+
+    lax.fori_loop(0, na, finish, 0)
+
+
+def scatter_sems(n_shard):
+    na = n_shard // 4
+    return [DMA((2 * na,)), DMA((2 * na,)), DMA((na,)), DMA((na,)), DMA((na,)), DMA((na + 1,))]
+
+
+def scatter_bufs(n_shard, count, width):
+    na = n_shard // 4
+    return [
+        pltpu.VMEM((n_shard * count, width), BF), pltpu.VMEM((2 * na * count, width), BF),
+        pltpu.VMEM((na * count, width), BF), pltpu.VMEM(((na + 1) * count, width), BF),
+    ]
+
+
+def scatter_loop(pos, count, bufs, sems, partial, out, hook=None):
+    p, cgot, ygot, zgot = bufs
+    csend, crecv, ysend, yrecv, zsend, zrecv = sems
+    a, b, c, na = pos
+    tile = 32
+
+    def to_core(q):
+        return send(
+            p.at[rows_of(q * 2 + 1 - c, count)], cgot.at[rows_of(q, count)],
+            csend.at[q], crecv.at[q], shard=index(a, b, 1 - c),
+        )
+
+    def to_pair(j):
+        return send(
+            p.at[rows_of(index(j, 1 - b, c), count)], ygot.at[rows_of(j, count)],
+            ysend.at[j], yrecv.at[j], shard=index(a, 1 - b, c),
+        )
+
+    def along(j, slot, target):
+        return send(
+            p.at[rows_of(index(j, b, c), count)], zgot.at[rows_of(slot, count)],
+            zsend.at[j], zrecv.at[slot], shard=target,
+        )
+
+    def add(i, others, into=None):
+        def one(k, _):
+            def at(slot):
+                return pl.ds(pl.multiple_of(slot * count + k * tile, tile), tile)
+
+            total = p[at(i), :].astype(F32)
+            for ref, slot in others:
+                total = total + ref[at(slot), :].astype(F32)
+            if into is None:
+                p[at(i), :] = total.astype(BF)
+            else:
+                into[at(0), :] = total
+            return 0
+
+        lax.fori_loop(0, count // tile, one, 0)
+
+    def first(t, _):
+        j = line_order(na - 1 - t, a, na)
+        far, near = j * 2 + 1 - b, j * 2 + b
+        partial(far)
+        to_core(far).start()
+        partial(near)
+        to_core(near).start()
+        to_core(far).wait_recv()
+        add(index(j, 1 - b, c), [(cgot, far)])
+        to_pair(j).start()
+        return 0
+
+    lax.fori_loop(0, na, first, 0)
+
+    def second(t, _):
+        j = line_order(na - 1 - t, a, na)
+        near = j * 2 + b
+        i = index(j, b, c)
+        if hook is not None:
+            hook(t)
+        to_core(near).wait_recv()
+        to_pair(j).wait_recv()
+        inner = ((j < a) & (a < na - 1)) | ((j > a) & (a > 0))
+
+        @pl.when(inner)
+        def _():
+            along(j, j, index(a, b, 1 - c)).wait_recv()
+            add(i, [(cgot, near), (ygot, j), (zgot, j)])
+
+        @pl.when(jnp.logical_not(inner))
+        def _():
+            add(i, [(cgot, near), (ygot, j)])
+
+        @pl.when(j > a)
+        def _():
+            along(j, j, index(a + 1, b, c)).start()
+
+        @pl.when(j < a)
+        def _():
+            along(j, jnp.where(j == a - 1, na, j), index(a - 1, b, c)).start()
+
+        return 0
+
+    lax.fori_loop(0, na - 1, second, 0)
+    near = a * 2 + b
+    to_core(near).wait_recv()
+    to_pair(a).wait_recv()
+    add(index(a, b, c), [(cgot, near), (ygot, a)], out)
+
+    def more(slot):
+        along(a, slot, index(a, b, 1 - c)).wait_recv()
+
+        def one(k, _):
+            got = zgot[pl.ds(pl.multiple_of(slot * count + k * tile, tile), tile), :]
+            out[rows_of(k, tile), :] += got.astype(F32)
+            return 0
+
+        lax.fori_loop(0, count // tile, one, 0)
+
+    @pl.when(a > 0)
+    def _():
+        more(a)
+
+    @pl.when(a < na - 1)
+    def _():
+        more(na)
+
+    def finish(j, _):
+        for bb in range(2):
+            to_core(j * 2 + bb).wait_send()
+        to_pair(j).wait_send()
+
+        @pl.when(j != a)
+        def _():
+            along(j, j, index(a, b, 1 - c)).wait_send()
+
+        return 0
+
+    lax.fori_loop(0, na, finish, 0)
+
+
+def columns_sems(n_shard, n_rep, groups):
+    return [
+        DMA((n_shard * groups,)), DMA((n_shard * groups,)),
+        DMA((n_shard * n_rep,)), DMA((n_shard * n_rep,)), DMA((groups + 1,)),
+    ]
+
+
+class Columns:
+    def __init__(self, w, out, stage, sems, groups, n_shard, n_rep):
+        self.w, self.out, self.stage, self.groups = w, out, stage, groups
+        self.ssem, self.rsem, self.fsend, self.frecv, self.lsem = sems
+        self.n_shard, self.n_rep = n_shard, n_rep
+        self.own = w.shape[0]
+        self.share = self.own // n_rep
+        self.total = w.shape[1] // groups
+        self.width = self.total // n_shard
+        self.s, self.r = lax.axis_index("shard"), lax.axis_index("rep")
+
+    def move(self, source, target, g):
+        cols = pl.ds(pl.multiple_of(g * self.total + target * self.width, 128), self.width)
+        src = self.w.at[rows_of(self.r, self.share), cols]
+        at = pl.ds(pl.multiple_of(source * self.own + self.r * self.share, self.share), self.share)
+        dst = self.out.at[at, pl.ds(g * self.width, self.width)]
+        return send(
+            src, dst, self.ssem.at[target * self.groups + g],
+            self.rsem.at[source * self.groups + g], shard=target,
+        )
+
+    def pass_on(self, source, k, replica):
+        at = pl.ds(
+            pl.multiple_of(source * self.own + replica * self.share, self.share), self.share
+        )
+        piece = self.out.at[at]
+        return send(
+            piece, piece, self.fsend.at[source * self.n_rep + k],
+            self.frecv.at[source * self.n_rep + replica],
+            rep=lax.rem(self.r + k, self.n_rep),
+        )
+
+    def local_in(self, g):
+        cols = pl.ds(pl.multiple_of(g * self.total + self.s * self.width, 128), self.width)
+        return pltpu.make_async_copy(
+            self.w.at[:, cols], self.stage.at[:, pl.ds(g * self.width, self.width)], self.lsem.at[g]
+        )
+
+    def local_out(self):
+        return pltpu.make_async_copy(
+            self.stage, self.out.at[rows_of(self.s, self.own)], self.lsem.at[self.groups]
+        )
+
+    def start(self):
+        for g in range(self.groups):
+            self.local_in(g).start()
+
+        def one(k, _):
+            target = lax.rem(self.s + k, self.n_shard)
+            for g in range(self.groups):
+                self.move(self.s, target, g).start()
+            return 0
+
+        lax.fori_loop(1, self.n_shard, one, 0)
+        for g in range(self.groups):
+            self.local_in(g).wait()
+        self.local_out().start()
+
+    def forward(self, low, high):
+        def one(k, _):
+            source = lax.rem(self.s + self.n_shard - k, self.n_shard)
+            for g in range(self.groups):
+                self.move(source, self.s, g).wait_recv()
+            for m in range(1, self.n_rep):
+                self.pass_on(source, m, self.r).start()
+            return 0
+
+        lax.fori_loop(low, high, one, 0)
+
+    def finish(self):
+        def one(k, _):
+            source = lax.rem(self.s + self.n_shard - k, self.n_shard)
+            for g in range(self.groups):
+                self.move(self.s, source, g).wait_send()
+            for m in range(1, self.n_rep):
+                self.pass_on(source, m, self.r).wait_send()
+                self.pass_on(source, m, lax.rem(self.r + m, self.n_rep)).wait_recv()
+            return 0
+
+        lax.fori_loop(1, self.n_shard, one, 0)
+        self.local_out().wait()
+
+    def spread(self, t, steps):
+        each = -(-(self.n_shard - 1) // steps)
+        low = 1 + t * each
+        self.forward(low, jnp.minimum(low + each, self.n_shard))
+
+
+def mm(left, right):
+    return jnp.dot(left, right, preferred_element_type=F32)
+
+
+def mm_nt(left, right):
+    return lax.dot_general(left, right, (((1,), (1,)), ((), ())), preferred_element_type=F32)
+
+
+def mm_tn(left, right):
+    return lax.dot_general(left, right, (((0,), (0,)), ((), ())), preferred_element_type=F32)
+
+
+def call(kernel, name, cid, outs, ins, scratch, *args, flops=0, moved=0):
+    return pl.pallas_call(
+        kernel,
+        name=name,
+        out_shape=[jax.ShapeDtypeStruct(shape, dtype) for shape, dtype, _ in outs],
+        in_specs=ins,
+        out_specs=[spec for _, _, spec in outs],
+        scratch_shapes=scratch,
+        compiler_params=pltpu.CompilerParams(
+            collective_id=cid, has_side_effects=True, vmem_limit_bytes=VMEM_LIMIT
+        ),
+        cost_estimate=pl.CostEstimate(flops=flops, bytes_accessed=moved, transcendentals=0),
+    )(*args)
+
+
+def load(src, dst, sem):
+    cp = pltpu.make_async_copy(src, dst, sem)
+    cp.start()
+    return cp
+
+
+def own_rows(pos, count):
+    a, b, c, _ = pos
+    return rows_of(index(a, b, c), count)
+
+
+class Out:
+    def __init__(self, src, dst, sem, size):
+        self.src, self.dst, self.sem, self.size = src, dst, sem, size
+
+    def desc(self, q):
+        r = rows_of(q, self.size)
+        return pltpu.make_async_copy(self.src.at[r], self.dst.at[r], self.sem.at[q])
+
+    def start(self, q):
+        self.desc(q).start()
+
+    def wait(self, q):
+        self.desc(q).wait()
+
+
+def wait_all(outs, chips):
+    def one(q, _):
+        for o in outs:
+            o.wait(q)
+        return 0
+
+    lax.fori_loop(0, chips, one, 0)
+
+
+def qkv_kernel(
+    n_shard, n_rep, x_ref, w_ref, g_ref, qkv_ref, cols_ref, sums_ref,
+    buf, wq, stage, qkv, stats, got, lsem, osem, vsem, xs, xr, *sems,
+):
+    pos = position(n_shard)
+    count = x_ref.shape[0]
+    chips = n_shard // 2
+    big = 2 * count
+    own = stage.shape[1] // 3
+    na = pos[3]
+    s = lax.axis_index("shard")
+    mine = load(x_ref, buf.at[own_rows(pos, count)], lsem.at[0])
+    weights = Columns(w_ref, cols_ref, stage, sems[5:], 3, n_shard, n_rep)
+    greet_all(n_shard, n_rep)
+    mine.wait()
+    out_x = Out(buf, g_ref, osem, big)
+
+    def hook(t):
+        @pl.when(t == 0)
+        def _():
+            weights.start()
+
+        @pl.when(t > 0)
+        def _():
+            weights.spread(t - 1, na - 1)
+
+    gather_loop(pos, count, buf, sems[:5], out_x.start, hook)
+    weights.finish()
+    pltpu.sync_copy(cols_ref, wq)
+    out_v = Out(qkv, qkv_ref, vsem, big)
+    ones = jnp.ones((8, own), F32)
+
+    def one(q, _):
+        r = rows_of(q, big)
+        v = mm(buf[r, :], wq[...])
+        qkv[r, :] = v
+        for g in range(2):
+            x = v[:, g * own : (g + 1) * own]
+            total = lax.dot_general(
+                ones, x * x, (((1,), (1,)), ((), ())),
+                preferred_element_type=F32, precision=lax.Precision.HIGHEST,
+            )
+            stats[pl.ds(g, 1), pl.ds(pl.multiple_of(q * big, big), big)] = total[:1]
+        out_v.start(q)
+        return 0
+
+    lax.fori_loop(0, chips, one, 0)
+    exchange(n_shard, stats, got, xs, xr, sums_ref)
+    wait_all([out_x, out_v], chips)
+
+
+def exchange(n_shard, stats, got, xs, xr, sums_ref):
+    s = lax.axis_index("shard")
+
+    def desc(k):
+        target = lax.rem(s + k, n_shard)
+        return send(stats, got.at[k - 1], xs.at[k - 1], xr.at[k - 1], shard=target)
+
+    def start(k, _):
+        desc(k).start()
+        return 0
+
+    lax.fori_loop(1, n_shard, start, 0)
+    sums_ref[...] = stats[...]
+
+    def take(k, _):
+        desc(k).wait_recv()
+        sums_ref[...] += got[k - 1]
+        return 0
+
+    lax.fori_loop(1, n_shard, take, 0)
+
+    def done(k, _):
+        desc(k).wait_send()
+        return 0
+
+    lax.fori_loop(1, n_shard, done, 0)
+
+
+def sum_kernel(n_shard, x_ref, sums_ref, stats, got, xs, xr):
+    barrier = pltpu.get_barrier_semaphore()
+    s = lax.axis_index("shard")
+
+    def one(k, _):
+        signal(barrier, shard=lax.rem(s + k, n_shard))
+        return 0
+
+    lax.fori_loop(1, n_shard, one, 0)
+    stats[...] = x_ref[...]
+    pl.semaphore_wait(barrier, n_shard - 1)
+    exchange(n_shard, stats, got, xs, xr, sums_ref)
+
+
+def attn_out_kernel(
+    n_shard, n_rep, ctx_ref, wo_ref, w_ref, out_ref, cols_ref, stage, *rest,
+):
+    pos = position(n_shard)
+    na = pos[3]
+    bufs, sems, csems = rest[:4], rest[4:10], rest[10:]
+    p = bufs[0]
+    count = out_ref.shape[0]
+    big = 2 * count
+    width = out_ref.shape[1]
+    weights = Columns(w_ref, cols_ref, stage, csems, 2, n_shard, n_rep)
+    greet_all(n_shard, n_rep)
+
+    def partial(q):
+        r = rows_of(q, big)
+        p[r, :] = mm(ctx_ref[r, :], wo_ref[...]).astype(BF)
+
+    def hook(t):
+        @pl.when(t == 0)
+        def _():
+            weights.start()
+
+        @pl.when(t > 0)
+        def _():
+            weights.spread(t - 1, na - 1)
+
+    scatter_loop(pos, count, bufs, sems, partial, out_ref, hook)
+    weights.spread(na - 2, na - 1)
+    weights.finish()
+
+
+def mlp_kernel(
+    n_shard, x_ref, wg_ref, wd_ref, g_ref, gu_ref, mixed_ref, out_ref,
+    buf, wg, wd, gu, mixed, lsem, osem, gsem, msem, *rest,
+):
+    pos = position(n_shard)
+    bufs, ssems, gsems = rest[:4], rest[4:10], rest[10:]
+    p = bufs[0]
+    count, width = out_ref.shape
+    big = 2 * count
+    chips = n_shard // 2
+    ff = wd.shape[0]
+    mine = load(x_ref, buf.at[own_rows(pos, count)], lsem.at[0])
+    w1 = load(wg_ref, wg, lsem.at[1])
+    w2 = load(wd_ref, wd, lsem.at[2])
+    greet(pos)
+    mine.wait()
+    out_x, out_g = Out(buf, g_ref, osem, big), Out(gu, gu_ref, gsem, big)
+    out_m = Out(mixed, mixed_ref, msem, big)
+    w1.wait()
+
+    def on_chip(q):
+        r = rows_of(q, big)
+        out_x.start(q)
+
+        def one(k, _):
+            lo = pl.ds(pl.multiple_of(k * 256, 256), 256)
+            hi = pl.ds(pl.multiple_of(ff + k * 256, 256), 256)
+            gate = mm(buf[r, :], wg[:, lo])
+            up = mm(buf[r, :], wg[:, hi])
+            gu[r, lo] = gate
+            gu[r, hi] = up
+            mixed[r, lo] = (gate * jax.nn.sigmoid(gate) * up).astype(BF)
+            return 0
+
+        lax.fori_loop(0, ff // 256, one, 0)
+        out_g.start(q)
+        out_m.start(q)
+
+    gather_loop(pos, count, buf, gsems, on_chip)
+    w2.wait()
+
+    def partial(q):
+        r = rows_of(q, big)
+
+        def one(k, _):
+            lo = rows_of(k, 512)
+            p[r, lo] = mm(mixed[r, :], wd[:, lo]).astype(BF)
+            return 0
+
+        lax.fori_loop(0, width // 512, one, 0)
+
+    scatter_loop(pos, count, bufs, ssems, partial, out_ref)
+    wait_all([out_x, out_g, out_m], chips)
+
+
+def mlp_back_kernel(
+    n_shard, x_ref, gu_ref, wg_ref, wd_ref, g_ref, dgu_ref, out_ref,
+    buf, wg, wd, gu, dgu, lsem, isem, osem, dsem, *rest,
+):
+    pos = position(n_shard)
+    bufs, ssems, gsems = rest[:4], rest[4:10], rest[10:]
+    p = bufs[0]
+    count, width = out_ref.shape
+    big = 2 * count
+    chips = n_shard // 2
+    ff = wd.shape[0]
+    mine = load(x_ref, buf.at[own_rows(pos, count)], lsem.at[0])
+    w2 = load(wd_ref, wd, lsem.at[2])
+    saved = Out(gu_ref, gu, isem, big)
+
+    def fetch(q, _):
+        saved.start(q)
+        return 0
+
+    lax.fori_loop(0, chips, fetch, 0)
+    w1 = load(wg_ref, wg, lsem.at[1])
+    greet(pos)
+    mine.wait()
+    out_x, out_d = Out(buf, g_ref, osem, big), Out(dgu, dgu_ref, dsem, big)
+    w2.wait()
+
+    def on_chip(q):
+        r = rows_of(q, big)
+        out_x.start(q)
+        saved.wait(q)
+
+        def one(k, _):
+            lo = pl.ds(pl.multiple_of(k * 256, 256), 256)
+            hi = pl.ds(pl.multiple_of(ff + k * 256, 256), 256)
+            d_mixed = mm_nt(buf[r, :], wd[lo, :])
+            gate, up = gu[r, lo], gu[r, hi]
+            sigma = jax.nn.sigmoid(gate)
+            d_gate = d_mixed * up * sigma * (1.0 + gate * (1.0 - sigma))
+            dgu[r, lo] = d_gate.astype(BF)
+            dgu[r, hi] = (d_mixed * gate * sigma).astype(BF)
+            return 0
+
+        lax.fori_loop(0, ff // 256, one, 0)
+        out_d.start(q)
+
+    gather_loop(pos, count, buf, gsems, on_chip)
+    w1.wait()
+
+    def partial(q):
+        r = rows_of(q, big)
+
+        def one(k, _):
+            lo = rows_of(k, 256)
+            p[r, lo] = mm_nt(dgu[r, :], wg[lo, :]).astype(BF)
+            return 0
+
+        lax.fori_loop(0, width // 256, one, 0)
+
+    scatter_loop(pos, count, bufs, ssems, partial, out_ref)
+    wait_all([out_x, out_d], chips)
+
+
+def context_back_kernel(n_shard, x_ref, wo_ref, g_ref, ctx_ref, buf, lsem, osem, *gsems):
+    pos = position(n_shard)
+    count = x_ref.shape[0]
+    big = 2 * count
+    mine = load(x_ref, buf.at[own_rows(pos, count)], lsem.at[0])
+    greet(pos)
+    mine.wait()
+    out_x = Out(buf, g_ref, osem, big)
+
+    def on_chip(q):
+        r = rows_of(q, big)
+        out_x.start(q)
+        ctx_ref[r, :] = mm_nt(buf[r, :], wo_ref[...]).astype(BF)
+
+    gather_loop(pos, count, buf, gsems, on_chip)
+    wait_all([out_x], n_shard // 2)
+
+
+def tokens_back_kernel(n_shard, d_ref, wq_ref, out_ref, *rest):
+    pos = position(n_shard)
+    bufs, sems = rest[:4], rest[4:]
+    p = bufs[0]
+    count, width = out_ref.shape
+    big = 2 * count
+    greet(pos)
+
+    def partial(q):
+        r = rows_of(q, big)
+
+        def one(k, _):
+            lo = rows_of(k, 512)
+            p[r, lo] = mm_nt(d_ref[r, :], wq_ref[lo, :]).astype(BF)
+            return 0
+
+        lax.fori_loop(0, width // 512, one, 0)
+
+    scatter_loop(pos, count, bufs, sems, partial, out_ref)
 
 
 def positions(seg):
@@ -33,18 +764,6 @@
     return jnp.concatenate([a * cosine - b * sine, b * cosine + a * sine], axis=-1)
 
 
-def mm(left, right):
-    return jnp.dot(left, right, preferred_element_type=F32)
-
-
-def mm_nt(left, right):
-    return lax.dot_general(left, right, (((1,), (1,)), ((), ())), preferred_element_type=F32)
-
-
-def mm_tn(left, right):
-    return lax.dot_general(left, right, (((0,), (0,)), ((), ())), preferred_element_type=F32)
-
-
 def norm_scale(vector):
     return lax.rsqrt(jnp.mean(vector * vector, axis=-1, keepdims=True) + EPSILON)
 
@@ -55,15 +774,9 @@
     return rscale * (scaled - normed * inner), jnp.sum(upstream * normed, axis=0)
 
 
-def gather(piece):
-    return lax.all_gather(piece, "shard", axis=0, tiled=True)
-
-
-def scatter(partial):
-    return lax.psum_scatter(partial.astype(BF), "shard", scatter_dimension=0, tiled=True).astype(F32)
-
-
 def make(n_rep, n_shard):
+    chips = n_shard // 2
+
     def rep_scatter(x):
         if n_rep == 2:
             me = lax.axis_index("rep")
@@ -98,11 +811,16 @@
         whole = whole.reshape(n_rep, n_shard, own // n_rep, groups, width)
         return whole.transpose(0, 2, 3, 1, 4).reshape(own, groups * n_shard * width).astype(F32)
 
-    def columns(w, groups):
-        rows, cols = w.shape
-        w = w.reshape(rows, groups, n_shard, cols // (groups * n_shard))
-        w = lax.all_to_all(w, "shard", split_axis=2, concat_axis=0, tiled=True)
-        return w.reshape(rows * n_shard, cols // n_shard)
+    def group_sum(x):
+        return call(
+            functools.partial(sum_kernel, n_shard), "group_sum", 11,
+            [(x.shape, F32, VM)], [VM],
+            [
+                pltpu.VMEM(x.shape, F32), pltpu.VMEM((n_shard - 1,) + x.shape, F32),
+                DMA((n_shard - 1,)), DMA((n_shard - 1,)),
+            ],
+            x,
+        )[0]
 
     def shards(
         tokens, segment_ids, cotangent, w_qkv, w_out, w_gate_up, w_down,
@@ -114,11 +832,11 @@
         own = width // n_shard
         ff = w_down.shape[0]
         total = count * n_shard
-
-        small = gather(jnp.stack([segment_ids.astype(BF), attn_gain, mlp_gain])[None])
-        tokens_g = gather(tokens)
-        wq = columns(w_qkv, 3)
-        wg = columns(w_gate_up, 2)
+        gathered = pltpu.VMEM((total, width), BF)
+
+        small = lax.all_gather(
+            jnp.stack([segment_ids.astype(BF), attn_gain, mlp_gain])[None], "shard", axis=0, tiled=True
+        )
         seg = small[:, 0].astype(jnp.int32)
         gain_attn = small[:, 1].reshape(-1).astype(F32)
         gain_mlp = small[:, 2].reshape(-1).astype(F32)
@@ -128,10 +846,22 @@
         cos3 = cosine[:, None, :]
         sin3 = sine[:, None, :]
 
-        qkv = mm(tokens_g, wq)
+        tokens_g, qkv, wq, squares = call(
+            functools.partial(qkv_kernel, n_shard, n_rep), "qkv", 1,
+            [
+                ((total, width), BF, ANY), ((total, 3 * own), F32, ANY),
+                ((width, 3 * own), BF, ANY), ((2, total), F32, VM),
+            ],
+            [ANY, ANY],
+            [
+                gathered, pltpu.VMEM((width, 3 * own), BF), pltpu.VMEM((own, 3 * own), BF),
+                pltpu.VMEM((total, 3 * own), F32), pltpu.VMEM((2, total), F32),
+                pltpu.VMEM((n_shard - 1, 2, total), F32),
+                DMA((1,)), DMA((chips,)), DMA((chips,)), DMA((n_shard - 1,)), DMA((n_shard - 1,)),
+            ] + gather_sems(n_shard) + columns_sems(n_shard, n_rep, 3),
+            tokens, w_qkv,
+        )
         query, keys, values_b = qkv[:, :own], qkv[:, own : 2 * own], qkv[:, 2 * own :].astype(BF)
-        squares = jnp.stack([jnp.sum(query * query, axis=-1), jnp.sum(keys * keys, axis=-1)])
-        squares = lax.psum(squares, "shard")
         scales = lax.rsqrt(squares / width + EPSILON)
         query_scale, keys_scale = scales[0][:, None], scales[1][:, None]
         query_hat, keys_hat = query * query_scale, keys * keys_scale
@@ -160,18 +890,32 @@
         context = jnp.einsum("bhts,bshd->bthd", probs_b, vb, preferred_element_type=F32)
         context_b = context.astype(BF).reshape(total, own)
 
-        attn_raw = scatter(mm(context_b, w_out))
+        attn_raw, wg = call(
+            functools.partial(attn_out_kernel, n_shard, n_rep), "attn_out", 2,
+            [((count, width), F32, VM), ((width, 2 * ff), BF, ANY)],
+            [VM, VM, ANY],
+            [pltpu.VMEM((own, 2 * ff), BF)] + scatter_bufs(n_shard, count, width)
+            + scatter_sems(n_shard) + columns_sems(n_shard, n_rep, 2),
+            context_b, w_out, w_gate_up,
+        )
         attn_scale = norm_scale(attn_raw)
         attn_hat = attn_raw * attn_scale
         resid = tokens.astype(F32) + attn_hat * gain_attn
-        resid_g = gather(resid.astype(BF))
-
-        gate_up = mm(resid_g, wg)
-        gate, up = gate_up[:, :ff], gate_up[:, ff:]
-        sigma = jax.nn.sigmoid(gate)
-        activated = gate * sigma
-        mixed_b = (activated * up).astype(BF)
-        down_raw = scatter(mm(mixed_b, w_down))
+
+        resid_g, gate_up, mixed_b, down_raw = call(
+            functools.partial(mlp_kernel, n_shard), "mlp", 3,
+            [
+                ((total, width), BF, ANY), ((total, 2 * ff), F32, ANY),
+                ((total, ff), BF, ANY), ((count, width), F32, VM),
+            ],
+            [ANY, ANY, ANY],
+            [
+                gathered, pltpu.VMEM((width, 2 * ff), BF), pltpu.VMEM((ff, width), BF),
+                pltpu.VMEM((total, 2 * ff), F32), pltpu.VMEM((total, ff), BF),
+                DMA((3,)), DMA((chips,)), DMA((chips,)), DMA((chips,)),
+            ] + scatter_bufs(n_shard, count, width) + scatter_sems(n_shard) + gather_sems(n_shard),
+            resid.astype(BF), wg, w_down,
+        )
         down_scale = norm_scale(down_raw)
         down_hat = down_raw * down_scale
         output = (resid + down_hat * gain_mlp).astype(BF)
@@ -179,18 +923,29 @@
         valid = (segment_ids >= 0).astype(F32)[:, None]
         d_out = cotangent.astype(F32) * valid
         d_down, grad_mlp = norm_back(d_out, down_hat, down_scale, gain_mlp)
-        d_down_g = gather(d_down.astype(BF))
-        d_mixed = mm_nt(d_down_g, w_down)
-        d_gate = d_mixed * up * sigma * (1.0 + gate * (1.0 - sigma))
-        d_up = d_mixed * activated
-        d_gu_b = jnp.concatenate([d_gate, d_up], axis=1).astype(BF)
-        d_resid = d_out + scatter(mm_nt(d_gu_b, wg))
+        d_down_g, d_gu_b, d_resid_sum = call(
+            functools.partial(mlp_back_kernel, n_shard), "mlp_back", 4,
+            [((total, width), BF, ANY), ((total, 2 * ff), BF, ANY), ((count, width), F32, VM)],
+            [ANY, ANY, ANY, ANY],
+            [
+                gathered, pltpu.VMEM((width, 2 * ff), BF), pltpu.VMEM((ff, width), BF),
+                pltpu.VMEM((total, 2 * ff), F32), pltpu.VMEM((total, 2 * ff), BF),
+                DMA((3,)), DMA((chips,)), DMA((chips,)), DMA((chips,)),
+            ] + scatter_bufs(n_shard, count, width) + scatter_sems(n_shard) + gather_sems(n_shard),
+            d_down.astype(BF), gate_up, wg, w_down,
+        )
+        d_resid = d_out + d_resid_sum
         grad_down = rep_sum(mm_tn(mixed_b, d_down_g))
         grad_gu = grad_back(mm_tn(resid_g, d_gu_b), 2)
 
         d_attn, grad_attn = norm_back(d_resid, attn_hat, attn_scale, gain_attn)
-        d_attn_g = gather(d_attn.astype(BF))
-        d_context_b = mm_nt(d_attn_g, w_out).astype(BF)
+        d_attn_g, d_context_b = call(
+            functools.partial(context_back_kernel, n_shard), "context_back", 5,
+            [((total, width), BF, ANY), ((total, own), BF, VM)],
+            [ANY, VM],
+            [gathered, DMA((1,)), DMA((chips,))] + gather_sems(n_shard),
+            d_attn.astype(BF), w_out,
+        )
         grad_out = rep_sum(mm_tn(context_b, d_attn_g))
 
         db = blocks(d_context_b)
@@ -206,16 +961,21 @@
         grad_keys = jnp.sum(d_keys_norm * keys_hat, axis=0)
         query_up = d_query_norm * gain_query
         keys_up = d_keys_norm * gain_keys
-        inner = jnp.stack(
-            [jnp.sum(query_up * query_hat, axis=-1), jnp.sum(keys_up * keys_hat, axis=-1)]
-        )
-        inner = lax.psum(inner, "shard") / width
+        inner = group_sum(
+            jnp.stack([jnp.sum(query_up * query_hat, axis=-1), jnp.sum(keys_up * keys_hat, axis=-1)])
+        ) / width
         d_query = query_scale * (query_up - query_hat * inner[0][:, None])
         d_keys = keys_scale * (keys_up - keys_hat * inner[1][:, None])
         d_qkv_b = jnp.concatenate(
             [d_query, d_keys, d_values.reshape(total, own)], axis=1
         ).astype(BF)
-        grad_tokens = d_resid + scatter(mm_nt(d_qkv_b, wq))
+        d_tokens_sum = call(
+            functools.partial(tokens_back_kernel, n_shard), "tokens_back", 6,
+            [((count, width), F32, VM)], [VM, VM],
+            scatter_bufs(n_shard, count, width) + scatter_sems(n_shard),
+            d_qkv_b, wq,
+        )[0]
+        grad_tokens = d_resid + d_tokens_sum
         grad_qkv = grad_back(mm_tn(tokens_g, d_qkv_b), 3)
 
         gains_local = lax.psum_scatter(

time: 1220 us -> 851 us (0.70)
  Pallas kernels: 0 us -> 558 us
  waiting for transfers between devices: 548 us -> 72.2 us
  blocking collectives: 327 us -> 26.5 us
  matrix products: 110 us -> 40.3 us
  local copies, waits for them, and re-layouts: 96.9 us -> 39.2 us
  starting transfers between devices: 56.4 us -> 19.3 us
    pallas_call x0 -> x7, Pallas kernels: none -> 558 us  [call(): pl.pallas_call(kernel, name=name, out_shape=[jax.ShapeDtypeStruct(shape,...]
    reduce_scatter x4 -> x0, waiting for transfers between devices: 307 us -> none  [scatter(): lax.psum_scatter(partial.astype(BF), 'shard', scatter_dimension=0, tiled=...]
    all_gather x4 -> x0, waiting for transfers between devices: 157 us -> none  [gather(): return lax.all_gather(piece, 'shard', axis=0, tiled=True)]
    all_to_all x1 -> x0, blocking collectives: 142 us -> none  [columns(): w = lax.all_to_all(w, 'shard', split_axis=2, concat_axis=0, tiled=True)]
    psum x2 -> x0, blocking collectives: 119 us -> none  [the longest x1 59.8 us: shards(): inner = lax.psum(inner, 'shard') / width]
    dot_general x8 -> x0, matrix products: 70.4 us -> none  [the longest x4 37.9 us: mm_nt(): lax.dot_general(left, right, (((1,), (1,)), ((), ())), preferred_element_...]
    all_gather x1, blocking collectives: 58.7 us -> 21.6 us  [shards(): lax.all_gather(jnp.stack([segment_ids.astype(BF), attn_gain, mlp_gain])[N...]
    ppermute x4, waiting for transfers between devices: 39.9 us -> 72.1 us  [rep_gather(): got = lax.ppermute(x, 'rep', [(0, 1), (1, 0)])]
  transfers between devices with their start and end apart: 20 -> 11, of which waited for: 11 -> 2; matrix products, arithmetic and copies ran while one was open for 14% -> 11% of each run, Pallas kernels for 0% -> 16%
where the time goes in v2:
time: 851 us; the launch traced here: 841 us
  Pallas kernels  558 us (66%)
  waiting for transfers between devices  72.2 us (8%)
  other arithmetic  71.3 us (8%)
  matrix products  40.3 us (5%)
  local copies, waits for them, and re-layouts  39.2 us (5%)
  blocking collectives  26.5 us (3%)
  starting transfers between devices  19.3 us (2%)
  between operations  14.9 us (2%)
    pallas_call x7, Pallas kernels, call(): pl.pallas_call(kernel, name=name, out_shape=[jax.ShapeDtypeStruct(shape,...  558 us
    ppermute x4, waiting for transfers between devices, rep_gather(): got = lax.ppermute(x, 'rep', [(0, 1), (1, 0)])  72.1 us
    dot_general x4, matrix products, mm_tn(): lax.dot_general(left, right, (((0,), (0,)), ((), ())), preferred_element_...  36.8 us
    all_gather x1, blocking collectives, shards(): lax.all_gather(jnp.stack([segment_ids.astype(BF), attn_gain, mlp_gain])[N...  21.6 us
  transfers between devices with their start and end apart: 11, of which 2 were waited for; matrix products, arithmetic and copies ran while one was open for 11% of the time, Pallas kernels for 16%

profile of v2, /device:TPU:0, one launch (start us, length us, event | category | flops | bytes accessed | tf_op | source)
XLA Modules:
  0.0 841.4 jit_solution(8155130127148098062)
XLA Ops:
  8.6 81.3 %qkv.1 = (bf16[2048,2048]{1,0:T(8,128)(2,1)}, f32[2048,384]{1,0:T(8,128)}, bf16[2048,384]{1,0:T(8,128)(2,1)}, f32[2,2048]{1,0:T(2,128)}) custom-call(bf16[128,2048]{1,0:T(8,128)(2,1)} %x_ref.1, bf16[128,6144]{1,0:T(8,128)(2,1)} %w_ref.2), custom_call_target="tpu_custom_call" | custom-call | tf_op jit(solution)/shard_map/qkv/pallas_call | solution.py:415
  92.6 21.6 %all-gather.1 = bf16[16,3,128]{2,1,0:T(4,128)(2,1)S(1)} all-gather(bf16[1,3,128]{2,1,0:T(4,128)(2,1)S(1)} %maximum_bitcast_fusion.2), channel_id=2, replica_groups=mesh['rep'=2,'shard'=16] {'shard'}, dimensions={0}, use_global_device_ids=true | all-gather | bytes 13056 | tf_op jit(solution)/shard_map/all_gather | solution.py:837
  118.1 5.1 fusion.36
  126.8 101.4 %attn_out.1 = (f32[128,2048]{1,0:T(8,128)}, bf16[2048,1024]{1,0:T(8,128)(2,1)}) custom-call(bf16[2048,128]{1,0:T(8,128)(2,1)} %bitcast.161, bf16[128,2048]{1,0:T(8,128)(2,1)} %wo_ref.3, bf16[128,16384]{1,0:T(8,128)(2,1)} %w_ref.3), custom_call_target="tpu_custom_call" | custom-call | tf_op jit(solution)/shard_map/attn_out/pallas_call | solution.py:415
  231.9 124.1 %mlp.1 = (bf16[2048,2048]{1,0:T(8,128)(2,1)}, f32[2048,1024]{1,0:T(8,128)}, bf16[2048,512]{1,0:T(8,128)(2,1)}, f32[128,2048]{1,0:T(8,128)}) custom-call(bf16[128,2048]{1,0:T(8,128)(2,1)} %fusion.45.x_ref, bf16[2048,1024]{1,0:T(8,128)(2,1)} %get-tuple-element.28.wg_ref, bf16[512,2048]{1,0:T(8,128)(2,1)} %wd_ref.3), custom_call_target="tpu_custom_call" | custom-call | tf_op jit(solution)/shard_map/mlp/pallas_call | solution.py:415
  360.3 116.5 %mlp_back.1 = (bf16[2048,2048]{1,0:T(8,128)(2,1)}, bf16[2048,1024]{1,0:T(8,128)(2,1)}, f32[128,2048]{1,0:T(8,128)}) custom-call(bf16[128,2048]{1,0:T(8,128)(2,1)} %multiply_convert_fusion.3.x_ref, f32[2048,1024]{1,0:T(8,128)} %get-tuple-element.30.gu_ref, bf16[2048,1024]{1,0:T(8,128)(2,1)} %get-tuple-element.28.wg_ref, bf16[512,2048]{1,0:T(8,128)(2,1)} %wd_ref.3), custom_call_target="tpu_custom_call" | custom-call | tf_op jit(solution)/shard_map/mlp_back/pallas_call | solution.py:415
  479.9 10.6 %fusion.58 = f32[512,2048]{1,0:T(8,128)} fusion(bf16[2048,512]{1,0:T(8,128)(2,1)} %get-tuple-element.38, bf16[2048,2048]{1,0:T(8,128)(2,1)} %get-tuple-element.39), kind=kOutput, calls=%fused_computation.139 | convolution fusion | flops 4294967296 | bytes 14680064 | tf_op jit(solution)/shard_map/dot_general | solution.py:411
  490.5 2.7 fusion.39
  494.8 13.1 %fusion.57 = f32[2048,1024]{1,0:T(8,128)S(1)} fusion(bf16[2048,2048]{1,0:T(8,128)(2,1)} %get-tuple-element.36, bf16[2048,1024]{1,0:T(8,128)(2,1)} %get-tuple-element.37), kind=kOutput, calls=%fused_computation.138 | convolution fusion | flops 8589934592 | bytes 20971520 | tf_op jit(solution)/shard_map/dot_general | solution.py:411
  513.1 56.5 %context_back.1 = (bf16[2048,2048]{1,0:T(8,128)(2,1)}, bf16[2048,128]{1,0:T(8,128)(2,1)}) custom-call(bf16[128,2048]{1,0:T(8,128)(2,1)} %get-tuple-element.64.x_ref, bf16[128,2048]{1,0:T(8,128)(2,1)} %wo_ref.3), custom_call_target="tpu_custom_call" | custom-call | tf_op jit(solution)/shard_map/context_back/pallas_call | solution.py:415
  570.9 4.8 fusion
  577.9 6.0 fusion.29
  583.9 3.9 multiply_reduce_fusion.1
  588.4 9.3 %group_sum.1 = f32[2,2048]{1,0:T(2,128)} custom-call(f32[2,2048]{1,0:T(2,128)} %pad_maximum_fusion.5.x_ref), custom_call_target="tpu_custom_call" | custom-call | tf_op jit(solution)/shard_map/group_sum/pallas_call | solution.py:415
  598.4 5.4 multiply_convert_fusion.1
  603.8 5.0 fusion.2
  608.8 6.6 all-to-all-start.1
  615.7 8.4 fusion.51
  627.9 68.6 %tokens_back.1 = f32[128,2048]{1,0:T(8,128)} custom-call(bf16[2048,384]{1,0:T(8,128)(2,1)} %pad_maximum_fusion.1.d_ref, bf16[2048,384]{1,0:T(8,128)(2,1)} %get-tuple-element.33.wq_ref), custom_call_target="tpu_custom_call" | custom-call | tf_op jit(solution)/shard_map/tokens_back/pallas_call | solution.py:415
  696.5 2.5 fusion.50
  699.9 4.9 psum.7
  707.4 2.7 fusion.5
  713.1 4.5 all-to-all-start
  719.6 18.3 %collective-permute-done.7 = bf16[256,2048]{1,0:T(8,128)(2,1)} collective-permute-done((bf16[256,2048]{1,0:T(8,128)(2,1)S(1)}, bf16[256,2048]{1,0:T(8,128)(2,1)}, u32[]{:S(2)}, u32[]{:S(2)}) %collective-permute-start.7) | collective-permute-done | bytes 1048608 | tf_op jit(solution)/shard_map/ppermute | solution.py:792
  740.9 2.7 bitcast_convert_fusion
  743.6 53.8 %collective-permute-done.1 = bf16[16,64,384]{2,1,0:T(8,128)(2,1)S(1)} collective-permute-done((bf16[16,64,384]{2,1,0:T(8,128)(2,1)}, bf16[16,64,384]{2,1,0:T(8,128)(2,1)S(1)}, u32[]{:S(2)}, u32[]{:S(2)}) %collective-permute-start.1) | collective-permute-done | bytes 786464 | tf_op jit(solution)/shard_map/ppermute | solution.py:792
  804.3 4.5 broadcast_select_fusion.1
  808.8 3.3 stack.85
  812.1 3.5 copy.50
  815.7 3.3 stack.86
  821.2 3.8 convert_bitcast_fusion
  825.0 9.4 %reshape.410 = f32[128,16384]{1,0:T(8,128)} reshape(f32[2,64,2,16,512]{4,3,2,1,0:T(8,128)} %convert_bitcast_fusion) | data formatting | bytes 16777216 | tf_op jit(solution)/shard_map/convert_element_type | solution.py:812
  (139 shorter events, 58.6 us)
Async XLA Ops:
  7.2 691.8 %reduce-scatter.4.cloned.1.call-start = ((), (), s32[]{:S(2)}) async-start(), calls=%async_computation.3 | async-start | bytes 1114112
  116.0 8.5 %copy-start.15 = (bf16[2048,128]{1,0:T(8,128)(2,1)}, bf16[2048,128]{1,0:T(8,128)(2,1)S(1)}, u32[]{:S(2)}) copy-start(bf16[2048,128]{1,0:T(8,128)(2,1)S(1)} %slice.159) | copy-start | bytes 1572868
  123.8 3.0 copy-start.21
  126.8 102.8 %copy-start.10 = (bf16[128,2048]{1,0:T(8,128)(2,1)S(1)}, bf16[128,2048]{1,0:T(8,128)(2,1)}, u32[]{:S(2)}) copy-start(bf16[128,2048]{1,0:T(8,128)(2,1)} %x_ref.1) | copy-start | bytes 1572868
  231.9 125.6 %copy-start.5 = (bf16[128,2048]{1,0:T(8,128)(2,1)S(1)}, bf16[128,2048]{1,0:T(8,128)(2,1)}, u32[]{:S(2)}) copy-start(bf16[128,2048]{1,0:T(8,128)(2,1)} %param.13) | copy-start | bytes 1572868
  356.0 3.1 copy-start.3
  360.3 116.5 %copy-start = (f32[128,2048]{1,0:T(8,128)S(1)}, f32[128,2048]{1,0:T(8,128)}, u32[]{:S(2)}) copy-start(f32[128,2048]{1,0:T(8,128)} %get-tuple-element.27) | copy-start | bytes 3145732
  493.3 216.9 %collective-permute-start.6 = (bf16[256,2048]{1,0:T(8,128)(2,1)}, bf16[256,2048]{1,0:T(8,128)(2,1)}, u32[]{:S(2)}, u32[]{:S(2)}) collective-permute-start(bf16[256,2048]{1,0:T(8,128)(2,1)} %fusion.39), channel_id=1, source_target_pairs={{0,16},{16,0},{1,17},{17,1},{2,18},{18,2},{3,19},{19,3},{4,20},{20... | collective-permute-start | bytes 3145736 | tf_op jit(solution)/shard_map/ppermute | solution.py:785
  507.9 5.2 copy-start.14
  507.9 3.1 copy-start.6
  507.9 3.6 copy-start.11
  509.6 94.2 %collective-permute-start.4 = (bf16[16,64,1024]{2,1,0:T(8,128)(2,1)}, bf16[16,64,1024]{2,1,0:T(8,128)(2,1)}, u32[]{:S(2)}, u32[]{:S(2)}) collective-permute-start(bf16[16,64,1024]{2,1,0:T(8,128)(2,1)} %fusion.3), channel_id=1, source_target_pairs={{0,16},{16,0},{1,17},{17,1},{2,18},{18,2},{3,19},{19,3},{4,20},{20... | collective-permute-start | bytes 6291464 | tf_op jit(solution)/shard_map/ppermute | solution.py:785
  570.8 5.5 copy-start.12
  570.8 5.5 copy-start.17
  570.8 5.8 copy-start.2
  570.9 5.8 copy-start.16
  575.7 129.7 %collective-permute-start.2 = (bf16[64,2048]{1,0:T(8,128)(2,1)S(1)}, bf16[64,2048]{1,0:T(8,128)(2,1)}, u32[]{:S(2)}, u32[]{:S(2)}) collective-permute-start(bf16[64,2048]{1,0:T(8,128)(2,1)S(1)} %fusion.47), channel_id=1, source_target_pairs={{0,16},{16,0},{1,17},{17,1},{2,18},{18,2},{3,19},{19,3},{4,20},{20... | collective-permute-start | bytes 786440 | tf_op jit(solution)/shard_map/ppermute | solution.py:785
  583.9 3.9 copy-start.8
  608.8 6.6 copy-start.13
  608.8 104.3 %all-to-all-start.1 = ((bf16[16,64,1024]{2,1,0:T(8,128)(2,1)}), bf16[16,64,1024]{2,1,0:T(8,128)(2,1)}, u32[]{:S(2)}, u32[]{:S(2)}) async-start(bf16[16,64,1024]{2,1,0:T(8,128)(2,1)} %fusion.2), calls=%async_computation.1 | async-start | bytes 4194304 | tf_op jit(solution)/shard_map/all_to_all | solution.py:809
  615.7 10.9 %copy-start.25 = (bf16[2048,128]{1,0:T(8,128)(2,1)S(1)}, bf16[2048,128]{1,0:T(8,128)(2,1)}, u32[]{:S(2)}) copy-start(bf16[2048,128]{1,0:T(8,128)(2,1)} %get-tuple-element.52) | copy-start | bytes 1572868
  615.7 10.9 %copy-start.26 = (bf16[2048,128]{1,0:T(8,128)(2,1)S(1)}, bf16[2048,128]{1,0:T(8,128)(2,1)}, u32[]{:S(2)}) copy-start(bf16[2048,128]{1,0:T(8,128)(2,1)} %get-tuple-element.53) | copy-start | bytes 1572868
  624.1 3.8 copy-start.27
  625.2 71.3 %copy-start.7 = (f32[128,2048]{1,0:T(8,128)S(1)}, f32[128,2048]{1,0:T(8,128)}, u32[]{:S(2)}) copy-start(f32[128,2048]{1,0:T(8,128)} %get-tuple-element.31) | copy-start | bytes 3145732
  625.2 82.2 %collective-permute-start = (bf16[16,64,384]{2,1,0:T(8,128)(2,1)}, bf16[16,64,384]{2,1,0:T(8,128)(2,1)}, u32[]{:S(2)}, u32[]{:S(2)}) collective-permute-start(bf16[16,64,384]{2,1,0:T(8,128)(2,1)} %fusion.44), channel_id=1, source_target_pairs={{0,16},{16,0},{1,17},{17,1},{2,18},{18,2},{3,19},{19,3},{4,20},{20... | collective-permute-start | bytes 2359304 | tf_op jit(solution)/shard_map/ppermute | solution.py:785
  696.5 8.9 %copy-start.19 = (f32[2,64,2048]{2,1,0:T(8,128)S(1)}, f32[2,64,2048]{2,1,0:T(8,128)}, u32[]{:S(2)}) copy-start(f32[2,64,2048]{2,1,0:T(8,128)} %copy-done.18) | copy-start | bytes 3145732
  704.8 5.3 copy-start.20
  706.7 10.9 %collective-permute-start.3 = (bf16[64,2048]{1,0:T(8,128)(2,1)S(1)}, bf16[64,2048]{1,0:T(8,128)(2,1)S(1)}, u32[]{:S(2)}, u32[]{:S(2)}) collective-permute-start(bf16[64,2048]{1,0:T(8,128)(2,1)S(1)} %fusion.46), channel_id=1, source_target_pairs={{0,16},{16,0},{1,17},{17,1},{2,18},{18,2},{3,19},{19,3},{4,20},{20... | collective-permute-start | bytes 786440 | tf_op jit(solution)/shard_map/ppermute | solution.py:792
  711.7 26.2 %collective-permute-start.7 = (bf16[256,2048]{1,0:T(8,128)(2,1)S(1)}, bf16[256,2048]{1,0:T(8,128)(2,1)}, u32[]{:S(2)}, u32[]{:S(2)}) collective-permute-start(bf16[256,2048]{1,0:T(8,128)(2,1)S(1)} %fusion.4), channel_id=1, source_target_pairs={{0,16},{16,0},{1,17},{17,1},{2,18},{18,2},{3,19},{19,3},{4,20},{20... | collective-permute-start | bytes 3145736 | tf_op jit(solution)/shard_map/ppermute | solution.py:792
  713.1 26.2 %all-to-all-start = ((bf16[16,64,384]{2,1,0:T(8,128)(2,1)}), bf16[16,64,384]{2,1,0:T(8,128)(2,1)}, u32[]{:S(2)}, u32[]{:S(2)}) async-start(bf16[16,64,384]{2,1,0:T(8,128)(2,1)} %fusion.5), calls=%async_computation | async-start | bytes 1572864 | tf_op jit(solution)/shard_map/all_to_all | solution.py:809
  717.7 86.6 %collective-permute-start.5 = (bf16[16,64,1024]{2,1,0:T(8,128)(2,1)}, bf16[16,64,1024]{2,1,0:T(8,128)(2,1)}, u32[]{:S(2)}, u32[]{:S(2)}) collective-permute-start(bf16[16,64,1024]{2,1,0:T(8,128)(2,1)} %all-to-all-done.1), channel_id=1, source_target_pairs={{0,16},{16,0},{1,17},{17,1},{2,18},{18,2},{3,19},{19,3},{4,20},{20... | collective-permute-start | bytes 6291464 | tf_op jit(solution)/shard_map/ppermute | solution.py:792
  739.3 58.1 %collective-permute-start.1 = (bf16[16,64,384]{2,1,0:T(8,128)(2,1)}, bf16[16,64,384]{2,1,0:T(8,128)(2,1)S(1)}, u32[]{:S(2)}, u32[]{:S(2)}) collective-permute-start(bf16[16,64,384]{2,1,0:T(8,128)(2,1)} %all-to-all-done), channel_id=1, source_target_pairs={{0,16},{16,0},{1,17},{17,1},{2,18},{18,2},{3,19},{19,3},{4,20},{20... | collective-permute-start | bytes 2359304 | tf_op jit(solution)/shard_map/ppermute | solution.py:792
  (7 other events, 13.2 us)
Sparse Core Ops, SparseCore 0:
  480.1 59.4 reduce-scatter.3

commit v3 on v2

--- a/solution.py
+++ b/solution.py
@@ -183,7 +183,7 @@
     ]
 
 
-def scatter_loop(pos, count, bufs, sems, partial, out, hook=None):
+def scatter_loop(pos, count, bufs, sems, partial, out, hook=None, final=None):
     p, cgot, ygot, zgot = bufs
     csend, crecv, ysend, yrecv, zsend, zrecv = sems
     a, b, c, na = pos
@@ -267,6 +267,8 @@
         return 0
 
     lax.fori_loop(0, na - 1, second, 0)
+    if final is not None:
+        final()
     near = a * 2 + b
     to_core(near).wait_recv()
     to_pair(a).wait_recv()
@@ -345,9 +347,12 @@
 
     def local_in(self, g):
         cols = pl.ds(pl.multiple_of(g * self.total + self.s * self.width, 128), self.width)
-        return pltpu.make_async_copy(
-            self.w.at[:, cols], self.stage.at[:, pl.ds(g * self.width, self.width)], self.lsem.at[g]
-        )
+        into = pl.ds(g * self.width, self.width)
+        if self.stage is None:
+            dst = self.out.at[rows_of(self.s, self.own), into]
+        else:
+            dst = self.stage.at[:, into]
+        return pltpu.make_async_copy(self.w.at[:, cols], dst, self.lsem.at[g])
 
     def local_out(self):
         return pltpu.make_async_copy(
@@ -365,9 +370,10 @@
             return 0
 
         lax.fori_loop(1, self.n_shard, one, 0)
-        for g in range(self.groups):
-            self.local_in(g).wait()
-        self.local_out().start()
+        if self.stage is not None:
+            for g in range(self.groups):
+                self.local_in(g).wait()
+            self.local_out().start()
 
     def forward(self, low, high):
         def one(k, _):
@@ -391,12 +397,203 @@
             return 0
 
         lax.fori_loop(1, self.n_shard, one, 0)
-        self.local_out().wait()
+        if self.stage is not None:
+            self.local_out().wait()
+        else:
+            for g in range(self.groups):
+                self.local_in(g).wait()
 
     def spread(self, t, steps):
         each = -(-(self.n_shard - 1) // steps)
         low = 1 + t * each
         self.forward(low, jnp.minimum(low + each, self.n_shard))
+
+
+class ShareSum:
+    def __init__(self, acc, got, sems, blocks, n_rep):
+        self.acc, self.got, self.blocks, self.n_rep = acc, got, blocks, n_rep
+        self.ssem, self.rsem = sems
+        self.share = acc.shape[0] // (blocks * n_rep)
+        self.r = lax.axis_index("rep")
+
+    def part(self, block, replica):
+        return rows_of(block * self.n_rep + replica, self.share)
+
+    def desc(self, block, m):
+        target = lax.rem(self.r + m, self.n_rep)
+        slot = (m - 1) * self.blocks + block
+        return send(
+            self.acc.at[self.part(block, target)], self.got.at[rows_of(slot, self.share)],
+            self.ssem.at[slot], self.rsem.at[slot], rep=target,
+        )
+
+    def start(self, block):
+        for m in range(1, self.n_rep):
+            self.desc(block, m).start()
+
+    def add(self, block):
+        for m in range(1, self.n_rep):
+            self.desc(block, m).wait_recv()
+        tile = min(self.share, 32)
+
+        def one(k, _):
+            at = pl.ds(
+                pl.multiple_of((block * self.n_rep + self.r) * self.share + k * tile, tile), tile
+            )
+            total = self.acc[at, :].astype(F32)
+            for m in range(1, self.n_rep):
+                slot = (m - 1) * self.blocks + block
+                total = total + self.got[
+                    pl.ds(pl.multiple_of(slot * self.share + k * tile, tile), tile), :
+                ].astype(F32)
+            self.acc[at, :] = total.astype(BF)
+            return 0
+
+        lax.fori_loop(0, self.share // tile, one, 0)
+
+    def sent(self, block):
+        for m in range(1, self.n_rep):
+            self.desc(block, m).wait_send()
+
+
+def share_scratch(rows, cols, blocks, n_rep):
+    return [
+        pltpu.VMEM((rows, cols), BF), pltpu.VMEM(((n_rep - 1) * rows // n_rep, cols), BF),
+        DMA(((n_rep - 1) * blocks,)), DMA(((n_rep - 1) * blocks,)),
+    ]
+
+
+class ShareGather:
+    def __init__(self, src, out, sems, n_rep):
+        self.src, self.out, self.n_rep = src, out, n_rep
+        self.ssem, self.rsem, self.lsem = sems
+        self.r = lax.axis_index("rep")
+        self.share = out.shape[0] // n_rep
+
+    def local(self):
+        return pltpu.make_async_copy(self.src, self.out.at[rows_of(self.r, self.share)], self.lsem)
+
+    def desc(self, m, replica):
+        return send(
+            self.src, self.out.at[rows_of(replica, self.share)],
+            self.ssem.at[m - 1], self.rsem.at[replica], rep=lax.rem(self.r + m, self.n_rep),
+        )
+
+    def start(self):
+        self.local().start()
+        for m in range(1, self.n_rep):
+            self.desc(m, self.r).start()
+
+    def finish(self):
+        self.local().wait()
+        for m in range(1, self.n_rep):
+            self.desc(m, self.r).wait_send()
+            self.desc(m, lax.rem(self.r + m, self.n_rep)).wait_recv()
+
+
+def share_gather_sems(n_rep):
+    return [DMA((n_rep - 1,)), DMA((n_rep,)), DMA(())]
+
+
+class RowsBack:
+    def __init__(self, src, out, sems, groups, n_shard, n_rep):
+        self.src, self.out, self.groups = src, out, groups
+        self.ssem, self.rsem, self.fsend, self.frecv, self.lsem = sems
+        self.n_shard, self.n_rep = n_shard, n_rep
+        self.share = out.shape[0] // n_rep
+        self.total = out.shape[1] // groups
+        self.width = self.total // n_shard
+        self.s, self.r = lax.axis_index("shard"), lax.axis_index("rep")
+
+    def place(self, source, replica, g):
+        cols = pl.ds(pl.multiple_of(g * self.total + source * self.width, 128), self.width)
+        return self.out.at[rows_of(replica, self.share), cols]
+
+    def piece(self, target, g):
+        return self.src(target).at[:, pl.ds(g * self.width, self.width)]
+
+    def move(self, source, target, g):
+        return send(
+            self.piece(target, g), self.place(source, self.r, g),
+            self.ssem.at[target * self.groups + g], self.rsem.at[source * self.groups + g],
+            shard=target,
+        )
+
+    def local(self, g):
+        return pltpu.make_async_copy(
+            self.piece(self.s, g), self.place(self.s, self.r, g), self.lsem.at[g]
+        )
+
+    def pass_on(self, source, m, replica, g):
+        at = self.place(source, replica, g)
+        return send(
+            at, at, self.fsend.at[(source * self.n_rep + m) * self.groups + g],
+            self.frecv.at[(source * self.n_rep + replica) * self.groups + g],
+            rep=lax.rem(self.r + m, self.n_rep),
+        )
+
+    def start(self):
+        for g in range(self.groups):
+            self.local(g).start()
+
+        def one(k, _):
+            for g in range(self.groups):
+                self.move(self.s, lax.rem(self.s + k, self.n_shard), g).start()
+            return 0
+
+        lax.fori_loop(1, self.n_shard, one, 0)
+
+    def relay(self, source):
+        for g in range(self.groups):
+            for m in range(1, self.n_rep):
+                self.pass_on(source, m, self.r, g).start()
+
+    def forward_own(self):
+        for g in range(self.groups):
+            self.local(g).wait()
+        self.relay(self.s)
+
+    def forward(self, low, high):
+        def one(k, _):
+            source = lax.rem(self.s + self.n_shard - k, self.n_shard)
+            for g in range(self.groups):
+                self.move(source, self.s, g).wait_recv()
+            self.relay(source)
+            return 0
+
+        lax.fori_loop(low, high, one, 0)
+
+    def spread(self, t, steps):
+        @pl.when(t == 0)
+        def _():
+            self.forward_own()
+
+        each = -(-(self.n_shard - 1) // steps)
+        low = 1 + t * each
+        self.forward(low, jnp.minimum(low + each, self.n_shard))
+
+    def finish(self):
+        def one(k, _):
+            source = lax.rem(self.s + self.n_shard - k, self.n_shard)
+            for g in range(self.groups):
+
+                @pl.when(k > 0)
+                def _():
+                    self.move(self.s, source, g).wait_send()
+
+                for m in range(1, self.n_rep):
+                    self.pass_on(source, m, self.r, g).wait_send()
+                    self.pass_on(source, m, lax.rem(self.r + m, self.n_rep), g).wait_recv()
+            return 0
+
+        lax.fori_loop(0, self.n_shard, one, 0)
+
+
+def rows_back_sems(n_shard, n_rep, groups):
+    return [
+        DMA((n_shard * groups,)), DMA((n_shard * groups,)),
+        DMA((n_shard * n_rep * groups,)), DMA((n_shard * n_rep * groups,)), DMA((groups,)),
+    ]
 
 
 def mm(left, right):
@@ -461,128 +658,178 @@
     lax.fori_loop(0, chips, one, 0)
 
 
-def qkv_kernel(
-    n_shard, n_rep, x_ref, w_ref, g_ref, qkv_ref, cols_ref, sums_ref,
-    buf, wq, stage, qkv, stats, got, lsem, osem, vsem, xs, xr, *sems,
+def turned(row, count):
+    return jnp.transpose(jnp.broadcast_to(row, (count, count)))
+
+
+def swap_halves(x):
+    return pltpu.roll(x, x.shape[1] // 2, 1)
+
+
+def rope_of(spots, table):
+    count = spots.shape[0]
+    lane = lax.broadcasted_iota(jnp.int32, (count, count), 1)
+    pick = jnp.where(lane.astype(F32) == spots, 1.0, 0.0).astype(F32)
+    both = jnp.dot(pick, table, preferred_element_type=F32, precision=lax.Precision.HIGHEST)
+    half = both.shape[1] // 2
+    return both[:, :half], both[:, half:]
+
+
+def row_sums(x):
+    ones = jnp.ones((8, x.shape[1]), F32)
+    return lax.dot_general(
+        ones, x, (((1,), (1,)), ((), ())),
+        preferred_element_type=F32, precision=lax.Precision.HIGHEST,
+    )[:1]
+
+
+def attn_kernel(
+    n_shard, n_rep, heads,
+    x_ref, aux_ref, wqkv_ref, wo_ref, wgu_ref, table_ref, qg_ref, kg_ref,
+    g_ref, wq_ref, wg_ref, auxg_ref, sums_ref, hats_ref, rot_ref, prob_ref, ctx_ref, out_ref,
+    buf, wq, stage, qkv, stats, got, lsem, osem, xs, xr, as_, ar, *rest,
 ):
     pos = position(n_shard)
-    count = x_ref.shape[0]
+    gsems, c3, c2, bufs, ssems = rest[:5], rest[5:10], rest[10:15], rest[15:19], rest[19:]
+    p = bufs[0]
+    count, width = out_ref.shape
     chips = n_shard // 2
     big = 2 * count
-    own = stage.shape[1] // 3
+    own = wo_ref.shape[0]
+    hw = own // heads
     na = pos[3]
     s = lax.axis_index("shard")
     mine = load(x_ref, buf.at[own_rows(pos, count)], lsem.at[0])
-    weights = Columns(w_ref, cols_ref, stage, sems[5:], 3, n_shard, n_rep)
+    qkv_w = Columns(wqkv_ref, wq, None, c3, 3, n_shard, n_rep)
+    gu_w = Columns(wgu_ref, wg_ref, stage, c2, 2, n_shard, n_rep)
+    auxg_ref[s] = aux_ref[...]
     greet_all(n_shard, n_rep)
     mine.wait()
     out_x = Out(buf, g_ref, osem, big)
 
+    def aux_desc(k):
+        target = lax.rem(s + k, n_shard)
+        return send(aux_ref, auxg_ref.at[s], as_.at[k - 1], ar.at[k - 1], shard=target)
+
     def hook(t):
         @pl.when(t == 0)
         def _():
-            weights.start()
+            qkv_w.start()
+
+            def one(k, _):
+                aux_desc(k).start()
+                return 0
+
+            lax.fori_loop(1, n_shard, one, 0)
 
         @pl.when(t > 0)
         def _():
-            weights.spread(t - 1, na - 1)
-
-    gather_loop(pos, count, buf, sems[:5], out_x.start, hook)
-    weights.finish()
-    pltpu.sync_copy(cols_ref, wq)
-    out_v = Out(qkv, qkv_ref, vsem, big)
-    ones = jnp.ones((8, own), F32)
-
-    def one(q, _):
+            qkv_w.spread(t - 1, na - 1)
+
+    gather_loop(pos, count, buf, gsems, out_x.start, hook)
+    qkv_w.finish()
+    gu_w.start()
+    keep = load(wq, wq_ref, lsem.at[1])
+
+    def project(q, _):
         r = rows_of(q, big)
         v = mm(buf[r, :], wq[...])
         qkv[r, :] = v
         for g in range(2):
             x = v[:, g * own : (g + 1) * own]
-            total = lax.dot_general(
-                ones, x * x, (((1,), (1,)), ((), ())),
-                preferred_element_type=F32, precision=lax.Precision.HIGHEST,
-            )
-            stats[pl.ds(g, 1), pl.ds(pl.multiple_of(q * big, big), big)] = total[:1]
-        out_v.start(q)
-        return 0
-
-    lax.fori_loop(0, chips, one, 0)
-    exchange(n_shard, stats, got, xs, xr, sums_ref)
-    wait_all([out_x, out_v], chips)
-
-
-def exchange(n_shard, stats, got, xs, xr, sums_ref):
-    s = lax.axis_index("shard")
-
-    def desc(k):
-        target = lax.rem(s + k, n_shard)
-        return send(stats, got.at[k - 1], xs.at[k - 1], xr.at[k - 1], shard=target)
-
-    def start(k, _):
-        desc(k).start()
-        return 0
-
-    lax.fori_loop(1, n_shard, start, 0)
-    sums_ref[...] = stats[...]
-
-    def take(k, _):
-        desc(k).wait_recv()
-        sums_ref[...] += got[k - 1]
-        return 0
-
-    lax.fori_loop(1, n_shard, take, 0)
-
-    def done(k, _):
-        desc(k).wait_send()
-        return 0
-
-    lax.fori_loop(1, n_shard, done, 0)
-
-
-def sum_kernel(n_shard, x_ref, sums_ref, stats, got, xs, xr):
-    barrier = pltpu.get_barrier_semaphore()
-    s = lax.axis_index("shard")
-
-    def one(k, _):
-        signal(barrier, shard=lax.rem(s + k, n_shard))
-        return 0
-
-    lax.fori_loop(1, n_shard, one, 0)
-    stats[...] = x_ref[...]
-    pl.semaphore_wait(barrier, n_shard - 1)
-    exchange(n_shard, stats, got, xs, xr, sums_ref)
-
-
-def attn_out_kernel(
-    n_shard, n_rep, ctx_ref, wo_ref, w_ref, out_ref, cols_ref, stage, *rest,
-):
-    pos = position(n_shard)
-    na = pos[3]
-    bufs, sems, csems = rest[:4], rest[4:10], rest[10:]
-    p = bufs[0]
-    count = out_ref.shape[0]
-    big = 2 * count
-    width = out_ref.shape[1]
-    weights = Columns(w_ref, cols_ref, stage, csems, 2, n_shard, n_rep)
-    greet_all(n_shard, n_rep)
+            stats[pl.ds(g, 1), pl.ds(pl.multiple_of(q * big, big), big)] = row_sums(x * x)
+        return 0
+
+    lax.fori_loop(0, chips, project, 0)
+    exchange_start(n_shard, stats, got, xs, xr)
+    exchange_finish(n_shard, stats, got, xs, xr, sums_ref)
+
+    def aux_done(k, _):
+        aux_desc(k).wait_recv()
+        aux_desc(k).wait_send()
+        return 0
+
+    lax.fori_loop(1, n_shard, aux_done, 0)
+    root = hw ** (-0.5)
+    lane = lax.broadcasted_iota(jnp.int32, (count, count), 1)
+    slot = lax.broadcasted_iota(jnp.int32, (count, count), 0)
+
+    def attend(i, _):
+        r = rows_of(i, count)
+        at = pl.ds(pl.multiple_of(i * count, count), count)
+        spots = turned(auxg_ref[i, 1:2, :], count)
+        cos, sin = rope_of(spots, table_ref[...])
+        ok = (lane <= slot) & (lane >= slot - spots.astype(jnp.int32))
+        scale = lax.rsqrt(sums_ref[:, at] / width + EPSILON)
+        q_scale = turned(scale[0:1], count)[:, :1]
+        k_scale = turned(scale[1:2], count)[:, :1]
+        for h in range(heads):
+            def part(g):
+                lo = g * own + h * hw
+                return slice(lo, lo + hw)
+
+            cols = slice(h * hw, (h + 1) * hw)
+
+            def turn(g, scale, gain):
+                hat = qkv[r, part(g)] * scale
+                hats_ref[r, part(g)] = hat
+                x = hat * gain
+                x = (x * cos + swap_halves(x) * sin).astype(BF)
+                rot_ref[r, part(g)] = x
+                return x
+
+            query = turn(0, q_scale, qg_ref[:, cols])
+            keys = turn(1, k_scale, kg_ref[:, cols])
+            values = qkv[r, part(2)].astype(BF)
+            rot_ref[r, part(2)] = values
+            scores = jnp.where(ok, mm_nt(query, keys) * root, -1e30)
+            e = jnp.exp(scores - jnp.max(scores, axis=-1, keepdims=True))
+            probs = e / jnp.sum(e, axis=-1, keepdims=True)
+            prob_ref[r, h * count : (h + 1) * count] = probs
+            ctx_ref[r, cols] = mm(probs.astype(BF), values).astype(BF)
+        return 0
+
+    lax.fori_loop(0, n_shard, attend, 0)
 
     def partial(q):
         r = rows_of(q, big)
         p[r, :] = mm(ctx_ref[r, :], wo_ref[...]).astype(BF)
 
-    def hook(t):
-        @pl.when(t == 0)
-        def _():
-            weights.start()
-
-        @pl.when(t > 0)
-        def _():
-            weights.spread(t - 1, na - 1)
-
-    scatter_loop(pos, count, bufs, sems, partial, out_ref, hook)
-    weights.spread(na - 2, na - 1)
-    weights.finish()
+    scatter_loop(pos, count, bufs, ssems, partial, out_ref, lambda t: gu_w.spread(t, na))
+    gu_w.spread(na - 1, na)
+    gu_w.finish()
+    keep.wait()
+    wait_all([out_x], chips)
+
+
+def exchange_desc(n_shard, stats, got, xs, xr, k):
+    target = lax.rem(lax.axis_index("shard") + k, n_shard)
+    return send(stats, got.at[k - 1], xs.at[k - 1], xr.at[k - 1], shard=target)
+
+
+def exchange_start(n_shard, stats, got, xs, xr):
+    def start(k, _):
+        exchange_desc(n_shard, stats, got, xs, xr, k).start()
+        return 0
+
+    lax.fori_loop(1, n_shard, start, 0)
+
+
+def exchange_finish(n_shard, stats, got, xs, xr, sums):
+    sums[...] = stats[...]
+
+    def take(k, _):
+        exchange_desc(n_shard, stats, got, xs, xr, k).wait_recv()
+        sums[...] += got[k - 1]
+        return 0
+
+    lax.fori_loop(1, n_shard, take, 0)
+
+    def done(k, _):
+        exchange_desc(n_shard, stats, got, xs, xr, k).wait_send()
+        return 0
+
+    lax.fori_loop(1, n_shard, done, 0)
 
 
 def mlp_kernel(
@@ -614,8 +861,8 @@
             hi = pl.ds(pl.multiple_of(ff + k * 256, 256), 256)
             gate = mm(buf[r, :], wg[:, lo])
             up = mm(buf[r, :], wg[:, hi])
-            gu[r, lo] = gate
-            gu[r, hi] = up
+            gu[r, lo] = gate.astype(BF)
+            gu[r, hi] = up.astype(BF)
             mixed[r, lo] = (gate * jax.nn.sigmoid(gate) * up).astype(BF)
             return 0
 
@@ -640,17 +887,32 @@
     wait_all([out_x, out_g, out_m], chips)
 
 
+def flip(src, cols, flipped):
+    step = 256
+
+    def one(k, _):
+        at = rows_of(k, step)
+        flipped[:, at] = jnp.transpose(src[at, cols])
+        return 0
+
+    lax.fori_loop(0, src.shape[0] // step, one, 0)
+
+
 def mlp_back_kernel(
-    n_shard, x_ref, gu_ref, wg_ref, wd_ref, g_ref, dgu_ref, out_ref,
-    buf, wg, wd, gu, dgu, lsem, isem, osem, dsem, *rest,
+    n_shard, n_rep, x_ref, gu_ref, wg_ref, wd_ref, resid_ref, mixed_ref,
+    gsum_ref, down_ref, out_ref,
+    buf, wg, wd, gu, dgu, resid, mixed, flipped, down, lsem, isem, osem, acc, got, xs, xr, *rest,
 ):
     pos = position(n_shard)
+    na = pos[3]
     bufs, ssems, gsems = rest[:4], rest[4:10], rest[10:]
     p = bufs[0]
     count, width = out_ref.shape
     big = 2 * count
     chips = n_shard // 2
     ff = wd.shape[0]
+    own = width // n_shard
+    share = own // n_rep
     mine = load(x_ref, buf.at[own_rows(pos, count)], lsem.at[0])
     w2 = load(wd_ref, wd, lsem.at[2])
     saved = Out(gu_ref, gu, isem, big)
@@ -661,21 +923,21 @@
 
     lax.fori_loop(0, chips, fetch, 0)
     w1 = load(wg_ref, wg, lsem.at[1])
-    greet(pos)
+    in_r = load(resid_ref, resid, lsem.at[3])
+    in_m = load(mixed_ref, mixed, lsem.at[4])
+    greet_all(n_shard, n_rep)
     mine.wait()
-    out_x, out_d = Out(buf, g_ref, osem, big), Out(dgu, dgu_ref, dsem, big)
     w2.wait()
 
     def on_chip(q):
         r = rows_of(q, big)
-        out_x.start(q)
         saved.wait(q)
 
         def one(k, _):
             lo = pl.ds(pl.multiple_of(k * 256, 256), 256)
             hi = pl.ds(pl.multiple_of(ff + k * 256, 256), 256)
             d_mixed = mm_nt(buf[r, :], wd[lo, :])
-            gate, up = gu[r, lo], gu[r, hi]
+            gate, up = gu[r, lo].astype(F32), gu[r, hi].astype(F32)
             sigma = jax.nn.sigmoid(gate)
             d_gate = d_mixed * up * sigma * (1.0 + gate * (1.0 - sigma))
             dgu[r, lo] = d_gate.astype(BF)
@@ -683,10 +945,11 @@
             return 0
 
         lax.fori_loop(0, ff // 256, one, 0)
-        out_d.start(q)
 
     gather_loop(pos, count, buf, gsems, on_chip)
     w1.wait()
+    in_r.wait()
+    in_m.wait()
 
     def partial(q):
         r = rows_of(q, big)
@@ -698,47 +961,251 @@
 
         lax.fori_loop(0, width // 256, one, 0)
 
-    scatter_loop(pos, count, bufs, ssems, partial, out_ref)
-    wait_all([out_x, out_d], chips)
-
-
-def context_back_kernel(n_shard, x_ref, wo_ref, g_ref, ctx_ref, buf, lsem, osem, *gsems):
+    shares = ShareSum(acc, got, (xs, xr), n_shard, n_rep)
+    most = flipped.shape[0]
+    owners = most // own
+    parts = width // most
+
+    def grad_rows(k):
+        flip(resid, pl.ds(pl.multiple_of(k * most, most), most), flipped)
+
+        def one(n, _):
+            lo = rows_of(n, 256)
+            acc[rows_of(k, most), lo] = mm(flipped[...], dgu[:, lo]).astype(BF)
+            return 0
+
+        lax.fori_loop(0, 2 * ff // 256, one, 0)
+        for d in range(owners):
+            shares.start(k * owners + d)
+
+    def hook(t):
+        def one(k, _):
+            grad_rows(k)
+            return 0
+
+        lax.fori_loop(parts * t // (na - 1), parts * (t + 1) // (na - 1), one, 0)
+
+    def grad_down():
+        def rows(m, _):
+            flip(mixed, pl.ds(pl.multiple_of(m * most, most), most), flipped)
+
+            def one(n, _):
+                lo = rows_of(n, 256)
+                down[rows_of(m, most), lo] = mm(flipped[...], buf[:, lo]).astype(BF)
+                return 0
+
+            lax.fori_loop(0, width // 256, one, 0)
+            return 0
+
+        lax.fori_loop(0, ff // most, rows, 0)
+        load(down, down_ref, lsem.at[3])
+
+    scatter_loop(pos, count, bufs, ssems, partial, out_ref, hook, grad_down)
+
+    def collect(d, _):
+        shares.add(d)
+        pltpu.make_async_copy(
+            acc.at[shares.part(d, shares.r)], gsum_ref.at[rows_of(d, share)], osem.at[d]
+        ).start()
+        return 0
+
+    lax.fori_loop(0, n_shard, collect, 0)
+
+    def end(d, _):
+        shares.sent(d)
+        pltpu.make_async_copy(
+            acc.at[shares.part(d, shares.r)], gsum_ref.at[rows_of(d, share)], osem.at[d]
+        ).wait()
+        return 0
+
+    lax.fori_loop(0, n_shard, end, 0)
+    pltpu.make_async_copy(down, down_ref, lsem.at[3]).wait()
+
+
+def attn_back_kernel(
+    n_shard, n_rep, heads,
+    x_ref, tok_ref, wo_ref, wq_ref, hats_ref, rot_ref, prob_ref, ctx_ref, aux_ref, sums_ref,
+    table_ref, qg_ref, kg_ref, gsum_ref, down_ref,
+    gu_ref, dn_ref, go_ref, gq_ref, gains_ref, out_ref,
+    buf, tok, wq, dctx, ups, dqkv, flipped, stats, inner, got, lsem, xs, xr, *rest,
+):
+    rest = list(rest)
+
+    def take(n):
+        out = rest[:n]
+        del rest[:n]
+        return out
+
     pos = position(n_shard)
-    count = x_ref.shape[0]
-    big = 2 * count
-    mine = load(x_ref, buf.at[own_rows(pos, count)], lsem.at[0])
-    greet(pos)
-    mine.wait()
-    out_x = Out(buf, g_ref, osem, big)
-
-    def on_chip(q):
-        r = rows_of(q, big)
-        out_x.start(q)
-        ctx_ref[r, :] = mm_nt(buf[r, :], wo_ref[...]).astype(BF)
-
-    gather_loop(pos, count, buf, gsems, on_chip)
-    wait_all([out_x], n_shard // 2)
-
-
-def tokens_back_kernel(n_shard, d_ref, wq_ref, out_ref, *rest):
-    pos = position(n_shard)
-    bufs, sems = rest[:4], rest[4:]
+    na = pos[3]
+    gsems, bufs, ssems = take(5), take(4), take(6)
+    dacc, dgot, *dsems = take(4)
+    oacc, ogot, *osems = take(4)
+    qacc, qgot, *qsems = take(4)
+    dgsems, ogsems, gusems, qksems = take(3), take(3), take(5), take(5)
     p = bufs[0]
     count, width = out_ref.shape
     big = 2 * count
-    greet(pos)
+    own = wo_ref.shape[0]
+    hw = own // heads
+    r_me = lax.axis_index("rep")
+    mine = load(x_ref, buf.at[own_rows(pos, count)], lsem.at[0])
+    in_d = load(down_ref, dacc, lsem.at[1])
+    in_t = load(tok_ref, tok, lsem.at[2])
+    in_w = load(wq_ref, wq, lsem.at[3])
+    share = own // n_rep
+    gu_rows = RowsBack(lambda d: gsum_ref.at[rows_of(d, share)], gu_ref, gusems, 2, n_shard, n_rep)
+    down = ShareSum(dacc, dgot, dsems, 1, n_rep)
+    down_all = ShareGather(dacc.at[down.part(0, r_me)], dn_ref, dgsems, n_rep)
+    wout = ShareSum(oacc, ogot, osems, 1, n_rep)
+    wout_all = ShareGather(oacc.at[wout.part(0, r_me)], go_ref, ogsems, n_rep)
+    wqkv = ShareSum(qacc, qgot, qsems, n_shard, n_rep)
+    wqkv_rows = RowsBack(
+        lambda d: qacc.at[wqkv.part(d, r_me)], gq_ref, qksems, 3, n_shard, n_rep
+    )
+    greet_all(n_shard, n_rep)
+    mine.wait()
+
+    def hook(t):
+        @pl.when(t == 0)
+        def _():
+            gu_rows.start()
+            in_d.wait()
+            down.start(0)
+
+        @pl.when(t > 0)
+        def _():
+            gu_rows.spread(t - 1, na - 1)
+
+    def on_chip(q):
+        r = rows_of(q, big)
+        dctx[r, :] = mm_nt(buf[r, :], wo_ref[...]).astype(BF)
+
+    gather_loop(pos, count, buf, gsems, on_chip, hook)
+    down.add(0)
+    down_all.start()
+    root = hw ** (-0.5)
+    gains_ref[...] = jnp.zeros_like(gains_ref)
+
+    def scale_of(i):
+        at = pl.ds(pl.multiple_of(i * count, count), count)
+        return lax.rsqrt(sums_ref[:, at] / width + EPSILON)
+
+    def attend(i, _):
+        r = rows_of(i, count)
+        at = pl.ds(pl.multiple_of(i * count, count), count)
+        cos, sin = rope_of(turned(aux_ref[i, 1:2, :], count), table_ref[...])
+        totals = [jnp.zeros((1, count), F32), jnp.zeros((1, count), F32)]
+        for h in range(heads):
+            def part(g):
+                lo = g * own + h * hw
+                return slice(lo, lo + hw)
+
+            cols = slice(h * hw, (h + 1) * hw)
+            query, keys, values = rot_ref[r, part(0)], rot_ref[r, part(1)], rot_ref[r, part(2)]
+            probs = prob_ref[r, h * count : (h + 1) * count]
+            probs_b = probs.astype(BF)
+            d_ctx = dctx[r, cols]
+            d_values = mm_tn(probs_b, d_ctx)
+            d_probs = mm_nt(d_ctx, values)
+            delta = jnp.sum(probs_b.astype(F32) * d_probs, axis=-1, keepdims=True)
+            d_scores = (probs * (d_probs - delta) * root).astype(BF)
+            d_query = mm(d_scores, keys)
+            d_keys = mm_tn(d_scores, query)
+            dqkv[r, part(2)] = d_values.astype(BF)
+            for g, (x, gain) in enumerate(((d_query, qg_ref), (d_keys, kg_ref))):
+                x = x * cos - swap_halves(x) * sin
+                hat = hats_ref[r, part(g)]
+                gains_ref[g : g + 1, cols] += jnp.sum(x * hat, axis=0, keepdims=True)
+                up = x * gain[:, cols]
+                ups[r, part(g)] = up
+                totals[g] = totals[g] + row_sums(up * hat)
+        for g in range(2):
+            stats[pl.ds(g, 1), at] = totals[g]
+        return 0
+
+    lax.fori_loop(0, n_shard, attend, 0)
+    exchange_start(n_shard, stats, got, xs, xr)
+
+    fo = flipped.at[pl.ds(0, own)]
+    flip(ctx_ref, slice(0, own), fo)
+
+    def out_cols(n, _):
+        lo = rows_of(n, 256)
+        oacc[:, lo] = mm(fo[...], buf[:, lo]).astype(BF)
+        return 0
+
+    lax.fori_loop(0, width // 256, out_cols, 0)
+    wout.start(0)
+    exchange_finish(n_shard, stats, got, xs, xr, inner)
+
+    def settle(i, _):
+        r = rows_of(i, count)
+        at = pl.ds(pl.multiple_of(i * count, count), count)
+        scale = scale_of(i)
+        mean = inner[:, at] / width
+        for g in range(2):
+            lo = slice(g * own, (g + 1) * own)
+            column = turned(scale[g : g + 1], count)[:, :1]
+            down_by = turned(mean[g : g + 1], count)[:, :1]
+            dqkv[r, lo] = (column * (ups[r, lo] - hats_ref[r, lo] * down_by)).astype(BF)
+        return 0
+
+    lax.fori_loop(0, n_shard, settle, 0)
+    in_w.wait()
+    in_t.wait()
 
     def partial(q):
         r = rows_of(q, big)
 
         def one(k, _):
             lo = rows_of(k, 512)
-            p[r, lo] = mm_nt(d_ref[r, :], wq_ref[lo, :]).astype(BF)
+            p[r, lo] = mm_nt(dqkv[r, :], wq[lo, :]).astype(BF)
             return 0
 
         lax.fori_loop(0, width // 512, one, 0)
 
-    scatter_loop(pos, count, bufs, sems, partial, out_ref)
+    most = flipped.shape[0]
+    owners = most // own
+
+    def grad_rows(k, _):
+        flip(tok, pl.ds(pl.multiple_of(k * most, most), most), flipped)
+        qacc[rows_of(k, most), :] = mm(flipped[...], dqkv[...]).astype(BF)
+        for d in range(owners):
+            wqkv.start(k * owners + d)
+        return 0
+
+    def sum_up(d, _):
+        wqkv.add(d)
+        return 0
+
+    def hook2(t):
+        @pl.when(t == 0)
+        def _():
+            lax.fori_loop(0, width // most, grad_rows, 0)
+
+        @pl.when(t == 1)
+        def _():
+            lax.fori_loop(0, n_shard, sum_up, 0)
+            wqkv_rows.start()
+            wout.add(0)
+            wout_all.start()
+
+    scatter_loop(
+        pos, count, bufs, ssems, partial, out_ref, hook2, lambda: wqkv_rows.spread(0, 1)
+    )
+
+    def end(d, _):
+        wqkv.sent(d)
+        return 0
+
+    lax.fori_loop(0, n_shard, end, 0)
+    down.sent(0)
+    wout.sent(0)
+    wqkv_rows.finish()
+    gu_rows.finish()
+    down_all.finish()
+    wout_all.finish()
 
 
 def positions(seg):
@@ -750,18 +1217,12 @@
     return slots - first
 
 
-def rope_tables(seg, head_width):
+def rope_table(count, head_width):
     half_width = head_width // 2
-    spots = positions(seg).astype(F32).reshape(-1)
     inverse = THETA ** (-(2.0 * jnp.arange(half_width, dtype=F32)) / head_width)
-    angle = spots[:, None] * inverse[None, :]
-    return jnp.cos(angle), jnp.sin(angle)
-
-
-def rotate(matrix, cosine, sine):
-    half = matrix.shape[-1] // 2
-    a, b = matrix[..., :half], matrix[..., half:]
-    return jnp.concatenate([a * cosine - b * sine, b * cosine + a * sine], axis=-1)
+    angle = jnp.arange(count, dtype=F32)[:, None] * inverse[None, :]
+    cosine, sine = jnp.cos(angle), jnp.sin(angle)
+    return jnp.concatenate([cosine, cosine, -sine, sine], axis=1)
 
 
 def norm_scale(vector):
@@ -776,51 +1237,6 @@
 
 def make(n_rep, n_shard):
     chips = n_shard // 2
-
-    def rep_scatter(x):
-        if n_rep == 2:
-            me = lax.axis_index("rep")
-            mine = lax.dynamic_index_in_dim(x, me, 0, keepdims=False)
-            other = lax.dynamic_index_in_dim(x, 1 - me, 0, keepdims=False)
-            got = lax.ppermute(other.astype(BF), "rep", [(0, 1), (1, 0)])
-            return (mine + got.astype(F32)).astype(BF)
-        return lax.psum_scatter(x.astype(BF), "rep", scatter_dimension=0, tiled=False)
-
-    def rep_gather(x):
-        if n_rep == 2:
-            me = lax.axis_index("rep")
-            got = lax.ppermute(x, "rep", [(0, 1), (1, 0)])
-            first = jnp.where(me == 0, x, got)
-            second = jnp.where(me == 0, got, x)
-            return jnp.stack([first, second])
-        return lax.all_gather(x, "rep", axis=0, tiled=False)
-
-    def rep_sum(x):
-        rows = x.shape[0]
-        part = rep_scatter(x.reshape(n_rep, rows // n_rep, x.shape[1]))
-        return rep_gather(part).reshape(x.shape).astype(F32)
-
-    def grad_back(x, groups):
-        rows, cols = x.shape
-        own = rows // n_shard
-        width = cols // groups
-        split = x.reshape(n_shard, n_rep, own // n_rep, cols).transpose(1, 0, 2, 3)
-        part = rep_scatter(split)
-        part = lax.all_to_all(part, "shard", split_axis=0, concat_axis=0, tiled=True)
-        whole = rep_gather(part)
-        whole = whole.reshape(n_rep, n_shard, own // n_rep, groups, width)
-        return whole.transpose(0, 2, 3, 1, 4).reshape(own, groups * n_shard * width).astype(F32)
-
-    def group_sum(x):
-        return call(
-            functools.partial(sum_kernel, n_shard), "group_sum", 11,
-            [(x.shape, F32, VM)], [VM],
-            [
-                pltpu.VMEM(x.shape, F32), pltpu.VMEM((n_shard - 1,) + x.shape, F32),
-                DMA((n_shard - 1,)), DMA((n_shard - 1,)),
-            ],
-            x,
-        )[0]
 
     def shards(
         tokens, segment_ids, cotangent, w_qkv, w_out, w_gate_up, w_down,
@@ -834,70 +1250,38 @@
         total = count * n_shard
         gathered = pltpu.VMEM((total, width), BF)
 
-        small = lax.all_gather(
-            jnp.stack([segment_ids.astype(BF), attn_gain, mlp_gain])[None], "shard", axis=0, tiled=True
-        )
-        seg = small[:, 0].astype(jnp.int32)
-        gain_attn = small[:, 1].reshape(-1).astype(F32)
-        gain_mlp = small[:, 2].reshape(-1).astype(F32)
         gain_query = q_gain.astype(F32)
         gain_keys = k_gain.astype(F32)
-        cosine, sine = rope_tables(seg, hw)
-        cos3 = cosine[:, None, :]
-        sin3 = sine[:, None, :]
-
-        tokens_g, qkv, wq, squares = call(
-            functools.partial(qkv_kernel, n_shard, n_rep), "qkv", 1,
+        spots = positions(segment_ids[None]).astype(F32)
+        aux = jnp.concatenate(
             [
-                ((total, width), BF, ANY), ((total, 3 * own), F32, ANY),
-                ((width, 3 * own), BF, ANY), ((2, total), F32, VM),
+                segment_ids.astype(F32)[None], spots, attn_gain.astype(F32)[None],
+                mlp_gain.astype(F32)[None], jnp.zeros((4, count), F32),
+            ]
+        )
+        table = rope_table(count, hw)
+        chunk = n_shard - 1
+        tokens_g, wq, wg, auxg, squares, hats, rots, probs, context_b, attn_raw = call(
+            functools.partial(attn_kernel, n_shard, n_rep, heads), "attn", 1,
+            [
+                ((total, width), BF, ANY), ((width, 3 * own), BF, ANY), ((width, 2 * ff), BF, ANY),
+                ((n_shard, 8, count), F32, VM), ((2, total), F32, VM), ((total, 2 * own), F32, VM),
+                ((total, 3 * own), BF, VM), ((total, heads * count), F32, VM),
+                ((total, own), BF, VM), ((count, width), F32, VM),
             ],
-            [ANY, ANY],
+            [ANY, VM, ANY, VM, ANY, VM, VM, VM],
             [
-                gathered, pltpu.VMEM((width, 3 * own), BF), pltpu.VMEM((own, 3 * own), BF),
+                gathered, pltpu.VMEM((width, 3 * own), BF), pltpu.VMEM((own, 2 * ff), BF),
                 pltpu.VMEM((total, 3 * own), F32), pltpu.VMEM((2, total), F32),
-                pltpu.VMEM((n_shard - 1, 2, total), F32),
-                DMA((1,)), DMA((chips,)), DMA((chips,)), DMA((n_shard - 1,)), DMA((n_shard - 1,)),
-            ] + gather_sems(n_shard) + columns_sems(n_shard, n_rep, 3),
-            tokens, w_qkv,
-        )
-        query, keys, values_b = qkv[:, :own], qkv[:, own : 2 * own], qkv[:, 2 * own :].astype(BF)
-        scales = lax.rsqrt(squares / width + EPSILON)
-        query_scale, keys_scale = scales[0][:, None], scales[1][:, None]
-        query_hat, keys_hat = query * query_scale, keys * keys_scale
-
-        def rot(x, sign):
-            return rotate(x.reshape(total, heads, hw), cos3, sign * sin3).reshape(total, own)
-
-        query_rot = rot(query_hat * gain_query, 1.0).astype(BF)
-        keys_rot = rot(keys_hat * gain_keys, 1.0).astype(BF)
-
-        slots = jnp.arange(count)
-        ok = (seg[:, :, None] == seg[:, None, :]) & (slots[None, :] <= slots[:, None])[None]
-        ok = ok[:, None]
-
-        def blocks(x):
-            return x.reshape(n_shard, count, heads, hw)
-
-        root = hw ** (-0.5)
-        qb, kb, vb = blocks(query_rot), blocks(keys_rot), blocks(values_b)
-        scores = jnp.einsum("bthd,bshd->bhts", qb, kb, preferred_element_type=F32) * root
-        scores = jnp.where(ok, scores, -1e30)
-        top = jnp.max(scores, axis=-1, keepdims=True)
-        lse = top + jnp.log(jnp.sum(jnp.exp(scores - top), axis=-1, keepdims=True))
-        probs = jnp.exp(scores - lse)
-        probs_b = probs.astype(BF)
-        context = jnp.einsum("bhts,bshd->bthd", probs_b, vb, preferred_element_type=F32)
-        context_b = context.astype(BF).reshape(total, own)
-
-        attn_raw, wg = call(
-            functools.partial(attn_out_kernel, n_shard, n_rep), "attn_out", 2,
-            [((count, width), F32, VM), ((width, 2 * ff), BF, ANY)],
-            [VM, VM, ANY],
-            [pltpu.VMEM((own, 2 * ff), BF)] + scatter_bufs(n_shard, count, width)
-            + scatter_sems(n_shard) + columns_sems(n_shard, n_rep, 2),
-            context_b, w_out, w_gate_up,
-        )
+                pltpu.VMEM((chunk, 2, total), F32),
+                DMA((2,)), DMA((chips,)), DMA((chunk,)), DMA((chunk,)), DMA((chunk,)), DMA((chunk,)),
+            ] + gather_sems(n_shard) + columns_sems(n_shard, n_rep, 3)
+            + columns_sems(n_shard, n_rep, 2)
+            + scatter_bufs(n_shard, count, width) + scatter_sems(n_shard),
+            tokens, aux, w_qkv, w_out, w_gate_up, table, gain_query[None], gain_keys[None],
+        )
+        gain_attn = auxg[:, 2].reshape(-1)
+        gain_mlp = auxg[:, 3].reshape(-1)
         attn_scale = norm_scale(attn_raw)
         attn_hat = attn_raw * attn_scale
         resid = tokens.astype(F32) + attn_hat * gain_attn
@@ -905,13 +1289,13 @@
         resid_g, gate_up, mixed_b, down_raw = call(
             functools.partial(mlp_kernel, n_shard), "mlp", 3,
             [
-                ((total, width), BF, ANY), ((total, 2 * ff), F32, ANY),
+                ((total, width), BF, ANY), ((total, 2 * ff), BF, ANY),
                 ((total, ff), BF, ANY), ((count, width), F32, VM),
             ],
             [ANY, ANY, ANY],
             [
                 gathered, pltpu.VMEM((width, 2 * ff), BF), pltpu.VMEM((ff, width), BF),
-                pltpu.VMEM((total, 2 * ff), F32), pltpu.VMEM((total, ff), BF),
+                pltpu.VMEM((total, 2 * ff), BF), pltpu.VMEM((total, ff), BF),
                 DMA((3,)), DMA((chips,)), DMA((chips,)), DMA((chips,)),
             ] + scatter_bufs(n_shard, count, width) + scatter_sems(n_shard) + gather_sems(n_shard),
             resid.astype(BF), wg, w_down,
@@ -923,70 +1307,55 @@
         valid = (segment_ids >= 0).astype(F32)[:, None]
         d_out = cotangent.astype(F32) * valid
         d_down, grad_mlp = norm_back(d_out, down_hat, down_scale, gain_mlp)
-        d_down_g, d_gu_b, d_resid_sum = call(
-            functools.partial(mlp_back_kernel, n_shard), "mlp_back", 4,
-            [((total, width), BF, ANY), ((total, 2 * ff), BF, ANY), ((count, width), F32, VM)],
-            [ANY, ANY, ANY, ANY],
+        most = 4 * own
+        gu_sum, down_acc, d_resid_sum = call(
+            functools.partial(mlp_back_kernel, n_shard, n_rep), "mlp_back", 4,
+            [
+                ((width // n_rep, 2 * ff), BF, ANY), ((ff, width), BF, ANY),
+                ((count, width), F32, VM),
+            ],
+            [ANY] * 6,
             [
                 gathered, pltpu.VMEM((width, 2 * ff), BF), pltpu.VMEM((ff, width), BF),
-                pltpu.VMEM((total, 2 * ff), F32), pltpu.VMEM((total, 2 * ff), BF),
-                DMA((3,)), DMA((chips,)), DMA((chips,)), DMA((chips,)),
-            ] + scatter_bufs(n_shard, count, width) + scatter_sems(n_shard) + gather_sems(n_shard),
-            d_down.astype(BF), gate_up, wg, w_down,
+                pltpu.VMEM((total, 2 * ff), BF), pltpu.VMEM((total, 2 * ff), BF),
+                gathered, pltpu.VMEM((total, ff), BF), pltpu.VMEM((most, total), BF),
+                pltpu.VMEM((ff, width), BF), DMA((5,)), DMA((chips,)), DMA((n_shard,)),
+            ] + share_scratch(width, 2 * ff, n_shard, n_rep)
+            + scatter_bufs(n_shard, count, width) + scatter_sems(n_shard) + gather_sems(n_shard),
+            d_down.astype(BF), gate_up, wg, w_down, resid_g, mixed_b,
         )
         d_resid = d_out + d_resid_sum
-        grad_down = rep_sum(mm_tn(mixed_b, d_down_g))
-        grad_gu = grad_back(mm_tn(resid_g, d_gu_b), 2)
-
         d_attn, grad_attn = norm_back(d_resid, attn_hat, attn_scale, gain_attn)
-        d_attn_g, d_context_b = call(
-            functools.partial(context_back_kernel, n_shard), "context_back", 5,
-            [((total, width), BF, ANY), ((total, own), BF, VM)],
-            [ANY, VM],
-            [gathered, DMA((1,)), DMA((chips,))] + gather_sems(n_shard),
-            d_attn.astype(BF), w_out,
-        )
-        grad_out = rep_sum(mm_tn(context_b, d_attn_g))
-
-        db = blocks(d_context_b)
-        d_values = jnp.einsum("bhts,bthd->bshd", probs_b, db, preferred_element_type=F32)
-        d_probs = jnp.einsum("bthd,bshd->bhts", db, vb, preferred_element_type=F32)
-        delta = jnp.sum(db.astype(F32) * context, axis=-1).transpose(0, 2, 1)[..., None]
-        d_scores_b = (probs * (d_probs - delta) * root).astype(BF)
-        d_query_rot = jnp.einsum("bhts,bshd->bthd", d_scores_b, kb, preferred_element_type=F32)
-        d_keys_rot = jnp.einsum("bhts,bthd->bshd", d_scores_b, qb, preferred_element_type=F32)
-        d_query_norm = rot(d_query_rot, -1.0)
-        d_keys_norm = rot(d_keys_rot, -1.0)
-        grad_query = jnp.sum(d_query_norm * query_hat, axis=0)
-        grad_keys = jnp.sum(d_keys_norm * keys_hat, axis=0)
-        query_up = d_query_norm * gain_query
-        keys_up = d_keys_norm * gain_keys
-        inner = group_sum(
-            jnp.stack([jnp.sum(query_up * query_hat, axis=-1), jnp.sum(keys_up * keys_hat, axis=-1)])
-        ) / width
-        d_query = query_scale * (query_up - query_hat * inner[0][:, None])
-        d_keys = keys_scale * (keys_up - keys_hat * inner[1][:, None])
-        d_qkv_b = jnp.concatenate(
-            [d_query, d_keys, d_values.reshape(total, own)], axis=1
-        ).astype(BF)
-        d_tokens_sum = call(
-            functools.partial(tokens_back_kernel, n_shard), "tokens_back", 6,
-            [((count, width), F32, VM)], [VM, VM],
-            scatter_bufs(n_shard, count, width) + scatter_sems(n_shard),
-            d_qkv_b, wq,
-        )[0]
+
+        gu_rows, down_rows, out_rows, qkv_rows, gains_qk, d_tokens_sum = call(
+            functools.partial(attn_back_kernel, n_shard, n_rep, heads), "attn_back", 5,
+            [
+                ((own, n_shard * 2 * ff), BF, ANY), ((ff, width), BF, ANY), ((own, width), BF, ANY),
+                ((own, 3 * width), BF, ANY), ((2, own), F32, VM), ((count, width), F32, VM),
+            ],
+            [ANY, ANY, VM, ANY, VM, VM, VM, VM, VM, VM, VM, VM, VM, ANY, ANY],
+            [
+                gathered, gathered, pltpu.VMEM((width, 3 * own), BF), pltpu.VMEM((total, own), BF),
+                pltpu.VMEM((total, 2 * own), F32), pltpu.VMEM((total, 3 * own), BF),
+                pltpu.VMEM((most, total), BF), pltpu.VMEM((2, total), F32),
+                pltpu.VMEM((2, total), F32), pltpu.VMEM((chunk, 2, total), F32),
+                DMA((4,)), DMA((chunk,)), DMA((chunk,)),
+            ] + gather_sems(n_shard) + scatter_bufs(n_shard, count, width) + scatter_sems(n_shard)
+            + share_scratch(ff, width, 1, n_rep) + share_scratch(own, width, 1, n_rep)
+            + share_scratch(width, 3 * own, n_shard, n_rep)
+            + share_gather_sems(n_rep) * 2
+            + rows_back_sems(n_shard, n_rep, 2) + rows_back_sems(n_shard, n_rep, 3),
+            d_attn.astype(BF), tokens_g, w_out, wq, hats, rots, probs, context_b, auxg, squares,
+            table, gain_query[None], gain_keys[None], gu_sum, down_acc,
+        )
         grad_tokens = d_resid + d_tokens_sum
-        grad_qkv = grad_back(mm_tn(tokens_g, d_qkv_b), 3)
-
         gains_local = lax.psum_scatter(
             jnp.stack([grad_attn, grad_mlp]), "shard", scatter_dimension=1, tiled=True
         )
-        gains = lax.psum(
-            jnp.concatenate([gains_local, jnp.stack([grad_query, grad_keys])]), "rep"
-        )
+        gains = lax.psum(jnp.concatenate([gains_local, gains_qk]), "rep")
         return (
-            output, grad_tokens, grad_qkv, grad_out, grad_gu, grad_down,
-            gains[2], gains[3], gains[0], gains[1],
+            output, grad_tokens, qkv_rows.astype(F32), out_rows.astype(F32), gu_rows.astype(F32),
+            down_rows.astype(F32), gains[2], gains[3], gains[0], gains[1],
         )
 
     return shards

time: 851 us -> 706 us (0.83)
  Pallas kernels: 558 us -> 646 us
  waiting for transfers between devices: 72.2 us -> 0.02 us
  other arithmetic: 71.3 us -> 30.6 us
  matrix products: 40.3 us -> 0 us
  local copies, waits for them, and re-layouts: 39.2 us -> 5.75 us
  blocking collectives: 26.5 us -> 4.93 us
  starting transfers between devices: 19.3 us -> 0.04 us
    pallas_call x7 -> x4, Pallas kernels: 558 us -> 646 us  [call(): pl.pallas_call(kernel, name=name, out_shape=[jax.ShapeDtypeStruct(shape,...]
    ppermute x8 -> x0, waiting for transfers between devices: 72.2 us -> none  [the longest x4 72.1 us: rep_gather(): got = lax.ppermute(x, 'rep', [(0, 1), (1, 0)])]
    dot_general x10 -> x0, matrix products: 40.3 us -> none  [the longest x4 36.8 us: mm_tn(): lax.dot_general(left, right, (((0,), (0,)), ((), ())), preferred_element_...]
    all_gather x1 -> x0, blocking collectives: 21.6 us -> none  [shards(): lax.all_gather(jnp.stack([segment_ids.astype(BF), attn_gain, mlp_gain])[N...]
    convert_element_type x7 -> x0, local copies, waits for them, and re-layouts: 18.6 us -> none  [the longest x3 13.1 us: grad_back(): whole.transpose(0, 2, 3, 1, 4).reshape(own, groups * n_shard * width)]
    another operation x8 -> x0, other arithmetic: 13.3 us -> none
    another operation x6 -> x0, local copies, waits for them, and re-layouts: 12.9 us -> none  [rep_gather(): return jnp.stack([first, second])]
    all_to_all x2 -> x0, starting transfers between devices: 11 us -> none  [grad_back(): lax.all_to_all(part, 'shard', split_axis=0, concat_axis=0, tiled=True)]
  transfers between devices with their start and end apart: 11 -> 1, of which waited for: 2 -> 0; matrix products, arithmetic and copies ran while one was open for 11% -> 2% of each run, Pallas kernels for 16% -> 30%
where the time goes in v3:
time: 706 us; the launch traced here: 702 us
  Pallas kernels  646 us (92%)
  other arithmetic  30.6 us (4%)
  between operations  14.2 us (2%)
    pallas_call x4, Pallas kernels, call(): pl.pallas_call(kernel, name=name, out_shape=[jax.ShapeDtypeStruct(shape,...  646 us
  transfers between devices with their start and end apart: 1, of which 0 were waited for; matrix products, arithmetic and copies ran while one was open for 2% of the time, Pallas kernels for 30%

profile of v3, /device:TPU:0, one launch (start us, length us, event | category | flops | bytes accessed | tf_op | source)
XLA Modules:
  0.0 701.8 jit_solution(2069687477909542204)
XLA Ops:
  7.2 0.7 compare_convert_fusion
  7.9 0.7 convert_bitcast_fusion
  8.6 0.8 slice_compare_fusion
  9.4 0.3 reduce_window_max.10
  9.8 0.3 fusion.4
  10.0 1.2 bitcast_convert_fusion.2
  11.2 0.7 bitcast_convert_fusion
  11.9 0.8 pad_maximum_fusion.table_ref
  12.7 0.6 concatenate.21.aux_ref
  13.3 200.1 %attn.1 = (bf16[2048,2048]{1,0:T(8,128)(2,1)}, bf16[2048,384]{1,0:T(8,128)(2,1)}, bf16[2048,1024]{1,0:T(8,128)(2,1)}, f32[16,8,128]{2,1,0:T(8,128)}, f32[2,2048]...) custom-call(bf16[128,2048]{1,0:T(8,128)(2,1)} %x_ref.1, ...), custom_call_target="tpu_custom_call" | custom-call | tf_op jit(solution)/shard_map/attn/pallas_call | solution.py:612
  213.4 1.4 multiply_reduce_fusion.5
  214.8 0.9 fusion.7
  215.8 2.2 fusion.2.x_ref
  218.0 106.9 %mlp.1 = (bf16[2048,2048]{1,0:T(8,128)(2,1)}, bf16[2048,1024]{1,0:T(8,128)(2,1)}, bf16[2048,512]{1,0:T(8,128)(2,1)}, f32[128,2048]{1,0:T(8,128)}) custom-call(bf16[128,2048]{1,0:T(8,128)(2,1)} %fusion.2.x_ref, bf16[2048,1024]{1,0:T(8,128)(2,1)} %get-tuple-element.35.wg_ref, bf16[512,2048]{1,0:T(8,128)(2,1)} %wd_ref.3), custom_call_target="tpu_custom_call" | custom-call | tf_op jit(solution)/shard_map/mlp/pallas_call | solution.py:612
  324.9 1.5 multiply_reduce_fusion.4
  326.4 1.6 multiply_reduce_fusion
  328.0 1.1 multiply_convert_fusion.1.x_ref
  329.2 129.3 %mlp_back.1 = (bf16[1024,1024]{1,0:T(8,128)(2,1)}, bf16[512,2048]{1,0:T(8,128)(2,1)}, f32[128,2048]{1,0:T(8,128)}) custom-call(bf16[128,2048]{1,0:T(8,128)(2,1)} %multiply_convert_fusion.1.x_ref, bf16[2048,1024]{1,0:T(8,128)(2,1)} %get-tuple-element.37.gu_ref, bf16[2048,1024]{1,0:T(8,128)(2,1)} %get-tuple-element.35.wg_ref, bf16[512,2048]{1,0:T(8,128)(2,1)} %wd_ref.3, ...), custom_call_target="tpu_custom_call" | custom-call | tf_op jit(solution)/shard_map/mlp_back/pallas_call | solution.py:612
  458.5 1.8 multiply_reduce_fusion.1
  460.3 1.4 copy.21
  461.7 2.9 multiply_convert_fusion
  464.6 210.0 %attn_back.1 = (bf16[128,16384]{1,0:T(8,128)(2,1)}, bf16[512,2048]{1,0:T(8,128)(2,1)}, bf16[128,2048]{1,0:T(8,128)(2,1)}, bf16[128,6144]{1,0:T(8,128)(2,1)}, f32[2,128]{1,0:T(2,128)}, /*index=5*/f32[128,2048]{1,0:T(8,128)}) custom-call(bf16[128,2048]{1,0:T(8,128)(2,1)} %get-tuple-element.60.x_ref, bf16[2048,2048]{1,0:T(8,128)(2,1)} %get-tuple-element.41.tok_ref, ...), custom_call_target="tpu_custom_call" | custom-call | tf_op jit(solution)/shard_map/attn_back/pallas_call | solution.py:612
  674.6 2.5 fusion.6
  677.2 1.1 convert_element_type.61
  678.3 2.0 convert_element_type.60
  680.3 0.3 copy-done.7
  680.6 2.7 convert_element_type.63
  683.3 1.0 copy-done.6
  684.3 4.2 convert_element_type.62
  688.5 0.9 copy.22
  689.5 4.9 psum.7
  694.4 0.5 slice_bitcast_fusion
  (33 shorter events, 0.3 us)
Async XLA Ops:
  7.2 681.4 %reduce-scatter.4.cloned.1.call-start = ((), (), s32[]{:S(2)}) async-start(), calls=%async_computation.1 | async-start | bytes 1114112
  13.3 202.5 %copy-start.5 = (bf16[128,2048]{1,0:T(8,128)(2,1)S(1)}, bf16[128,2048]{1,0:T(8,128)(2,1)}, u32[]{:S(2)}) copy-start(bf16[128,2048]{1,0:T(8,128)(2,1)} %x_ref.1) | copy-start | bytes 1572868
  218.0 108.4 %copy-start.3 = (bf16[128,2048]{1,0:T(8,128)(2,1)S(1)}, bf16[128,2048]{1,0:T(8,128)(2,1)}, u32[]{:S(2)}) copy-start(bf16[128,2048]{1,0:T(8,128)(2,1)} %param.13) | copy-start | bytes 1572868
  324.9 3.1 copy-start.1
  329.2 129.3 %copy-start = (f32[128,2048]{1,0:T(8,128)S(1)}, f32[128,2048]{1,0:T(8,128)}, u32[]{:S(2)}) copy-start(f32[128,2048]{1,0:T(8,128)} %get-tuple-element.33) | copy-start | bytes 3145732
  458.5 3.2 copy-start.2
  464.6 210.0 %copy-start.4 = (f32[128,2048]{1,0:T(8,128)S(1)}, f32[128,2048]{1,0:T(8,128)}, u32[]{:S(2)}) copy-start(f32[128,2048]{1,0:T(8,128)} %get-tuple-element.40) | copy-start | bytes 3145732
  674.6 2.6 copy-start.9
  674.6 3.6 copy-start.8
  678.3 2.3 copy-start.7
  680.6 3.7 copy-start.6
  684.3 5.1 copy-start.10
Sparse Core Ops, SparseCore 0:
  461.8 88.8 reduce-scatter.3

commit v4 on v3

--- a/solution.py
+++ b/solution.py
@@ -17,6 +17,7 @@
 ANY = pl.BlockSpec(memory_space=pl.ANY)
 VM = pl.BlockSpec(memory_space=pltpu.VMEM)
 CHUNKS = 2
+UNROLL = 2
 VMEM_LIMIT = 62 << 20
 
 
@@ -34,6 +35,13 @@
     near = jnp.where(t % 2 == 1, a - (t + 1) // 2, a + (t + 1) // 2)
     far = jnp.where(m == a, t, na - 1 - t)
     return jnp.where(t <= 2 * m, near, far)
+
+
+def peer(k, flip, sign):
+    s = lax.axis_index("shard")
+    na = lax.axis_size("shard") // 4
+    a, b, c = s // 4, (s // 2) % 2, s % 2
+    return index(lax.rem(a + na + sign * (k // 2), na), (b + flip) % 2, (c + k) % 2)
 
 
 def rows_of(i, size):
@@ -359,25 +367,25 @@
             self.stage, self.out.at[rows_of(self.s, self.own)], self.lsem.at[self.groups]
         )
 
-    def start(self):
+    def start(self, flip, low, high):
+        def one(k, _):
+            for g in range(self.groups):
+                self.move(self.s, peer(k, flip, 1), g).start()
+            return 0
+
+        lax.fori_loop(low, high, one, 0)
+
+    def start_own(self):
         for g in range(self.groups):
             self.local_in(g).start()
-
-        def one(k, _):
-            target = lax.rem(self.s + k, self.n_shard)
-            for g in range(self.groups):
-                self.move(self.s, target, g).start()
-            return 0
-
-        lax.fori_loop(1, self.n_shard, one, 0)
         if self.stage is not None:
             for g in range(self.groups):
                 self.local_in(g).wait()
             self.local_out().start()
 
-    def forward(self, low, high):
-        def one(k, _):
-            source = lax.rem(self.s + self.n_shard - k, self.n_shard)
+    def forward(self, flip, low, high):
+        def one(k, _):
+            source = peer(k, flip, -1)
             for g in range(self.groups):
                 self.move(source, self.s, g).wait_recv()
             for m in range(1, self.n_rep):
@@ -402,11 +410,6 @@
         else:
             for g in range(self.groups):
                 self.local_in(g).wait()
-
-    def spread(self, t, steps):
-        each = -(-(self.n_shard - 1) // steps)
-        low = 1 + t * each
-        self.forward(low, jnp.minimum(low + each, self.n_shard))
 
 
 class ShareSum:
@@ -532,16 +535,17 @@
             rep=lax.rem(self.r + m, self.n_rep),
         )
 
-    def start(self):
+    def start(self, flip, low, high):
+        def one(k, _):
+            for g in range(self.groups):
+                self.move(self.s, peer(k, flip, 1), g).start()
+            return 0
+
+        lax.fori_loop(low, high, one, 0)
+
+    def start_own(self):
         for g in range(self.groups):
             self.local(g).start()
-
-        def one(k, _):
-            for g in range(self.groups):
-                self.move(self.s, lax.rem(self.s + k, self.n_shard), g).start()
-            return 0
-
-        lax.fori_loop(1, self.n_shard, one, 0)
 
     def relay(self, source):
         for g in range(self.groups):
@@ -553,24 +557,15 @@
             self.local(g).wait()
         self.relay(self.s)
 
-    def forward(self, low, high):
-        def one(k, _):
-            source = lax.rem(self.s + self.n_shard - k, self.n_shard)
+    def forward(self, flip, low, high):
+        def one(k, _):
+            source = peer(k, flip, -1)
             for g in range(self.groups):
                 self.move(source, self.s, g).wait_recv()
             self.relay(source)
             return 0
 
         lax.fori_loop(low, high, one, 0)
-
-    def spread(self, t, steps):
-        @pl.when(t == 0)
-        def _():
-            self.forward_own()
-
-        each = -(-(self.n_shard - 1) // steps)
-        low = 1 + t * each
-        self.forward(low, jnp.minimum(low + each, self.n_shard))
 
     def finish(self):
         def one(k, _):
@@ -714,7 +709,10 @@
     def hook(t):
         @pl.when(t == 0)
         def _():
-            qkv_w.start()
+            qkv_w.start_own()
+            gu_w.start_own()
+            qkv_w.start(0, 1, half)
+            qkv_w.start(1, 0, half)
 
             def one(k, _):
                 aux_desc(k).start()
@@ -722,13 +720,18 @@
 
             lax.fori_loop(1, n_shard, one, 0)
 
-        @pl.when(t > 0)
-        def _():
-            qkv_w.spread(t - 1, na - 1)
+        @pl.when(t == na - 1)
+        def _():
+            gu_w.start(0, 1, half)
+            qkv_w.forward(0, 1, half)
+            qkv_w.forward(1, 0, half)
+
+    half = n_shard // 2
 
     gather_loop(pos, count, buf, gsems, out_x.start, hook)
+    early = half * 3 // 8
+    gu_w.start(1, 0, early)
     qkv_w.finish()
-    gu_w.start()
     keep = load(wq, wq_ref, lsem.at[1])
 
     def project(q, _):
@@ -742,6 +745,7 @@
 
     lax.fori_loop(0, chips, project, 0)
     exchange_start(n_shard, stats, got, xs, xr)
+    gu_w.start(1, early, half)
     exchange_finish(n_shard, stats, got, xs, xr, sums_ref)
 
     def aux_done(k, _):
@@ -787,16 +791,23 @@
             probs = e / jnp.sum(e, axis=-1, keepdims=True)
             prob_ref[r, h * count : (h + 1) * count] = probs
             ctx_ref[r, cols] = mm(probs.astype(BF), values).astype(BF)
-        return 0
-
-    lax.fori_loop(0, n_shard, attend, 0)
+
+        @pl.when(i >= half + 1)
+        def _():
+            gu_w.forward(0, i - half, i - half + 1)
+
+        return 0
+
+    lax.fori_loop(0, n_shard, attend, 0, unroll=UNROLL)
 
     def partial(q):
         r = rows_of(q, big)
         p[r, :] = mm(ctx_ref[r, :], wo_ref[...]).astype(BF)
 
-    scatter_loop(pos, count, bufs, ssems, partial, out_ref, lambda t: gu_w.spread(t, na))
-    gu_w.spread(na - 1, na)
+    def hook2(t):
+        gu_w.forward(1, half * t // (na - 1), half * (t + 1) // (na - 1))
+
+    scatter_loop(pos, count, bufs, ssems, partial, out_ref, hook2)
     gu_w.finish()
     keep.wait()
     wait_all([out_x], chips)
@@ -887,21 +898,10 @@
     wait_all([out_x, out_g, out_m], chips)
 
 
-def flip(src, cols, flipped):
-    step = 256
-
-    def one(k, _):
-        at = rows_of(k, step)
-        flipped[:, at] = jnp.transpose(src[at, cols])
-        return 0
-
-    lax.fori_loop(0, src.shape[0] // step, one, 0)
-
-
 def mlp_back_kernel(
     n_shard, n_rep, x_ref, gu_ref, wg_ref, wd_ref, resid_ref, mixed_ref,
     gsum_ref, down_ref, out_ref,
-    buf, wg, wd, gu, dgu, resid, mixed, flipped, down, lsem, isem, osem, acc, got, xs, xr, *rest,
+    buf, wg, wd, gu, dgu, resid, mixed, down, lsem, isem, osem, acc, got, xs, xr, *rest,
 ):
     pos = position(n_shard)
     na = pos[3]
@@ -962,16 +962,16 @@
         lax.fori_loop(0, width // 256, one, 0)
 
     shares = ShareSum(acc, got, (xs, xr), n_shard, n_rep)
-    most = flipped.shape[0]
-    owners = most // own
+    owners = 4
+    most = owners * own
     parts = width // most
 
     def grad_rows(k):
-        flip(resid, pl.ds(pl.multiple_of(k * most, most), most), flipped)
+        at = rows_of(k, most)
 
         def one(n, _):
             lo = rows_of(n, 256)
-            acc[rows_of(k, most), lo] = mm(flipped[...], dgu[:, lo]).astype(BF)
+            acc[at, lo] = mm_tn(resid[:, at], dgu[:, lo]).astype(BF)
             return 0
 
         lax.fori_loop(0, 2 * ff // 256, one, 0)
@@ -983,15 +983,17 @@
             grad_rows(k)
             return 0
 
-        lax.fori_loop(parts * t // (na - 1), parts * (t + 1) // (na - 1), one, 0)
+        lax.fori_loop(
+            (parts * t + na - 2) // (na - 1), (parts * (t + 1) + na - 2) // (na - 1), one, 0
+        )
 
     def grad_down():
         def rows(m, _):
-            flip(mixed, pl.ds(pl.multiple_of(m * most, most), most), flipped)
+            at = rows_of(m, most)
 
             def one(n, _):
                 lo = rows_of(n, 256)
-                down[rows_of(m, most), lo] = mm(flipped[...], buf[:, lo]).astype(BF)
+                down[at, lo] = mm_tn(mixed[:, at], buf[:, lo]).astype(BF)
                 return 0
 
             lax.fori_loop(0, width // 256, one, 0)
@@ -1027,7 +1029,7 @@
     x_ref, tok_ref, wo_ref, wq_ref, hats_ref, rot_ref, prob_ref, ctx_ref, aux_ref, sums_ref,
     table_ref, qg_ref, kg_ref, gsum_ref, down_ref,
     gu_ref, dn_ref, go_ref, gq_ref, gains_ref, out_ref,
-    buf, tok, wq, dctx, ups, dqkv, flipped, stats, inner, got, lsem, xs, xr, *rest,
+    buf, tok, wq, dctx, ups, dqkv, stats, inner, got, lsem, xs, xr, *rest,
 ):
     rest = list(rest)
 
@@ -1069,21 +1071,26 @@
     def hook(t):
         @pl.when(t == 0)
         def _():
-            gu_rows.start()
+            gu_rows.start_own()
             in_d.wait()
             down.start(0)
 
-        @pl.when(t > 0)
-        def _():
-            gu_rows.spread(t - 1, na - 1)
+        @pl.when(t == na - 1)
+        def _():
+            gu_rows.start(0, 1, half)
+            gu_rows.forward_own()
+            down.add(0)
+            down_all.start()
+
+    half = n_shard // 2
 
     def on_chip(q):
         r = rows_of(q, big)
         dctx[r, :] = mm_nt(buf[r, :], wo_ref[...]).astype(BF)
 
     gather_loop(pos, count, buf, gsems, on_chip, hook)
-    down.add(0)
-    down_all.start()
+    early = half * 5 // 8
+    gu_rows.start(1, 0, early)
     root = hw ** (-0.5)
     gains_ref[...] = jnp.zeros_like(gains_ref)
 
@@ -1122,17 +1129,20 @@
                 totals[g] = totals[g] + row_sums(up * hat)
         for g in range(2):
             stats[pl.ds(g, 1), at] = totals[g]
-        return 0
-
-    lax.fori_loop(0, n_shard, attend, 0)
+
+        @pl.when(i >= half + 1)
+        def _():
+            gu_rows.forward(0, i - half, i - half + 1)
+
+        return 0
+
+    lax.fori_loop(0, n_shard, attend, 0, unroll=UNROLL)
     exchange_start(n_shard, stats, got, xs, xr)
-
-    fo = flipped.at[pl.ds(0, own)]
-    flip(ctx_ref, slice(0, own), fo)
+    gu_rows.start(1, early, half)
 
     def out_cols(n, _):
         lo = rows_of(n, 256)
-        oacc[:, lo] = mm(fo[...], buf[:, lo]).astype(BF)
+        oacc[:, lo] = mm_tn(ctx_ref[...], buf[:, lo]).astype(BF)
         return 0
 
     lax.fori_loop(0, width // 256, out_cols, 0)
@@ -1165,35 +1175,47 @@
 
         lax.fori_loop(0, width // 512, one, 0)
 
-    most = flipped.shape[0]
-    owners = most // own
+    most = 4 * own
 
     def grad_rows(k, _):
-        flip(tok, pl.ds(pl.multiple_of(k * most, most), most), flipped)
-        qacc[rows_of(k, most), :] = mm(flipped[...], dqkv[...]).astype(BF)
-        for d in range(owners):
-            wqkv.start(k * owners + d)
-        return 0
-
-    def sum_up(d, _):
-        wqkv.add(d)
-        return 0
+        at = rows_of(k, most)
+        qacc[at, :] = mm_tn(tok[:, at], dqkv[...]).astype(BF)
+        return 0
+
+    def near_far(do, flip):
+        def one(k, _):
+            do(peer(k, flip, 1))
+            return 0
+
+        lax.fori_loop(0, half, one, 0)
 
     def hook2(t):
         @pl.when(t == 0)
         def _():
             lax.fori_loop(0, width // most, grad_rows, 0)
-
-        @pl.when(t == 1)
-        def _():
-            lax.fori_loop(0, n_shard, sum_up, 0)
-            wqkv_rows.start()
+            near_far(wqkv.start, 0)
+            near_far(wqkv.start, 1)
             wout.add(0)
             wout_all.start()
-
-    scatter_loop(
-        pos, count, bufs, ssems, partial, out_ref, hook2, lambda: wqkv_rows.spread(0, 1)
-    )
+            gu_rows.forward(1, 0, half)
+
+        @pl.when(t == 1)
+        def _():
+            near_far(wqkv.add, 0)
+            wqkv_rows.start_own()
+            wqkv_rows.start(0, 1, half)
+
+        @pl.when(t == 2)
+        def _():
+            near_far(wqkv.add, 1)
+            wqkv_rows.start(1, 0, half)
+
+    def final():
+        wqkv_rows.forward_own()
+        wqkv_rows.forward(0, 1, half)
+
+    scatter_loop(pos, count, bufs, ssems, partial, out_ref, hook2, final)
+    wqkv_rows.forward(1, 0, half)
 
     def end(d, _):
         wqkv.sent(d)
@@ -1307,7 +1329,6 @@
         valid = (segment_ids >= 0).astype(F32)[:, None]
         d_out = cotangent.astype(F32) * valid
         d_down, grad_mlp = norm_back(d_out, down_hat, down_scale, gain_mlp)
-        most = 4 * own
         gu_sum, down_acc, d_resid_sum = call(
             functools.partial(mlp_back_kernel, n_shard, n_rep), "mlp_back", 4,
             [
@@ -1318,7 +1339,7 @@
             [
                 gathered, pltpu.VMEM((width, 2 * ff), BF), pltpu.VMEM((ff, width), BF),
                 pltpu.VMEM((total, 2 * ff), BF), pltpu.VMEM((total, 2 * ff), BF),
-                gathered, pltpu.VMEM((total, ff), BF), pltpu.VMEM((most, total), BF),
+                gathered, pltpu.VMEM((total, ff), BF),
                 pltpu.VMEM((ff, width), BF), DMA((5,)), DMA((chips,)), DMA((n_shard,)),
             ] + share_scratch(width, 2 * ff, n_shard, n_rep)
             + scatter_bufs(n_shard, count, width) + scatter_sems(n_shard) + gather_sems(n_shard),
@@ -1337,7 +1358,7 @@
             [
                 gathered, gathered, pltpu.VMEM((width, 3 * own), BF), pltpu.VMEM((total, own), BF),
                 pltpu.VMEM((total, 2 * own), F32), pltpu.VMEM((total, 3 * own), BF),
-                pltpu.VMEM((most, total), BF), pltpu.VMEM((2, total), F32),
+                pltpu.VMEM((2, total), F32),
                 pltpu.VMEM((2, total), F32), pltpu.VMEM((chunk, 2, total), F32),
                 DMA((4,)), DMA((chunk,)), DMA((chunk,)),
             ] + gather_sems(n_shard) + scatter_bufs(n_shard, count, width) + scatter_sems(n_shard)

time: 706 us -> 658 us (0.932)
  Pallas kernels: 646 us -> 602 us
    pallas_call x4, Pallas kernels: 646 us -> 602 us  [call(): pl.pallas_call(kernel, name=name, out_shape=[jax.ShapeDtypeStruct(shape,...]
  transfers between devices with their start and end apart: 1 -> 1, of which waited for: 0 -> 0; matrix products, arithmetic and copies ran while one was open for 2% -> 2% of each run, Pallas kernels for 30% -> 29%
where the time goes in v4:
time: 658 us
  Pallas kernels  602 us (91%)
  other arithmetic  30.6 us (5%)
  between operations  14.2 us (2%)
    pallas_call x4, Pallas kernels, call(): pl.pallas_call(kernel, name=name, out_shape=[jax.ShapeDtypeStruct(shape,...  602 us
  transfers between devices with their start and end apart: 1, of which 0 were waited for; matrix products, arithmetic and copies ran while one was open for 2% of the time, Pallas kernels for 29%

profile of v4, /device:TPU:0, one launch (start us, length us, event | category | flops | bytes accessed | tf_op | source)
XLA Modules:
  0.0 657.7 jit_solution(13510601063174884879)
XLA Ops:
  7.2 0.7 compare_convert_fusion
  7.9 0.7 convert_bitcast_fusion
  8.6 0.8 slice_compare_fusion
  9.4 0.3 reduce_window_max.10
  9.8 0.3 fusion.4
  10.0 1.2 bitcast_convert_fusion.2
  11.2 0.7 bitcast_convert_fusion
  11.9 0.8 pad_maximum_fusion.table_ref
  12.7 0.6 concatenate.21.aux_ref
  13.3 173.4 %attn.1 = (bf16[2048,2048]{1,0:T(8,128)(2,1)}, bf16[2048,384]{1,0:T(8,128)(2,1)}, bf16[2048,1024]{1,0:T(8,128)(2,1)}, f32[16,8,128]{2,1,0:T(8,128)}, f32[2,2048]...) custom-call(bf16[128,2048]{1,0:T(8,128)(2,1)} %x_ref.1, ...), custom_call_target="tpu_custom_call" | custom-call | tf_op jit(solution)/shard_map/attn/pallas_call | solution.py:607
  186.7 1.4 multiply_reduce_fusion.5
  188.0 0.9 fusion.7
  189.0 2.2 fusion.2.x_ref
  191.2 108.7 %mlp.1 = (bf16[2048,2048]{1,0:T(8,128)(2,1)}, bf16[2048,1024]{1,0:T(8,128)(2,1)}, bf16[2048,512]{1,0:T(8,128)(2,1)}, f32[128,2048]{1,0:T(8,128)}) custom-call(bf16[128,2048]{1,0:T(8,128)(2,1)} %fusion.2.x_ref, bf16[2048,1024]{1,0:T(8,128)(2,1)} %get-tuple-element.35.wg_ref, bf16[512,2048]{1,0:T(8,128)(2,1)} %wd_ref.3), custom_call_target="tpu_custom_call" | custom-call | tf_op jit(solution)/shard_map/mlp/pallas_call | solution.py:607
  300.0 1.5 multiply_reduce_fusion.4
  301.5 1.6 multiply_reduce_fusion
  303.1 1.1 multiply_convert_fusion.1.x_ref
  304.3 127.2 %mlp_back.1 = (bf16[1024,1024]{1,0:T(8,128)(2,1)}, bf16[512,2048]{1,0:T(8,128)(2,1)}, f32[128,2048]{1,0:T(8,128)}) custom-call(bf16[128,2048]{1,0:T(8,128)(2,1)} %multiply_convert_fusion.1.x_ref, bf16[2048,1024]{1,0:T(8,128)(2,1)} %get-tuple-element.37.gu_ref, bf16[2048,1024]{1,0:T(8,128)(2,1)} %get-tuple-element.35.wg_ref, bf16[512,2048]{1,0:T(8,128)(2,1)} %wd_ref.3, ...), custom_call_target="tpu_custom_call" | custom-call | tf_op jit(solution)/shard_map/mlp_back/pallas_call | solution.py:607
  431.5 1.8 multiply_reduce_fusion.1
  433.3 1.4 copy.21
  434.7 2.9 multiply_convert_fusion
  437.6 192.9 %attn_back.1 = (bf16[128,16384]{1,0:T(8,128)(2,1)}, bf16[512,2048]{1,0:T(8,128)(2,1)}, bf16[128,2048]{1,0:T(8,128)(2,1)}, bf16[128,6144]{1,0:T(8,128)(2,1)}, f32[2,128]{1,0:T(2,128)}, /*index=5*/f32[128,2048]{1,0:T(8,128)}) custom-call(bf16[128,2048]{1,0:T(8,128)(2,1)} %get-tuple-element.60.x_ref, bf16[2048,2048]{1,0:T(8,128)(2,1)} %get-tuple-element.41.tok_ref, ...), custom_call_target="tpu_custom_call" | custom-call | tf_op jit(solution)/shard_map/attn_back/pallas_call | solution.py:607
  630.6 2.5 fusion.6
  633.1 1.1 convert_element_type.61
  634.2 2.0 convert_element_type.60
  636.2 0.3 copy-done.7
  636.5 2.7 convert_element_type.63
  639.2 1.0 copy-done.6
  640.2 4.2 convert_element_type.62
  644.5 0.9 copy.22
  645.4 4.9 psum.7
  650.3 0.5 slice_bitcast_fusion
  (33 shorter events, 0.3 us)
Async XLA Ops:
  7.2 637.3 %reduce-scatter.4.cloned.1.call-start = ((), (), s32[]{:S(2)}) async-start(), calls=%async_computation.1 | async-start | bytes 1114112
  13.3 175.7 %copy-start.5 = (bf16[128,2048]{1,0:T(8,128)(2,1)S(1)}, bf16[128,2048]{1,0:T(8,128)(2,1)}, u32[]{:S(2)}) copy-start(bf16[128,2048]{1,0:T(8,128)(2,1)} %x_ref.1) | copy-start | bytes 1572868
  191.2 110.2 %copy-start.3 = (bf16[128,2048]{1,0:T(8,128)(2,1)S(1)}, bf16[128,2048]{1,0:T(8,128)(2,1)}, u32[]{:S(2)}) copy-start(bf16[128,2048]{1,0:T(8,128)(2,1)} %param.13) | copy-start | bytes 1572868
  300.0 3.1 copy-start.1
  304.3 127.2 %copy-start = (f32[128,2048]{1,0:T(8,128)S(1)}, f32[128,2048]{1,0:T(8,128)}, u32[]{:S(2)}) copy-start(f32[128,2048]{1,0:T(8,128)} %get-tuple-element.33) | copy-start | bytes 3145732
  431.5 3.2 copy-start.2
  437.6 192.9 %copy-start.4 = (f32[128,2048]{1,0:T(8,128)S(1)}, f32[128,2048]{1,0:T(8,128)}, u32[]{:S(2)}) copy-start(f32[128,2048]{1,0:T(8,128)} %get-tuple-element.40) | copy-start | bytes 3145732
  630.5 2.6 copy-start.9
  630.6 3.6 copy-start.8
  634.2 2.3 copy-start.7
  636.5 3.7 copy-start.6
  640.2 5.1 copy-start.10
Sparse Core Ops, SparseCore 0:
  434.8 61.0 reduce-scatter.3

commit v5 on v4

--- a/solution.py
+++ b/solution.py
@@ -124,14 +124,14 @@
     def arrived(i, ch):
         desc(i, ch, csend.at[0], index(a, b, 1 - c)).wait_recv()
 
-    def pair_step(j):
+    def pair_step(j, t):
         i = index(j, 1 - b, c)
         for ch in range(CHUNKS):
             arrived(i, ch)
             desc(i, ch, csend.at[(j * 2 + 1 - b) * CHUNKS + ch], index(a, b, 1 - c)).start()
         for ch in range(CHUNKS):
             arrived(index(j, 1 - b, 1 - c), ch)
-        on_chip(j * 2 + 1 - b)
+        on_chip(j * 2 + 1 - b, t)
 
     def step(t, _):
         j = line_order(t, a, na)
@@ -146,16 +146,16 @@
             hook(t)
         for ch in range(CHUNKS):
             arrived(index(j, b, 1 - c), ch)
-        on_chip(j * 2 + b)
+        on_chip(j * 2 + b, t)
 
         @pl.when(t > 0)
         def _():
-            pair_step(line_order(t - 1, a, na))
+            pair_step(line_order(t - 1, a, na), t)
 
         return 0
 
     lax.fori_loop(0, na, step, 0)
-    pair_step(line_order(na - 1, a, na))
+    pair_step(line_order(na - 1, a, na), na)
 
     def finish(j, _):
         i = index(j, b, c)
@@ -191,7 +191,7 @@
     ]
 
 
-def scatter_loop(pos, count, bufs, sems, partial, out, hook=None, final=None):
+def scatter_loop(pos, count, bufs, sems, partial, out, works=(), order=None):
     p, cgot, ygot, zgot = bufs
     csend, crecv, ysend, yrecv, zsend, zrecv = sems
     a, b, c, na = pos
@@ -243,14 +243,10 @@
         to_pair(j).start()
         return 0
 
-    lax.fori_loop(0, na, first, 0)
-
     def second(t, _):
         j = line_order(na - 1 - t, a, na)
         near = j * 2 + b
         i = index(j, b, c)
-        if hook is not None:
-            hook(t)
         to_core(near).wait_recv()
         to_pair(j).wait_recv()
         inner = ((j < a) & (a < na - 1)) | ((j > a) & (a > 0))
@@ -274,9 +270,21 @@
 
         return 0
 
-    lax.fori_loop(0, na - 1, second, 0)
-    if final is not None:
-        final()
+    if order is None:
+        lax.fori_loop(0, na, first, 0)
+        lax.fori_loop(0, na - 1, second, 0)
+    else:
+        done_first = done_second = 0
+        for token in order:
+            if token == "f":
+                first(done_first, 0)
+                done_first += 1
+            elif token == "s":
+                second(done_second, 0)
+                done_second += 1
+            else:
+                works[int(token)]()
+        assert done_first == na and done_second == na - 1
     near = a * 2 + b
     to_core(near).wait_recv()
     to_pair(a).wait_recv()
@@ -728,12 +736,6 @@
 
     half = n_shard // 2
 
-    gather_loop(pos, count, buf, gsems, out_x.start, hook)
-    early = half * 3 // 8
-    gu_w.start(1, 0, early)
-    qkv_w.finish()
-    keep = load(wq, wq_ref, lsem.at[1])
-
     def project(q, _):
         r = rows_of(q, big)
         v = mm(buf[r, :], wq[...])
@@ -743,6 +745,11 @@
             stats[pl.ds(g, 1), pl.ds(pl.multiple_of(q * big, big), big)] = row_sums(x * x)
         return 0
 
+    gather_loop(pos, count, buf, gsems, lambda q, t: out_x.start(q), hook)
+    early = half * 3 // 8
+    gu_w.start(1, 0, early)
+    qkv_w.finish()
+    keep = load(wq, wq_ref, lsem.at[1])
     lax.fori_loop(0, chips, project, 0)
     exchange_start(n_shard, stats, got, xs, xr)
     gu_w.start(1, early, half)
@@ -804,10 +811,13 @@
         r = rows_of(q, big)
         p[r, :] = mm(ctx_ref[r, :], wo_ref[...]).astype(BF)
 
-    def hook2(t):
-        gu_w.forward(1, half * t // (na - 1), half * (t + 1) // (na - 1))
-
-    scatter_loop(pos, count, bufs, ssems, partial, out_ref, hook2)
+    def pass_far(t):
+        return lambda: gu_w.forward(1, half * t // 3, half * (t + 1) // 3)
+
+    scatter_loop(
+        pos, count, bufs, ssems, partial, out_ref, [pass_far(t) for t in range(3)],
+        "f" * na + "0s1s2" + "s" * (na - 3),
+    )
     gu_w.finish()
     keep.wait()
     wait_all([out_x], chips)
@@ -863,7 +873,7 @@
     out_m = Out(mixed, mixed_ref, msem, big)
     w1.wait()
 
-    def on_chip(q):
+    def on_chip(q, t):
         r = rows_of(q, big)
         out_x.start(q)
 
@@ -929,7 +939,7 @@
     mine.wait()
     w2.wait()
 
-    def on_chip(q):
+    def on_chip(q, t):
         r = rows_of(q, big)
         saved.wait(q)
 
@@ -955,11 +965,11 @@
         r = rows_of(q, big)
 
         def one(k, _):
-            lo = rows_of(k, 256)
+            lo = rows_of(k, 512)
             p[r, lo] = mm_nt(dgu[r, :], wg[lo, :]).astype(BF)
             return 0
 
-        lax.fori_loop(0, width // 256, one, 0)
+        lax.fori_loop(0, width // 512, one, 0)
 
     shares = ShareSum(acc, got, (xs, xr), n_shard, n_rep)
     owners = 4
@@ -978,15 +988,6 @@
         for d in range(owners):
             shares.start(k * owners + d)
 
-    def hook(t):
-        def one(k, _):
-            grad_rows(k)
-            return 0
-
-        lax.fori_loop(
-            (parts * t + na - 2) // (na - 1), (parts * (t + 1) + na - 2) // (na - 1), one, 0
-        )
-
     def grad_down():
         def rows(m, _):
             at = rows_of(m, most)
@@ -1002,7 +1003,20 @@
         lax.fori_loop(0, ff // most, rows, 0)
         load(down, down_ref, lsem.at[3])
 
-    scatter_loop(pos, count, bufs, ssems, partial, out_ref, hook, grad_down)
+    def chunk(t):
+        def run():
+            def one(k, _):
+                grad_rows(k)
+                return 0
+
+            lax.fori_loop(parts * t // 4, parts * (t + 1) // 4, one, 0)
+
+        return run
+
+    scatter_loop(
+        pos, count, bufs, ssems, partial, out_ref, [chunk(t) for t in range(4)] + [grad_down],
+        "0ff1" + "f" * (na - 2) + "s2s3" + "s" * (na - 3) + "4",
+    )
 
     def collect(d, _):
         shares.add(d)
@@ -1027,9 +1041,9 @@
 def attn_back_kernel(
     n_shard, n_rep, heads,
     x_ref, tok_ref, wo_ref, wq_ref, hats_ref, rot_ref, prob_ref, ctx_ref, aux_ref, sums_ref,
-    table_ref, qg_ref, kg_ref, gsum_ref, down_ref,
+    table_ref, qg_ref, kg_ref, gain_ref, gsum_ref, down_ref,
     gu_ref, dn_ref, go_ref, gq_ref, gains_ref, out_ref,
-    buf, tok, wq, dctx, ups, dqkv, stats, inner, got, lsem, xs, xr, *rest,
+    buf, tok, wq, dctx, ups, dqkv, stats, inner, got, ggot, mine_g, rgot, lsem, xs, xr, gs, gr, rs, rr, *rest,
 ):
     rest = list(rest)
 
@@ -1075,16 +1089,33 @@
             in_d.wait()
             down.start(0)
 
+            def one(k, _):
+                gain_desc(k).start()
+                return 0
+
+            lax.fori_loop(1, n_shard, one, 0)
+
+        @pl.when(t == na - 2)
+        def _():
+            down.add(0)
+            down_all.start()
+
         @pl.when(t == na - 1)
         def _():
             gu_rows.start(0, 1, half)
             gu_rows.forward_own()
-            down.add(0)
-            down_all.start()
 
     half = n_shard // 2
 
-    def on_chip(q):
+    def gain_desc(k):
+        target = lax.rem(lax.axis_index("shard") + k, n_shard)
+        return send(gain_ref.at[target], ggot.at[k - 1], gs.at[k - 1], gr.at[k - 1], shard=target)
+
+    def gain_rep(m):
+        target = lax.rem(r_me + m, n_rep)
+        return send(mine_g, rgot.at[m - 1], rs.at[m - 1], rr.at[m - 1], rep=target)
+
+    def on_chip(q, t):
         r = rows_of(q, big)
         dctx[r, :] = mm_nt(buf[r, :], wo_ref[...]).astype(BF)
 
@@ -1092,7 +1123,7 @@
     early = half * 5 // 8
     gu_rows.start(1, 0, early)
     root = hw ** (-0.5)
-    gains_ref[...] = jnp.zeros_like(gains_ref)
+    mine_g[...] = gain_ref[lax.axis_index("shard")]
 
     def scale_of(i):
         at = pl.ds(pl.multiple_of(i * count, count), count)
@@ -1123,16 +1154,16 @@
             for g, (x, gain) in enumerate(((d_query, qg_ref), (d_keys, kg_ref))):
                 x = x * cos - swap_halves(x) * sin
                 hat = hats_ref[r, part(g)]
-                gains_ref[g : g + 1, cols] += jnp.sum(x * hat, axis=0, keepdims=True)
+                mine_g[2 + g : 3 + g, cols] += jnp.sum(x * hat, axis=0, keepdims=True)
                 up = x * gain[:, cols]
                 ups[r, part(g)] = up
                 totals[g] = totals[g] + row_sums(up * hat)
         for g in range(2):
             stats[pl.ds(g, 1), at] = totals[g]
 
-        @pl.when(i >= half + 1)
+        @pl.when((i > 0) & (i < half))
         def _():
-            gu_rows.forward(0, i - half, i - half + 1)
+            gu_rows.forward(0, i, i + 1)
 
         return 0
 
@@ -1147,6 +1178,15 @@
 
     lax.fori_loop(0, width // 256, out_cols, 0)
     wout.start(0)
+
+    def gain_take(k, _):
+        gain_desc(k).wait_recv()
+        mine_g[...] += ggot[k - 1]
+        return 0
+
+    lax.fori_loop(1, n_shard, gain_take, 0)
+    for m in range(1, n_rep):
+        gain_rep(m).start()
     exchange_finish(n_shard, stats, got, xs, xr, inner)
 
     def settle(i, _):
@@ -1189,33 +1229,38 @@
 
         lax.fori_loop(0, half, one, 0)
 
-    def hook2(t):
-        @pl.when(t == 0)
-        def _():
-            lax.fori_loop(0, width // most, grad_rows, 0)
-            near_far(wqkv.start, 0)
-            near_far(wqkv.start, 1)
-            wout.add(0)
-            wout_all.start()
-            gu_rows.forward(1, 0, half)
-
-        @pl.when(t == 1)
-        def _():
-            near_far(wqkv.add, 0)
-            wqkv_rows.start_own()
-            wqkv_rows.start(0, 1, half)
-
-        @pl.when(t == 2)
-        def _():
-            near_far(wqkv.add, 1)
-            wqkv_rows.start(1, 0, half)
-
-    def final():
+    def work0():
+        lax.fori_loop(0, width // most, grad_rows, 0)
+        near_far(wqkv.start, 0)
+        near_far(wqkv.start, 1)
+
+    def work1():
+        gu_rows.forward(1, 0, half)
+
+    def work2():
+        wout.add(0)
+        wout_all.start()
+
+    def work3():
+        near_far(wqkv.add, 0)
+        wqkv_rows.start_own()
+        wqkv_rows.start(0, 1, half)
+
+    def work4():
+        near_far(wqkv.add, 1)
+        wqkv_rows.start(1, 0, half)
+
+    def work5():
         wqkv_rows.forward_own()
         wqkv_rows.forward(0, 1, half)
 
-    scatter_loop(pos, count, bufs, ssems, partial, out_ref, hook2, final)
-    wqkv_rows.forward(1, 0, half)
+    def work6():
+        wqkv_rows.forward(1, 0, half)
+
+    scatter_loop(
+        pos, count, bufs, ssems, partial, out_ref, [work0, work1, work2, work3, work4, work5, work6],
+        "0" + "f" * na + "12s3s45" + "s" * (na - 3) + "6",
+    )
 
     def end(d, _):
         wqkv.sent(d)
@@ -1224,6 +1269,18 @@
     lax.fori_loop(0, n_shard, end, 0)
     down.sent(0)
     wout.sent(0)
+
+    def gain_sent(k, _):
+        gain_desc(k).wait_send()
+        return 0
+
+    lax.fori_loop(1, n_shard, gain_sent, 0)
+    gains_ref[...] = mine_g[...]
+    for m in range(1, n_rep):
+        gain_rep(m).wait_recv()
+        gains_ref[...] += rgot[m - 1]
+    for m in range(1, n_rep):
+        gain_rep(m).wait_send()
     wqkv_rows.finish()
     gu_rows.finish()
     down_all.finish()
@@ -1348,32 +1405,33 @@
         d_resid = d_out + d_resid_sum
         d_attn, grad_attn = norm_back(d_resid, attn_hat, attn_scale, gain_attn)
 
-        gu_rows, down_rows, out_rows, qkv_rows, gains_qk, d_tokens_sum = call(
+        norm_gains = jnp.stack([grad_attn.reshape(n_shard, own), grad_mlp.reshape(n_shard, own)], axis=1)
+        norm_gains = jnp.pad(norm_gains, ((0, 0), (0, 6), (0, 0)))
+        gu_rows, down_rows, out_rows, qkv_rows, gains, d_tokens_sum = call(
             functools.partial(attn_back_kernel, n_shard, n_rep, heads), "attn_back", 5,
             [
                 ((own, n_shard * 2 * ff), BF, ANY), ((ff, width), BF, ANY), ((own, width), BF, ANY),
-                ((own, 3 * width), BF, ANY), ((2, own), F32, VM), ((count, width), F32, VM),
+                ((own, 3 * width), BF, ANY), ((8, own), F32, VM), ((count, width), F32, VM),
             ],
-            [ANY, ANY, VM, ANY, VM, VM, VM, VM, VM, VM, VM, VM, VM, ANY, ANY],
+            [ANY, ANY, VM, ANY, VM, VM, VM, VM, VM, VM, VM, VM, VM, VM, ANY, ANY],
             [
                 gathered, gathered, pltpu.VMEM((width, 3 * own), BF), pltpu.VMEM((total, own), BF),
                 pltpu.VMEM((total, 2 * own), F32), pltpu.VMEM((total, 3 * own), BF),
                 pltpu.VMEM((2, total), F32),
                 pltpu.VMEM((2, total), F32), pltpu.VMEM((chunk, 2, total), F32),
-                DMA((4,)), DMA((chunk,)), DMA((chunk,)),
+                pltpu.VMEM((chunk, 8, own), F32), pltpu.VMEM((8, own), F32),
+                pltpu.VMEM((n_rep - 1, 8, own), F32),
+                DMA((4,)), DMA((chunk,)), DMA((chunk,)), DMA((chunk,)), DMA((chunk,)),
+                DMA((n_rep - 1,)), DMA((n_rep - 1,)),
             ] + gather_sems(n_shard) + scatter_bufs(n_shard, count, width) + scatter_sems(n_shard)
             + share_scratch(ff, width, 1, n_rep) + share_scratch(own, width, 1, n_rep)
             + share_scratch(width, 3 * own, n_shard, n_rep)
             + share_gather_sems(n_rep) * 2
             + rows_back_sems(n_shard, n_rep, 2) + rows_back_sems(n_shard, n_rep, 3),
             d_attn.astype(BF), tokens_g, w_out, wq, hats, rots, probs, context_b, auxg, squares,
-            table, gain_query[None], gain_keys[None], gu_sum, down_acc,
+            table, gain_query[None], gain_keys[None], norm_gains, gu_sum, down_acc,
         )
         grad_tokens = d_resid + d_tokens_sum
-        gains_local = lax.psum_scatter(
-            jnp.stack([grad_attn, grad_mlp]), "shard", scatter_dimension=1, tiled=True
-        )
-        gains = lax.psum(jnp.concatenate([gains_local, gains_qk]), "rep")
         return (
             output, grad_tokens, qkv_rows.astype(F32), out_rows.astype(F32), gu_rows.astype(F32),
             down_rows.astype(F32), gains[2], gains[3], gains[0], gains[1],

time: 658 us -> 619 us (0.941)
  Pallas kernels: 602 us -> 584 us
  between operations: 14.2 us -> 0.81 us
    pallas_call x4, Pallas kernels: 602 us -> 584 us  [call(): pl.pallas_call(kernel, name=name, out_shape=[jax.ShapeDtypeStruct(shape,...]
  transfers between devices with their start and end apart: 1 -> 0, of which waited for: 0 -> 0; matrix products, arithmetic and copies ran while one was open for 2% -> 0% of each run, Pallas kernels for 29% -> 0%
where the time goes in v5:
time: 619 us; the launch traced here: 618 us
  Pallas kernels  584 us (94%)
  other arithmetic  29.9 us (5%)
    pallas_call x4, Pallas kernels, call(): pl.pallas_call(kernel, name=name, out_shape=[jax.ShapeDtypeStruct(shape,...  584 us

profile of v5, /device:TPU:0, one launch (start us, length us, event | category | flops | bytes accessed | tf_op | source)
XLA Modules:
  0.0 618.3 jit_solution(15367734650925209742)
XLA Ops:
  0.6 0.7 compare_convert_fusion
  1.3 0.8 slice_compare_fusion
  2.1 0.1 add_select_fusion
  2.2 0.3 reduce_window_max.10
  2.5 0.7 convert_bitcast_fusion
  3.2 1.2 bitcast_convert_fusion.2
  4.4 0.7 bitcast_convert_fusion
  5.0 0.6 concatenate.18.aux_ref
  5.7 0.3 fusion.4
  5.9 0.8 pad_maximum_fusion.table_ref
  6.7 173.3 %attn.1 = (bf16[2048,2048]{1,0:T(8,128)(2,1)}, bf16[2048,384]{1,0:T(8,128)(2,1)}, bf16[2048,1024]{1,0:T(8,128)(2,1)}, f32[16,8,128]{2,1,0:T(8,128)}, f32[2,2048]...) custom-call(bf16[128,2048]{1,0:T(8,128)(2,1)} %x_ref.1, ...), custom_call_target="tpu_custom_call" | custom-call | tf_op jit(solution)/shard_map/attn/pallas_call | solution.py:615
  180.0 1.4 multiply_reduce_fusion.5
  181.4 0.9 fusion.7
  182.4 2.2 fusion.2.x_ref
  184.6 108.9 %mlp.1 = (bf16[2048,2048]{1,0:T(8,128)(2,1)}, bf16[2048,1024]{1,0:T(8,128)(2,1)}, bf16[2048,512]{1,0:T(8,128)(2,1)}, f32[128,2048]{1,0:T(8,128)}) custom-call(bf16[128,2048]{1,0:T(8,128)(2,1)} %fusion.2.x_ref, bf16[2048,1024]{1,0:T(8,128)(2,1)} %get-tuple-element.35.wg_ref, bf16[512,2048]{1,0:T(8,128)(2,1)} %wd_ref.3), custom_call_target="tpu_custom_call" | custom-call | tf_op jit(solution)/shard_map/mlp/pallas_call | solution.py:615
  293.5 1.5 multiply_reduce_fusion.4
  295.0 1.6 multiply_reduce_fusion
  296.6 1.1 multiply_convert_fusion.1.x_ref
  297.8 121.7 %mlp_back.1 = (bf16[1024,1024]{1,0:T(8,128)(2,1)}, bf16[512,2048]{1,0:T(8,128)(2,1)}, f32[128,2048]{1,0:T(8,128)}) custom-call(bf16[128,2048]{1,0:T(8,128)(2,1)} %multiply_convert_fusion.1.x_ref, bf16[2048,1024]{1,0:T(8,128)(2,1)} %get-tuple-element.37.gu_ref, bf16[2048,1024]{1,0:T(8,128)(2,1)} %get-tuple-element.35.wg_ref, bf16[512,2048]{1,0:T(8,128)(2,1)} %wd_ref.3, ...), custom_call_target="tpu_custom_call" | custom-call | tf_op jit(solution)/shard_map/mlp_back/pallas_call | solution.py:615
  419.5 1.8 multiply_reduce_fusion.1
  421.4 0.1 copy-done.7
  421.4 1.6 multiply_convert_fusion
  423.0 0.6 select_maximum_fusion.gain_ref
  423.7 180.2 %attn_back.1 = (bf16[128,16384]{1,0:T(8,128)(2,1)}, bf16[512,2048]{1,0:T(8,128)(2,1)}, bf16[128,2048]{1,0:T(8,128)(2,1)}, bf16[128,6144]{1,0:T(8,128)(2,1)}, f32[8,128]{1,0:T(8,128)}, /*index=5*/f32[128,2048]{1,0:T(8,128)}) custom-call(bf16[128,2048]{1,0:T(8,128)(2,1)} %get-tuple-element.60.x_ref, bf16[2048,2048]{1,0:T(8,128)(2,1)} %get-tuple-element.41.tok_ref, ...), custom_call_target="tpu_custom_call" | custom-call | tf_op jit(solution)/shard_map/attn_back/pallas_call | solution.py:615
  603.9 2.5 fusion.6
  606.5 0.5 slice_bitcast_fusion
  607.0 1.1 convert_element_type.63
  608.1 2.0 convert_element_type.62
  610.0 0.3 copy-done.9
  610.4 2.7 convert_element_type.65
  613.0 1.0 copy-done.8
  614.1 4.2 convert_element_type.64
  (30 shorter events, 0.1 us)
Async XLA Ops:
  6.7 175.7 %copy-start.6 = (bf16[128,2048]{1,0:T(8,128)(2,1)S(1)}, bf16[128,2048]{1,0:T(8,128)(2,1)}, u32[]{:S(2)}) copy-start(bf16[128,2048]{1,0:T(8,128)(2,1)} %x_ref.1) | copy-start | bytes 1572868
  184.6 110.3 %copy-start.3 = (bf16[128,2048]{1,0:T(8,128)(2,1)S(1)}, bf16[128,2048]{1,0:T(8,128)(2,1)}, u32[]{:S(2)}) copy-start(bf16[128,2048]{1,0:T(8,128)(2,1)} %param.13) | copy-start | bytes 1572868
  293.5 3.1 copy-start.1
  297.8 121.7 %copy-start = (f32[128,2048]{1,0:T(8,128)S(1)}, f32[128,2048]{1,0:T(8,128)}, u32[]{:S(2)}) copy-start(f32[128,2048]{1,0:T(8,128)} %get-tuple-element.33) | copy-start | bytes 3145732
  419.5 1.9 copy-start.2
  419.5 1.9 copy-start.4
  419.5 2.0 copy-start.7
  423.7 180.2 %copy-start.5 = (f32[128,2048]{1,0:T(8,128)S(1)}, f32[128,2048]{1,0:T(8,128)}, u32[]{:S(2)}) copy-start(f32[128,2048]{1,0:T(8,128)} %get-tuple-element.40) | copy-start | bytes 3145732
  603.9 2.6 copy-start.12
  603.9 3.1 copy-start.11
  603.9 4.2 copy-start.10
  608.1 2.3 copy-start.9
  610.4 3.7 copy-start.8

commit v6 on v5

--- a/solution.py
+++ b/solution.py
@@ -2,6 +2,7 @@
 
 import jax
 import jax.numpy as jnp
+import numpy as np
 from jax import lax
 from jax.experimental import pallas as pl
 from jax.experimental.pallas import tpu as pltpu
@@ -665,6 +666,14 @@
     return jnp.transpose(jnp.broadcast_to(row, (count, count)))
 
 
+def spots_of(seg_row, count):
+    lane = lax.broadcasted_iota(jnp.int32, (count, count), 1).astype(F32)
+    slot = lax.broadcasted_iota(jnp.int32, (count, count), 0).astype(F32)
+    same = turned(seg_row, count) == seg_row
+    first = jnp.min(jnp.where(same, lane, float(count)), axis=-1, keepdims=True)
+    return same & (lane <= slot), slot[:, :1] - first
+
+
 def swap_halves(x):
     return pltpu.roll(x, x.shape[1] // 2, 1)
 
@@ -686,11 +695,38 @@
     )[:1]
 
 
+def gain_rows(aux_ref, k, row):
+    own = aux_ref.shape[2]
+    for d in range(aux_ref.shape[0]):
+        row[:, d * own : (d + 1) * own] = aux_ref[d, k : k + 1, :]
+
+
+def norm_rows(rows, do):
+    tile = 32
+
+    def one(k, _):
+        do(rows_of(k, tile))
+        return 0
+
+    lax.fori_loop(0, rows // tile, one, 0)
+
+
+def row_scale(v):
+    return lax.rsqrt(jnp.mean(v * v, axis=-1, keepdims=True) + EPSILON)
+
+
+def norm_back(upstream, normed, rscale, gain):
+    scaled = upstream * gain
+    inner = jnp.mean(scaled * normed, axis=-1, keepdims=True)
+    return rscale * (scaled - normed * inner)
+
+
 def attn_kernel(
     n_shard, n_rep, heads,
-    x_ref, aux_ref, wqkv_ref, wo_ref, wgu_ref, table_ref, qg_ref, kg_ref,
-    g_ref, wq_ref, wg_ref, auxg_ref, sums_ref, hats_ref, rot_ref, prob_ref, ctx_ref, out_ref,
-    buf, wq, stage, qkv, stats, got, lsem, osem, xs, xr, as_, ar, *rest,
+    x_ref, aux_ref, wqkv_ref, wo_ref, wgu_ref, table_ref,
+    g_ref, wq_ref, wg_ref, auxg_ref, sums_ref, hats_ref, rot_ref, prob_ref, ctx_ref,
+    out_ref, scale_ref, resid_ref, residb_ref,
+    row, buf, wq, stage, qkv, stats, got, lsem, osem, xs, xr, as_, ar, *rest,
 ):
     pos = position(n_shard)
     gsems, c3, c2, bufs, ssems = rest[:5], rest[5:10], rest[10:15], rest[15:19], rest[19:]
@@ -743,16 +779,19 @@
         for g in range(2):
             x = v[:, g * own : (g + 1) * own]
             stats[pl.ds(g, 1), pl.ds(pl.multiple_of(q * big, big), big)] = row_sums(x * x)
+
+        @pl.when(q > 0)
+        def _():
+            gu_w.forward(0, q, q + 1)
+
         return 0
 
     gather_loop(pos, count, buf, gsems, lambda q, t: out_x.start(q), hook)
-    early = half * 3 // 8
-    gu_w.start(1, 0, early)
     qkv_w.finish()
     keep = load(wq, wq_ref, lsem.at[1])
     lax.fori_loop(0, chips, project, 0)
     exchange_start(n_shard, stats, got, xs, xr)
-    gu_w.start(1, early, half)
+    gu_w.start(1, 0, half)
     exchange_finish(n_shard, stats, got, xs, xr, sums_ref)
 
     def aux_done(k, _):
@@ -762,15 +801,12 @@
 
     lax.fori_loop(1, n_shard, aux_done, 0)
     root = hw ** (-0.5)
-    lane = lax.broadcasted_iota(jnp.int32, (count, count), 1)
-    slot = lax.broadcasted_iota(jnp.int32, (count, count), 0)
 
     def attend(i, _):
         r = rows_of(i, count)
         at = pl.ds(pl.multiple_of(i * count, count), count)
-        spots = turned(auxg_ref[i, 1:2, :], count)
+        ok, spots = spots_of(auxg_ref[i, 0:1, :], count)
         cos, sin = rope_of(spots, table_ref[...])
-        ok = (lane <= slot) & (lane >= slot - spots.astype(jnp.int32))
         scale = lax.rsqrt(sums_ref[:, at] / width + EPSILON)
         q_scale = turned(scale[0:1], count)[:, :1]
         k_scale = turned(scale[1:2], count)[:, :1]
@@ -789,8 +825,8 @@
                 rot_ref[r, part(g)] = x
                 return x
 
-            query = turn(0, q_scale, qg_ref[:, cols])
-            keys = turn(1, k_scale, kg_ref[:, cols])
+            query = turn(0, q_scale, aux_ref[3:4, cols])
+            keys = turn(1, k_scale, aux_ref[4:5, cols])
             values = qkv[r, part(2)].astype(BF)
             rot_ref[r, part(2)] = values
             scores = jnp.where(ok, mm_nt(query, keys) * root, -1e30)
@@ -799,10 +835,6 @@
             prob_ref[r, h * count : (h + 1) * count] = probs
             ctx_ref[r, cols] = mm(probs.astype(BF), values).astype(BF)
 
-        @pl.when(i >= half + 1)
-        def _():
-            gu_w.forward(0, i - half, i - half + 1)
-
         return 0
 
     lax.fori_loop(0, n_shard, attend, 0, unroll=UNROLL)
@@ -818,6 +850,20 @@
         pos, count, bufs, ssems, partial, out_ref, [pass_far(t) for t in range(3)],
         "f" * na + "0s1s2" + "s" * (na - 3),
     )
+    gain_rows(auxg_ref, 1, row)
+
+    def close(at):
+        v = out_ref[at, :]
+        scale = row_scale(v)
+        hat = v * scale
+        out_ref[at, :] = hat
+        scale_ref[at, :] = jnp.broadcast_to(scale, (scale.shape[0], scale_ref.shape[1]))
+        mine_at = pl.ds(pl.multiple_of(s * count + at.start, at.size), at.size)
+        resid = buf[mine_at, :].astype(F32) + hat * row[...]
+        resid_ref[at, :] = resid
+        residb_ref[at, :] = resid.astype(BF)
+
+    norm_rows(count, close)
     gu_w.finish()
     keep.wait()
     wait_all([out_x], chips)
@@ -853,9 +899,16 @@
     lax.fori_loop(1, n_shard, done, 0)
 
 
+def live_rows(aux_ref, pos, mask):
+    a, b, c, _ = pos
+    segs = turned(aux_ref[index(a, b, c), 0:1, :], mask.shape[0])
+    mask[...] = jnp.where(segs >= 0.0, 1.0, 0.0).astype(F32)
+
+
 def mlp_kernel(
-    n_shard, x_ref, wg_ref, wd_ref, g_ref, gu_ref, mixed_ref, out_ref,
-    buf, wg, wd, gu, mixed, lsem, osem, gsem, msem, *rest,
+    n_shard, x_ref, wg_ref, wd_ref, aux_ref, resid_ref, cot_ref,
+    g_ref, gu_ref, mixed_ref, y_ref, d_ref, gain_ref,
+    out_ref, row, mask, buf, wg, wd, gu, mixed, lsem, osem, gsem, msem, *rest,
 ):
     pos = position(n_shard)
     bufs, ssems, gsems = rest[:4], rest[4:10], rest[10:]
@@ -904,14 +957,29 @@
 
         lax.fori_loop(0, width // 512, one, 0)
 
+    gain_rows(aux_ref, 2, row)
+    live_rows(aux_ref, pos, mask)
     scatter_loop(pos, count, bufs, ssems, partial, out_ref)
+    gain_ref[...] = jnp.zeros_like(gain_ref)
+
+    def close(at):
+        v = out_ref[at, :]
+        scale = row_scale(v)
+        hat = v * scale
+        y_ref[at, :] = (resid_ref[at, :] + hat * row[...]).astype(BF)
+        d_out = cot_ref[at, :].astype(F32) * mask[at, :1]
+        gain_ref[...] += jnp.sum(d_out * hat, axis=0, keepdims=True)
+        d_ref[at, :] = norm_back(d_out, hat, scale, row[...]).astype(BF)
+
+    norm_rows(count, close)
     wait_all([out_x, out_g, out_m], chips)
 
 
 def mlp_back_kernel(
     n_shard, n_rep, x_ref, gu_ref, wg_ref, wd_ref, resid_ref, mixed_ref,
-    gsum_ref, down_ref, out_ref,
-    buf, wg, wd, gu, dgu, resid, mixed, down, lsem, isem, osem, acc, got, xs, xr, *rest,
+    aux_ref, cot_ref, hat_ref, scale_ref, mlp_gain_ref,
+    gsum_ref, down_ref, out_ref, d_ref, gain_ref,
+    row, sums, mask, buf, wg, wd, gu, dgu, resid, mixed, down, lsem, isem, osem, acc, got, xs, xr, *rest,
 ):
     pos = position(n_shard)
     na = pos[3]
@@ -1018,6 +1086,24 @@
         "0ff1" + "f" * (na - 2) + "s2s3" + "s" * (na - 3) + "4",
     )
 
+    gain_rows(aux_ref, 1, row)
+    live_rows(aux_ref, pos, mask)
+    sums[...] = jnp.zeros_like(sums)
+
+    def close(at):
+        d_resid = cot_ref[at, :].astype(F32) * mask[at, :1] + out_ref[at, :]
+        out_ref[at, :] = d_resid
+        hat = hat_ref[at, :]
+        sums[...] += jnp.sum(d_resid * hat, axis=0, keepdims=True)
+        d_ref[at, :] = norm_back(d_resid, hat, scale_ref[at, :1], row[...]).astype(BF)
+
+    norm_rows(count, close)
+    gain_ref[...] = jnp.zeros_like(gain_ref)
+    for d in range(n_shard):
+        cols = slice(d * own, (d + 1) * own)
+        gain_ref[d, 0:1, :] = sums[:, cols]
+        gain_ref[d, 1:2, :] = mlp_gain_ref[:, cols]
+
     def collect(d, _):
         shares.add(d)
         pltpu.make_async_copy(
@@ -1041,7 +1127,7 @@
 def attn_back_kernel(
     n_shard, n_rep, heads,
     x_ref, tok_ref, wo_ref, wq_ref, hats_ref, rot_ref, prob_ref, ctx_ref, aux_ref, sums_ref,
-    table_ref, qg_ref, kg_ref, gain_ref, gsum_ref, down_ref,
+    table_ref, gain_ref, gsum_ref, down_ref,
     gu_ref, dn_ref, go_ref, gq_ref, gains_ref, out_ref,
     buf, tok, wq, dctx, ups, dqkv, stats, inner, got, ggot, mine_g, rgot, lsem, xs, xr, gs, gr, rs, rr, *rest,
 ):
@@ -1123,7 +1209,8 @@
     early = half * 5 // 8
     gu_rows.start(1, 0, early)
     root = hw ** (-0.5)
-    mine_g[...] = gain_ref[lax.axis_index("shard")]
+    me = lax.axis_index("shard")
+    mine_g[...] = gain_ref[me]
 
     def scale_of(i):
         at = pl.ds(pl.multiple_of(i * count, count), count)
@@ -1132,7 +1219,7 @@
     def attend(i, _):
         r = rows_of(i, count)
         at = pl.ds(pl.multiple_of(i * count, count), count)
-        cos, sin = rope_of(turned(aux_ref[i, 1:2, :], count), table_ref[...])
+        cos, sin = rope_of(spots_of(aux_ref[i, 0:1, :], count)[1], table_ref[...])
         totals = [jnp.zeros((1, count), F32), jnp.zeros((1, count), F32)]
         for h in range(heads):
             def part(g):
@@ -1151,11 +1238,11 @@
             d_query = mm(d_scores, keys)
             d_keys = mm_tn(d_scores, query)
             dqkv[r, part(2)] = d_values.astype(BF)
-            for g, (x, gain) in enumerate(((d_query, qg_ref), (d_keys, kg_ref))):
+            for g, x in enumerate((d_query, d_keys)):
                 x = x * cos - swap_halves(x) * sin
                 hat = hats_ref[r, part(g)]
                 mine_g[2 + g : 3 + g, cols] += jnp.sum(x * hat, axis=0, keepdims=True)
-                up = x * gain[:, cols]
+                up = x * aux_ref[me, 3 + g : 4 + g, cols]
                 ups[r, part(g)] = up
                 totals[g] = totals[g] + row_sums(up * hat)
         for g in range(2):
@@ -1287,31 +1374,12 @@
     wout_all.finish()
 
 
-def positions(seg):
-    slots = lax.broadcasted_iota(jnp.int32, seg.shape, 1)
-    starts = jnp.concatenate(
-        [jnp.ones((seg.shape[0], 1), jnp.bool_), seg[:, 1:] != seg[:, :-1]], axis=1
-    )
-    first = lax.cummax(jnp.where(starts, slots, 0), axis=1)
-    return slots - first
-
-
 def rope_table(count, head_width):
     half_width = head_width // 2
-    inverse = THETA ** (-(2.0 * jnp.arange(half_width, dtype=F32)) / head_width)
-    angle = jnp.arange(count, dtype=F32)[:, None] * inverse[None, :]
-    cosine, sine = jnp.cos(angle), jnp.sin(angle)
-    return jnp.concatenate([cosine, cosine, -sine, sine], axis=1)
-
-
-def norm_scale(vector):
-    return lax.rsqrt(jnp.mean(vector * vector, axis=-1, keepdims=True) + EPSILON)
-
-
-def norm_back(upstream, normed, rscale, gain):
-    scaled = upstream * gain
-    inner = jnp.mean(scaled * normed, axis=-1, keepdims=True)
-    return rscale * (scaled - normed * inner), jnp.sum(upstream * normed, axis=0)
+    inverse = np.float32(THETA) ** (-(np.float32(2.0) * np.arange(half_width, dtype=np.float32)) / np.float32(head_width))
+    angle = np.arange(count, dtype=np.float32)[:, None] * inverse[None, :].astype(np.float32)
+    cosine, sine = np.cos(angle), np.sin(angle)
+    return np.concatenate([cosine, cosine, -sine, sine], axis=1).astype(np.float32)
 
 
 def make(n_rep, n_shard):
@@ -1329,91 +1397,77 @@
         total = count * n_shard
         gathered = pltpu.VMEM((total, width), BF)
 
-        gain_query = q_gain.astype(F32)
-        gain_keys = k_gain.astype(F32)
-        spots = positions(segment_ids[None]).astype(F32)
-        aux = jnp.concatenate(
-            [
-                segment_ids.astype(F32)[None], spots, attn_gain.astype(F32)[None],
-                mlp_gain.astype(F32)[None], jnp.zeros((4, count), F32),
-            ]
-        )
-        table = rope_table(count, hw)
+        assert own == count
+        aux = jnp.stack(
+            [x.astype(F32) for x in (segment_ids, attn_gain, mlp_gain, q_gain, k_gain)]
+            + [jnp.zeros((count,), F32)] * 3
+        )
+        table = jnp.asarray(rope_table(count, hw))
         chunk = n_shard - 1
-        tokens_g, wq, wg, auxg, squares, hats, rots, probs, context_b, attn_raw = call(
+        (
+            tokens_g, wq, wg, auxg, squares, hats, rots, probs, context_b,
+            attn_hat, attn_scale, resid, resid_b,
+        ) = call(
             functools.partial(attn_kernel, n_shard, n_rep, heads), "attn", 1,
             [
                 ((total, width), BF, ANY), ((width, 3 * own), BF, ANY), ((width, 2 * ff), BF, ANY),
                 ((n_shard, 8, count), F32, VM), ((2, total), F32, VM), ((total, 2 * own), F32, VM),
                 ((total, 3 * own), BF, VM), ((total, heads * count), F32, VM),
-                ((total, own), BF, VM), ((count, width), F32, VM),
+                ((total, own), BF, VM), ((count, width), F32, VM), ((count, 128), F32, VM),
+                ((count, width), F32, VM), ((count, width), BF, VM),
             ],
-            [ANY, VM, ANY, VM, ANY, VM, VM, VM],
+            [ANY, VM, ANY, VM, ANY, VM],
             [
-                gathered, pltpu.VMEM((width, 3 * own), BF), pltpu.VMEM((own, 2 * ff), BF),
+                pltpu.VMEM((1, width), F32), gathered, pltpu.VMEM((width, 3 * own), BF), pltpu.VMEM((own, 2 * ff), BF),
                 pltpu.VMEM((total, 3 * own), F32), pltpu.VMEM((2, total), F32),
                 pltpu.VMEM((chunk, 2, total), F32),
                 DMA((2,)), DMA((chips,)), DMA((chunk,)), DMA((chunk,)), DMA((chunk,)), DMA((chunk,)),
             ] + gather_sems(n_shard) + columns_sems(n_shard, n_rep, 3)
             + columns_sems(n_shard, n_rep, 2)
             + scatter_bufs(n_shard, count, width) + scatter_sems(n_shard),
-            tokens, aux, w_qkv, w_out, w_gate_up, table, gain_query[None], gain_keys[None],
-        )
-        gain_attn = auxg[:, 2].reshape(-1)
-        gain_mlp = auxg[:, 3].reshape(-1)
-        attn_scale = norm_scale(attn_raw)
-        attn_hat = attn_raw * attn_scale
-        resid = tokens.astype(F32) + attn_hat * gain_attn
-
-        resid_g, gate_up, mixed_b, down_raw = call(
+            tokens, aux, w_qkv, w_out, w_gate_up, table,
+        )
+        resid_g, gate_up, mixed_b, output, d_down, grad_mlp = call(
             functools.partial(mlp_kernel, n_shard), "mlp", 3,
             [
                 ((total, width), BF, ANY), ((total, 2 * ff), BF, ANY),
-                ((total, ff), BF, ANY), ((count, width), F32, VM),
+                ((total, ff), BF, ANY), ((count, width), BF, VM), ((count, width), BF, VM),
+                ((1, width), F32, VM),
             ],
-            [ANY, ANY, ANY],
+            [ANY, ANY, ANY, VM, VM, VM],
             [
-                gathered, pltpu.VMEM((width, 2 * ff), BF), pltpu.VMEM((ff, width), BF),
+                pltpu.VMEM((count, width), F32), pltpu.VMEM((1, width), F32),
+                pltpu.VMEM((count, count), F32), gathered, pltpu.VMEM((width, 2 * ff), BF), pltpu.VMEM((ff, width), BF),
                 pltpu.VMEM((total, 2 * ff), BF), pltpu.VMEM((total, ff), BF),
                 DMA((3,)), DMA((chips,)), DMA((chips,)), DMA((chips,)),
             ] + scatter_bufs(n_shard, count, width) + scatter_sems(n_shard) + gather_sems(n_shard),
-            resid.astype(BF), wg, w_down,
-        )
-        down_scale = norm_scale(down_raw)
-        down_hat = down_raw * down_scale
-        output = (resid + down_hat * gain_mlp).astype(BF)
-
-        valid = (segment_ids >= 0).astype(F32)[:, None]
-        d_out = cotangent.astype(F32) * valid
-        d_down, grad_mlp = norm_back(d_out, down_hat, down_scale, gain_mlp)
-        gu_sum, down_acc, d_resid_sum = call(
+            resid_b, wg, w_down, auxg, resid, cotangent,
+        )
+        gu_sum, down_acc, d_resid, d_attn, norm_gains = call(
             functools.partial(mlp_back_kernel, n_shard, n_rep), "mlp_back", 4,
             [
                 ((width // n_rep, 2 * ff), BF, ANY), ((ff, width), BF, ANY),
-                ((count, width), F32, VM),
+                ((count, width), F32, VM), ((count, width), BF, VM), ((n_shard, 8, own), F32, VM),
             ],
-            [ANY] * 6,
+            [ANY] * 6 + [VM] * 5,
             [
-                gathered, pltpu.VMEM((width, 2 * ff), BF), pltpu.VMEM((ff, width), BF),
+                pltpu.VMEM((1, width), F32), pltpu.VMEM((1, width), F32),
+                pltpu.VMEM((count, count), F32), gathered, pltpu.VMEM((width, 2 * ff), BF), pltpu.VMEM((ff, width), BF),
                 pltpu.VMEM((total, 2 * ff), BF), pltpu.VMEM((total, 2 * ff), BF),
                 gathered, pltpu.VMEM((total, ff), BF),
                 pltpu.VMEM((ff, width), BF), DMA((5,)), DMA((chips,)), DMA((n_shard,)),
             ] + share_scratch(width, 2 * ff, n_shard, n_rep)
             + scatter_bufs(n_shard, count, width) + scatter_sems(n_shard) + gather_sems(n_shard),
-            d_down.astype(BF), gate_up, wg, w_down, resid_g, mixed_b,
-        )
-        d_resid = d_out + d_resid_sum
-        d_attn, grad_attn = norm_back(d_resid, attn_hat, attn_scale, gain_attn)
-
-        norm_gains = jnp.stack([grad_attn.reshape(n_shard, own), grad_mlp.reshape(n_shard, own)], axis=1)
-        norm_gains = jnp.pad(norm_gains, ((0, 0), (0, 6), (0, 0)))
+            d_down, gate_up, wg, w_down, resid_g, mixed_b,
+            auxg, cotangent, attn_hat, attn_scale, grad_mlp,
+        )
         gu_rows, down_rows, out_rows, qkv_rows, gains, d_tokens_sum = call(
             functools.partial(attn_back_kernel, n_shard, n_rep, heads), "attn_back", 5,
             [
                 ((own, n_shard * 2 * ff), BF, ANY), ((ff, width), BF, ANY), ((own, width), BF, ANY),
                 ((own, 3 * width), BF, ANY), ((8, own), F32, VM), ((count, width), F32, VM),
             ],
-            [ANY, ANY, VM, ANY, VM, VM, VM, VM, VM, VM, VM, VM, VM, VM, ANY, ANY],
+            [ANY, ANY, VM, ANY, VM, VM, VM, VM, VM, VM, VM, VM, ANY, ANY],
             [
                 gathered, gathered, pltpu.VMEM((width, 3 * own), BF), pltpu.VMEM((total, own), BF),
                 pltpu.VMEM((total, 2 * own), F32), pltpu.VMEM((total, 3 * own), BF),
@@ -1428,8 +1482,8 @@
             + share_scratch(width, 3 * own, n_shard, n_rep)
             + share_gather_sems(n_rep) * 2
             + rows_back_sems(n_shard, n_rep, 2) + rows_back_sems(n_shard, n_rep, 3),
-            d_attn.astype(BF), tokens_g, w_out, wq, hats, rots, probs, context_b, auxg, squares,
-            table, gain_query[None], gain_keys[None], norm_gains, gu_sum, down_acc,
+            d_attn, tokens_g, w_out, wq, hats, rots, probs, context_b, auxg, squares,
+            table, norm_gains, gu_sum, down_acc,
         )
         grad_tokens = d_resid + d_tokens_sum
         return (

time: 619 us -> 606 us (0.979)
  other arithmetic: 29.9 us -> 14.4 us
    reduce_sum x4 -> x0, other arithmetic: 6.33 us -> none  [the longest x2 3.48 us: norm_back(): jnp.sum(upstream * normed, axis=0)]
where the time goes in v6:
time: 606 us; the launch traced here: 605 us
  Pallas kernels  587 us (97%)
  other arithmetic  14.4 us (2%)
    pallas_call x4, Pallas kernels, call(): pl.pallas_call(kernel, name=name, out_shape=[jax.ShapeDtypeStruct(shape,...  587 us

profile of v6, /device:TPU:0, one launch (start us, length us, event | category | flops | bytes accessed | tf_op | source)
XLA Modules:
  0.0 605.4 jit_solution(727460064622692378)
XLA Ops:
  0.6 0.7 convert_bitcast_fusion
  1.3 0.7 bitcast_convert_fusion
  2.0 0.7 bitcast_convert_fusion.2
  2.7 0.6 stack.43.aux_ref
  3.3 171.7 %attn.1 = (bf16[2048,2048]{1,0:T(8,128)(2,1)}, bf16[2048,384]{1,0:T(8,128)(2,1)}, bf16[2048,1024]{1,0:T(8,128)(2,1)}, f32[16,8,128]{2,1,0:T(8,128)}, f32[2,2048]...) custom-call(bf16[128,2048]{1,0:T(8,128)(2,1)} %x_ref.1, ...), custom_call_target="tpu_custom_call" | custom-call | tf_op jit(solution)/shard_map/attn/pallas_call | solution.py:616
  174.9 110.9 %mlp.1 = (bf16[2048,2048]{1,0:T(8,128)(2,1)}, bf16[2048,1024]{1,0:T(8,128)(2,1)}, bf16[2048,512]{1,0:T(8,128)(2,1)}, bf16[128,2048]{1,0:T(8,128)(2,1)}, bf16[128,2048]{1,0:T(8,128)(2,1)}, /*index=5*/f32[1,2048]{1,0:T(1,128)}) custom-call(bf16[128,2048]{1,0:T(8,128)(2,1)} %get-tuple-element.40.x_ref, bf16[2048,1024]{1,0:T(8,128)(2,1)} %get-tuple-element.41.wg_ref, ...), custom_call_target="tpu_custom_call" | custom-call | tf_op jit(solution)/shard_map/mlp/pallas_call | solution.py:616
  285.9 124.5 %mlp_back.1 = (bf16[1024,1024]{1,0:T(8,128)(2,1)}, bf16[512,2048]{1,0:T(8,128)(2,1)}, f32[128,2048]{1,0:T(8,128)}, bf16[128,2048]{1,0:T(8,128)(2,1)}, f32[16,8,128]{2,1,0:T(8,128)}) custom-call(bf16[128,2048]{1,0:T(8,128)(2,1)} %get-tuple-element.45.x_ref, bf16[2048,1024]{1,0:T(8,128)(2,1)} %get-tuple-element.46.gu_ref, ...), custom_call_target="tpu_custom_call" | custom-call | tf_op jit(solution)/shard_map/mlp_back/pallas_call | solution.py:616
  410.3 0.0 copy-start.3
  410.3 179.9 %attn_back.1 = (bf16[128,16384]{1,0:T(8,128)(2,1)}, bf16[512,2048]{1,0:T(8,128)(2,1)}, bf16[128,2048]{1,0:T(8,128)(2,1)}, bf16[128,6144]{1,0:T(8,128)(2,1)}, f32[8,128]{1,0:T(8,128)}, /*index=5*/f32[128,2048]{1,0:T(8,128)}) custom-call(bf16[128,2048]{1,0:T(8,128)(2,1)} %get-tuple-element.53.x_ref, bf16[2048,2048]{1,0:T(8,128)(2,1)} %get-tuple-element.54.tok_ref, ...), custom_call_target="tpu_custom_call" | custom-call | tf_op jit(solution)/shard_map/attn_back/pallas_call | solution.py:616
  590.2 0.0 copy-start.6
  590.3 0.0 copy-start.4
  590.3 0.0 copy-done.3
  590.3 0.0 copy-start.2
  590.3 2.5 add.3
  592.8 0.0 copy-done.6
  592.8 0.5 slice_bitcast_fusion
  593.3 0.0 copy-done.4
  593.3 1.1 convert_element_type.21
  594.4 0.0 copy-done.2
  594.4 0.0 copy-start.1
  594.4 2.0 convert_element_type.20
  596.3 0.3 copy-done.1
  596.7 0.0 copy-start
  596.7 2.7 convert_element_type.23
  599.3 1.0 copy-done
  600.4 0.0 copy-start.5
  600.4 4.2 convert_element_type.22
  604.6 0.0 copy-done.5
  604.6 0.8 copy.23
  (2 shorter events, 0.0 us)
Async XLA Ops:
  410.3 179.9 %copy-start.3 = (f32[128,2048]{1,0:T(8,128)S(1)}, f32[128,2048]{1,0:T(8,128)}, u32[]{:S(2)}) copy-start(f32[128,2048]{1,0:T(8,128)} %get-tuple-element.52) | copy-start | bytes 3145732
  590.2 2.5 copy-start.6
  590.3 3.0 copy-start.4
  590.3 4.1 copy-start.2
  594.4 2.3 copy-start.1
  596.7 3.7 copy-start
  600.4 4.2 copy-start.5

commit v7 on v6

--- a/solution.py
+++ b/solution.py
@@ -681,10 +681,11 @@
 def rope_of(spots, table):
     count = spots.shape[0]
     lane = lax.broadcasted_iota(jnp.int32, (count, count), 1)
-    pick = jnp.where(lane.astype(F32) == spots, 1.0, 0.0).astype(F32)
-    both = jnp.dot(pick, table, preferred_element_type=F32, precision=lax.Precision.HIGHEST)
-    half = both.shape[1] // 2
-    return both[:, :half], both[:, half:]
+    pick = jnp.where(lane.astype(F32) == spots, 1.0, 0.0).astype(BF)
+    parts = mm(pick, table)
+    n = parts.shape[1] // 3
+    both = parts[:, :n] + parts[:, n : 2 * n] + parts[:, 2 * n :]
+    return both[:, : n // 2], both[:, n // 2 :]
 
 
 def row_sums(x):
@@ -724,9 +725,9 @@
 def attn_kernel(
     n_shard, n_rep, heads,
     x_ref, aux_ref, wqkv_ref, wo_ref, wgu_ref, table_ref,
-    g_ref, wq_ref, wg_ref, auxg_ref, sums_ref, hats_ref, rot_ref, prob_ref, ctx_ref,
+    g_ref, wq_ref, wg_ref, auxg_ref, sums_ref, hats_out, rot_out, prob_out, ctx_out,
     out_ref, scale_ref, resid_ref, residb_ref,
-    row, buf, wq, stage, qkv, stats, got, lsem, osem, xs, xr, as_, ar, *rest,
+    hats_ref, rot_ref, prob_ref, ctx_ref, row, buf, wq, stage, qkv, stats, got, packed, lsem, osem, xs, xr, as_, ar, *rest,
 ):
     pos = position(n_shard)
     gsems, c3, c2, bufs, ssems = rest[:5], rest[5:10], rest[10:15], rest[15:19], rest[19:]
@@ -790,9 +791,10 @@
     qkv_w.finish()
     keep = load(wq, wq_ref, lsem.at[1])
     lax.fori_loop(0, chips, project, 0)
-    exchange_start(n_shard, stats, got, xs, xr)
+    packed[...] = stats[...].astype(BF)
+    exchange_start(n_shard, packed, got, xs, xr)
     gu_w.start(1, 0, half)
-    exchange_finish(n_shard, stats, got, xs, xr, sums_ref)
+    exchange_finish(n_shard, stats, packed, got, xs, xr, sums_ref)
 
     def aux_done(k, _):
         aux_desc(k).wait_recv()
@@ -838,6 +840,10 @@
         return 0
 
     lax.fori_loop(0, n_shard, attend, 0, unroll=UNROLL)
+    kept = [
+        load(hats_ref, hats_out, lsem.at[2]), load(rot_ref, rot_out, lsem.at[3]),
+        load(prob_ref, prob_out, lsem.at[4]), load(ctx_ref, ctx_out, lsem.at[5]),
+    ]
 
     def partial(q):
         r = rows_of(q, big)
@@ -866,6 +872,8 @@
     norm_rows(count, close)
     gu_w.finish()
     keep.wait()
+    for cp in kept:
+        cp.wait()
     wait_all([out_x], chips)
 
 
@@ -882,18 +890,18 @@
     lax.fori_loop(1, n_shard, start, 0)
 
 
-def exchange_finish(n_shard, stats, got, xs, xr, sums):
+def exchange_finish(n_shard, stats, packed, got, xs, xr, sums):
     sums[...] = stats[...]
 
     def take(k, _):
-        exchange_desc(n_shard, stats, got, xs, xr, k).wait_recv()
-        sums[...] += got[k - 1]
+        exchange_desc(n_shard, packed, got, xs, xr, k).wait_recv()
+        sums[...] += got[k - 1].astype(F32)
         return 0
 
     lax.fori_loop(1, n_shard, take, 0)
 
     def done(k, _):
-        exchange_desc(n_shard, stats, got, xs, xr, k).wait_send()
+        exchange_desc(n_shard, packed, got, xs, xr, k).wait_send()
         return 0
 
     lax.fori_loop(1, n_shard, done, 0)
@@ -1126,10 +1134,10 @@
 
 def attn_back_kernel(
     n_shard, n_rep, heads,
-    x_ref, tok_ref, wo_ref, wq_ref, hats_ref, rot_ref, prob_ref, ctx_ref, aux_ref, sums_ref,
+    x_ref, tok_ref, wo_ref, wq_ref, hats_in, rot_in, prob_in, ctx_in, aux_ref, sums_ref,
     table_ref, gain_ref, gsum_ref, down_ref,
     gu_ref, dn_ref, go_ref, gq_ref, gains_ref, out_ref,
-    buf, tok, wq, dctx, ups, dqkv, stats, inner, got, ggot, mine_g, rgot, lsem, xs, xr, gs, gr, rs, rr, *rest,
+    hats_ref, rot_ref, prob_ref, ctx_ref, buf, tok, wq, dctx, ups, dqkv, stats, inner, got, packed, ggot, mine_g, rgot, lsem, xs, xr, gs, gr, rs, rr, *rest,
 ):
     rest = list(rest)
 
@@ -1153,6 +1161,10 @@
     r_me = lax.axis_index("rep")
     mine = load(x_ref, buf.at[own_rows(pos, count)], lsem.at[0])
     in_d = load(down_ref, dacc, lsem.at[1])
+    kept = [
+        load(hats_in, hats_ref, lsem.at[4]), load(rot_in, rot_ref, lsem.at[5]),
+        load(prob_in, prob_ref, lsem.at[6]), load(ctx_in, ctx_ref, lsem.at[7]),
+    ]
     in_t = load(tok_ref, tok, lsem.at[2])
     in_w = load(wq_ref, wq, lsem.at[3])
     share = own // n_rep
@@ -1211,6 +1223,8 @@
     root = hw ** (-0.5)
     me = lax.axis_index("shard")
     mine_g[...] = gain_ref[me]
+    for cp in kept:
+        cp.wait()
 
     def scale_of(i):
         at = pl.ds(pl.multiple_of(i * count, count), count)
@@ -1255,7 +1269,8 @@
         return 0
 
     lax.fori_loop(0, n_shard, attend, 0, unroll=UNROLL)
-    exchange_start(n_shard, stats, got, xs, xr)
+    packed[...] = stats[...].astype(BF)
+    exchange_start(n_shard, packed, got, xs, xr)
     gu_rows.start(1, early, half)
 
     def out_cols(n, _):
@@ -1274,7 +1289,7 @@
     lax.fori_loop(1, n_shard, gain_take, 0)
     for m in range(1, n_rep):
         gain_rep(m).start()
-    exchange_finish(n_shard, stats, got, xs, xr, inner)
+    exchange_finish(n_shard, stats, packed, got, xs, xr, inner)
 
     def settle(i, _):
         r = rows_of(i, count)
@@ -1346,7 +1361,7 @@
 
     scatter_loop(
         pos, count, bufs, ssems, partial, out_ref, [work0, work1, work2, work3, work4, work5, work6],
-        "0" + "f" * na + "12s3s45" + "s" * (na - 3) + "6",
+        "ff0" + "f" * (na - 2) + "12s3s45" + "s" * (na - 3) + "6",
     )
 
     def end(d, _):
@@ -1379,7 +1394,12 @@
     inverse = np.float32(THETA) ** (-(np.float32(2.0) * np.arange(half_width, dtype=np.float32)) / np.float32(head_width))
     angle = np.arange(count, dtype=np.float32)[:, None] * inverse[None, :].astype(np.float32)
     cosine, sine = np.cos(angle), np.sin(angle)
-    return np.concatenate([cosine, cosine, -sine, sine], axis=1).astype(np.float32)
+    rest = np.concatenate([cosine, cosine, -sine, sine], axis=1).astype(np.float32)
+    parts = []
+    for _ in range(3):
+        parts.append(rest.astype(BF))
+        rest = rest - parts[-1].astype(np.float32)
+    return np.concatenate(parts, axis=1)
 
 
 def make(n_rep, n_shard):
@@ -1404,6 +1424,10 @@
         )
         table = jnp.asarray(rope_table(count, hw))
         chunk = n_shard - 1
+        saved = [
+            pltpu.VMEM((total, 2 * own), F32), pltpu.VMEM((total, 3 * own), BF),
+            pltpu.VMEM((total, heads * count), F32), pltpu.VMEM((total, own), BF),
+        ]
         (
             tokens_g, wq, wg, auxg, squares, hats, rots, probs, context_b,
             attn_hat, attn_scale, resid, resid_b,
@@ -1411,17 +1435,17 @@
             functools.partial(attn_kernel, n_shard, n_rep, heads), "attn", 1,
             [
                 ((total, width), BF, ANY), ((width, 3 * own), BF, ANY), ((width, 2 * ff), BF, ANY),
-                ((n_shard, 8, count), F32, VM), ((2, total), F32, VM), ((total, 2 * own), F32, VM),
-                ((total, 3 * own), BF, VM), ((total, heads * count), F32, VM),
-                ((total, own), BF, VM), ((count, width), F32, VM), ((count, 128), F32, VM),
+                ((n_shard, 8, count), F32, VM), ((2, total), F32, VM), ((total, 2 * own), F32, ANY),
+                ((total, 3 * own), BF, ANY), ((total, heads * count), F32, ANY),
+                ((total, own), BF, ANY), ((count, width), F32, VM), ((count, 128), F32, VM),
                 ((count, width), F32, VM), ((count, width), BF, VM),
             ],
             [ANY, VM, ANY, VM, ANY, VM],
-            [
+            saved + [
                 pltpu.VMEM((1, width), F32), gathered, pltpu.VMEM((width, 3 * own), BF), pltpu.VMEM((own, 2 * ff), BF),
                 pltpu.VMEM((total, 3 * own), F32), pltpu.VMEM((2, total), F32),
-                pltpu.VMEM((chunk, 2, total), F32),
-                DMA((2,)), DMA((chips,)), DMA((chunk,)), DMA((chunk,)), DMA((chunk,)), DMA((chunk,)),
+                pltpu.VMEM((chunk, 2, total), BF), pltpu.VMEM((2, total), BF),
+                DMA((6,)), DMA((chips,)), DMA((chunk,)), DMA((chunk,)), DMA((chunk,)), DMA((chunk,)),
             ] + gather_sems(n_shard) + columns_sems(n_shard, n_rep, 3)
             + columns_sems(n_shard, n_rep, 2)
             + scatter_bufs(n_shard, count, width) + scatter_sems(n_shard),
@@ -1467,15 +1491,15 @@
                 ((own, n_shard * 2 * ff), BF, ANY), ((ff, width), BF, ANY), ((own, width), BF, ANY),
                 ((own, 3 * width), BF, ANY), ((8, own), F32, VM), ((count, width), F32, VM),
             ],
-            [ANY, ANY, VM, ANY, VM, VM, VM, VM, VM, VM, VM, VM, ANY, ANY],
-            [
+            [ANY, ANY, VM, ANY, ANY, ANY, ANY, ANY, VM, VM, VM, VM, ANY, ANY],
+            saved + [
                 gathered, gathered, pltpu.VMEM((width, 3 * own), BF), pltpu.VMEM((total, own), BF),
                 pltpu.VMEM((total, 2 * own), F32), pltpu.VMEM((total, 3 * own), BF),
                 pltpu.VMEM((2, total), F32),
-                pltpu.VMEM((2, total), F32), pltpu.VMEM((chunk, 2, total), F32),
-                pltpu.VMEM((chunk, 8, own), F32), pltpu.VMEM((8, own), F32),
+                pltpu.VMEM((2, total), F32), pltpu.VMEM((chunk, 2, total), BF),
+                pltpu.VMEM((2, total), BF), pltpu.VMEM((chunk, 8, own), F32), pltpu.VMEM((8, own), F32),
                 pltpu.VMEM((n_rep - 1, 8, own), F32),
-                DMA((4,)), DMA((chunk,)), DMA((chunk,)), DMA((chunk,)), DMA((chunk,)),
+                DMA((8,)), DMA((chunk,)), DMA((chunk,)), DMA((chunk,)), DMA((chunk,)),
                 DMA((n_rep - 1,)), DMA((n_rep - 1,)),
             ] + gather_sems(n_shard) + scatter_bufs(n_shard, count, width) + scatter_sems(n_shard)
             + share_scratch(ff, width, 1, n_rep) + share_scratch(own, width, 1, n_rep)

time: 606 us -> 596 us (0.983)
  Pallas kernels: 587 us -> 575 us
    pallas_call x4, Pallas kernels: 587 us -> 575 us  [call(): pl.pallas_call(kernel, name=name, out_shape=[jax.ShapeDtypeStruct(shape,...]
where the time goes in v7:
time: 596 us; the launch traced here: 594 us
  Pallas kernels  575 us (96%)
  other arithmetic  14.4 us (2%)
    pallas_call x4, Pallas kernels, call(): pl.pallas_call(kernel, name=name, out_shape=[jax.ShapeDtypeStruct(shape,...  575 us

profile of v7, /device:TPU:0, one launch (start us, length us, event | category | flops | bytes accessed | tf_op | source)
XLA Modules:
  0.0 593.6 jit_solution(16208251282191187002)
XLA Ops:
  0.6 0.7 convert_bitcast_fusion
  1.3 0.7 bitcast_convert_fusion
  2.0 0.7 bitcast_convert_fusion.2
  2.7 0.6 stack.43.aux_ref
  3.3 168.5 %attn.1 = (bf16[2048,2048]{1,0:T(8,128)(2,1)}, bf16[2048,384]{1,0:T(8,128)(2,1)}, bf16[2048,1024]{1,0:T(8,128)(2,1)}, f32[16,8,128]{2,1,0:T(8,128)}, f32[2,2048]...) custom-call(bf16[128,2048]{1,0:T(8,128)(2,1)} %x_ref.1, ...), custom_call_target="tpu_custom_call" | custom-call | tf_op jit(solution)/shard_map/attn/pallas_call | solution.py:616
  171.8 110.4 %mlp.1 = (bf16[2048,2048]{1,0:T(8,128)(2,1)}, bf16[2048,1024]{1,0:T(8,128)(2,1)}, bf16[2048,512]{1,0:T(8,128)(2,1)}, bf16[128,2048]{1,0:T(8,128)(2,1)}, bf16[128,2048]{1,0:T(8,128)(2,1)}, /*index=5*/f32[1,2048]{1,0:T(1,128)}) custom-call(bf16[128,2048]{1,0:T(8,128)(2,1)} %get-tuple-element.40.x_ref, bf16[2048,1024]{1,0:T(8,128)(2,1)} %get-tuple-element.41.wg_ref, ...), custom_call_target="tpu_custom_call" | custom-call | tf_op jit(solution)/shard_map/mlp/pallas_call | solution.py:616
  282.2 124.5 %mlp_back.1 = (bf16[1024,1024]{1,0:T(8,128)(2,1)}, bf16[512,2048]{1,0:T(8,128)(2,1)}, f32[128,2048]{1,0:T(8,128)}, bf16[128,2048]{1,0:T(8,128)(2,1)}, f32[16,8,128]{2,1,0:T(8,128)}) custom-call(bf16[128,2048]{1,0:T(8,128)(2,1)} %get-tuple-element.45.x_ref, bf16[2048,1024]{1,0:T(8,128)(2,1)} %get-tuple-element.46.gu_ref, ...), custom_call_target="tpu_custom_call" | custom-call | tf_op jit(solution)/shard_map/mlp_back/pallas_call | solution.py:616
  406.7 0.0 copy-start.3
  406.7 171.8 %attn_back.1 = (bf16[128,16384]{1,0:T(8,128)(2,1)}, bf16[512,2048]{1,0:T(8,128)(2,1)}, bf16[128,2048]{1,0:T(8,128)(2,1)}, bf16[128,6144]{1,0:T(8,128)(2,1)}, f32[8,128]{1,0:T(8,128)}, /*index=5*/f32[128,2048]{1,0:T(8,128)}) custom-call(bf16[128,2048]{1,0:T(8,128)(2,1)} %get-tuple-element.53.x_ref, bf16[2048,2048]{1,0:T(8,128)(2,1)} %get-tuple-element.54.tok_ref, ...), custom_call_target="tpu_custom_call" | custom-call | tf_op jit(solution)/shard_map/attn_back/pallas_call | solution.py:616
  578.5 0.0 copy-start.6
  578.5 0.0 copy-start.4
  578.5 0.0 copy-done.3
  578.5 0.0 copy-start.2
  578.5 2.5 add.3
  581.0 0.0 copy-done.6
  581.0 0.5 slice_bitcast_fusion
  581.5 0.0 copy-done.4
  581.5 1.1 convert_element_type.21
  582.6 0.0 copy-done.2
  582.6 0.0 copy-start.1
  582.6 2.0 convert_element_type.20
  584.6 0.3 copy-done.1
  584.9 0.0 copy-start
  584.9 2.7 convert_element_type.23
  587.6 1.0 copy-done
  588.6 0.0 copy-start.5
  588.6 4.2 convert_element_type.22
  592.8 0.0 copy-done.5
  592.9 0.8 copy.23
  (2 shorter events, 0.0 us)
Async XLA Ops:
  406.7 171.8 %copy-start.3 = (f32[128,2048]{1,0:T(8,128)S(1)}, f32[128,2048]{1,0:T(8,128)}, u32[]{:S(2)}) copy-start(f32[128,2048]{1,0:T(8,128)} %get-tuple-element.52) | copy-start | bytes 3145732
  578.5 2.5 copy-start.6
  578.5 3.0 copy-start.4
  578.5 4.1 copy-start.2
  582.6 2.3 copy-start.1
  584.9 3.7 copy-start
  588.6 4.2 copy-start.5

commit v8 on v7

--- a/solution.py
+++ b/solution.py
@@ -99,7 +99,7 @@
     ]
 
 
-def gather_loop(pos, count, buf, sems, on_chip, hook=None):
+def gather_loop(pos, count, buf, sems, on_chip, hook=None, late=None):
     recv, up, down, ysend, csend = sems
     a, b, c, na = pos
     rows = count // CHUNKS
@@ -156,6 +156,8 @@
         return 0
 
     lax.fori_loop(0, na, step, 0)
+    if late is not None:
+        late()
     pair_step(line_order(na - 1, a, na), na)
 
     def finish(j, _):
@@ -765,15 +767,18 @@
 
             lax.fori_loop(1, n_shard, one, 0)
 
+        @pl.when(t == na - 2)
+        def _():
+            qkv_w.forward(0, 1, half)
+            qkv_w.forward(1, 0, half)
+
         @pl.when(t == na - 1)
         def _():
             gu_w.start(0, 1, half)
-            qkv_w.forward(0, 1, half)
-            qkv_w.forward(1, 0, half)
 
     half = n_shard // 2
 
-    def project(q, _):
+    def project(q):
         r = rows_of(q, big)
         v = mm(buf[r, :], wq[...])
         qkv[r, :] = v
@@ -781,19 +786,30 @@
             x = v[:, g * own : (g + 1) * own]
             stats[pl.ds(g, 1), pl.ds(pl.multiple_of(q * big, big), big)] = row_sums(x * x)
 
-        @pl.when(q > 0)
-        def _():
-            gu_w.forward(0, q, q + 1)
-
-        return 0
-
-    gather_loop(pos, count, buf, gsems, lambda q, t: out_x.start(q), hook)
-    qkv_w.finish()
+
+    a, b = pos[:2]
+
+    def late():
+        qkv_w.finish()
+
+        def there(u, _):
+            project(line_order(u, a, na) * 2 + b)
+
+            @pl.when(u < na - 1)
+            def _():
+                project(line_order(u, a, na) * 2 + 1 - b)
+
+            return 0
+
+        lax.fori_loop(0, na, there, 0)
+
+    gather_loop(pos, count, buf, gsems, lambda q, t: out_x.start(q), hook, late)
     keep = load(wq, wq_ref, lsem.at[1])
-    lax.fori_loop(0, chips, project, 0)
+    project(line_order(na - 1, a, na) * 2 + 1 - b)
     packed[...] = stats[...].astype(BF)
     exchange_start(n_shard, packed, got, xs, xr)
     gu_w.start(1, 0, half)
+    gu_w.forward(0, 1, half)
     exchange_finish(n_shard, stats, packed, got, xs, xr, sums_ref)
 
     def aux_done(k, _):

time: 596 us -> 590 us (0.990)
  no operation moved by 1% of the time
where the time goes in v8:
time: 590 us; the launch traced here: 589 us
  Pallas kernels  570 us (97%)
  other arithmetic  14.4 us (2%)
    pallas_call x4, Pallas kernels, call(): pl.pallas_call(kernel, name=name, out_shape=[jax.ShapeDtypeStruct(shape,...  570 us

profile of v8, /device:TPU:0, one launch (start us, length us, event | category | flops | bytes accessed | tf_op | source)
XLA Modules:
  0.0 588.8 jit_solution(4878374333729172649)
XLA Ops:
  0.6 0.7 convert_bitcast_fusion
  1.3 0.7 bitcast_convert_fusion
  2.0 0.7 bitcast_convert_fusion.2
  2.7 0.6 stack.43.aux_ref
  3.3 162.7 %attn.1 = (bf16[2048,2048]{1,0:T(8,128)(2,1)}, bf16[2048,384]{1,0:T(8,128)(2,1)}, bf16[2048,1024]{1,0:T(8,128)(2,1)}, f32[16,8,128]{2,1,0:T(8,128)}, f32[2,2048]...) custom-call(bf16[128,2048]{1,0:T(8,128)(2,1)} %x_ref.1, ...), custom_call_target="tpu_custom_call" | custom-call | tf_op jit(solution)/shard_map/attn/pallas_call | solution.py:618
  165.9 110.3 %mlp.1 = (bf16[2048,2048]{1,0:T(8,128)(2,1)}, bf16[2048,1024]{1,0:T(8,128)(2,1)}, bf16[2048,512]{1,0:T(8,128)(2,1)}, bf16[128,2048]{1,0:T(8,128)(2,1)}, bf16[128,2048]{1,0:T(8,128)(2,1)}, /*index=5*/f32[1,2048]{1,0:T(1,128)}) custom-call(bf16[128,2048]{1,0:T(8,128)(2,1)} %get-tuple-element.40.x_ref, bf16[2048,1024]{1,0:T(8,128)(2,1)} %get-tuple-element.41.wg_ref, ...), custom_call_target="tpu_custom_call" | custom-call | tf_op jit(solution)/shard_map/mlp/pallas_call | solution.py:618
  276.3 124.5 %mlp_back.1 = (bf16[1024,1024]{1,0:T(8,128)(2,1)}, bf16[512,2048]{1,0:T(8,128)(2,1)}, f32[128,2048]{1,0:T(8,128)}, bf16[128,2048]{1,0:T(8,128)(2,1)}, f32[16,8,128]{2,1,0:T(8,128)}) custom-call(bf16[128,2048]{1,0:T(8,128)(2,1)} %get-tuple-element.45.x_ref, bf16[2048,1024]{1,0:T(8,128)(2,1)} %get-tuple-element.46.gu_ref, ...), custom_call_target="tpu_custom_call" | custom-call | tf_op jit(solution)/shard_map/mlp_back/pallas_call | solution.py:618
  400.8 0.0 copy-start.3
  400.8 172.9 %attn_back.1 = (bf16[128,16384]{1,0:T(8,128)(2,1)}, bf16[512,2048]{1,0:T(8,128)(2,1)}, bf16[128,2048]{1,0:T(8,128)(2,1)}, bf16[128,6144]{1,0:T(8,128)(2,1)}, f32[8,128]{1,0:T(8,128)}, /*index=5*/f32[128,2048]{1,0:T(8,128)}) custom-call(bf16[128,2048]{1,0:T(8,128)(2,1)} %get-tuple-element.53.x_ref, bf16[2048,2048]{1,0:T(8,128)(2,1)} %get-tuple-element.54.tok_ref, ...), custom_call_target="tpu_custom_call" | custom-call | tf_op jit(solution)/shard_map/attn_back/pallas_call | solution.py:618
  573.7 0.0 copy-start.6
  573.7 0.0 copy-start.4
  573.7 0.0 copy-done.3
  573.7 0.0 copy-start.2
  573.7 2.5 add.3
  576.2 0.0 copy-done.6
  576.2 0.5 slice_bitcast_fusion
  576.7 0.0 copy-done.4
  576.7 1.1 convert_element_type.21
  577.8 0.0 copy-done.2
  577.8 0.0 copy-start.1
  577.8 2.0 convert_element_type.20
  579.8 0.3 copy-done.1
  580.1 0.0 copy-start
  580.1 2.7 convert_element_type.23
  582.8 1.0 copy-done
  583.8 0.0 copy-start.5
  583.8 4.2 convert_element_type.22
  588.0 0.0 copy-done.5
  588.0 0.8 copy.23
  (2 shorter events, 0.0 us)
Async XLA Ops:
  400.8 172.9 %copy-start.3 = (f32[128,2048]{1,0:T(8,128)S(1)}, f32[128,2048]{1,0:T(8,128)}, u32[]{:S(2)}) copy-start(f32[128,2048]{1,0:T(8,128)} %get-tuple-element.52) | copy-start | bytes 3145732
  573.7 2.5 copy-start.6
  573.7 3.0 copy-start.4
  573.7 4.1 copy-start.2
  577.8 2.3 copy-start.1
  580.1 3.7 copy-start
  583.8 4.2 copy-start.5

commit v9 on v8

--- a/solution.py
+++ b/solution.py
@@ -1233,9 +1233,6 @@
         r = rows_of(q, big)
         dctx[r, :] = mm_nt(buf[r, :], wo_ref[...]).astype(BF)
 
-    gather_loop(pos, count, buf, gsems, on_chip, hook)
-    early = half * 5 // 8
-    gu_rows.start(1, 0, early)
     root = hw ** (-0.5)
     me = lax.axis_index("shard")
     mine_g[...] = gain_ref[me]
@@ -1246,7 +1243,7 @@
         at = pl.ds(pl.multiple_of(i * count, count), count)
         return lax.rsqrt(sums_ref[:, at] / width + EPSILON)
 
-    def attend(i, _):
+    def attend(i):
         r = rows_of(i, count)
         at = pl.ds(pl.multiple_of(i * count, count), count)
         cos, sin = rope_of(spots_of(aux_ref[i, 0:1, :], count)[1], table_ref[...])
@@ -1278,16 +1275,32 @@
         for g in range(2):
             stats[pl.ds(g, 1), at] = totals[g]
 
-        @pl.when((i > 0) & (i < half))
-        def _():
-            gu_rows.forward(0, i, i + 1)
-
-        return 0
-
-    lax.fori_loop(0, n_shard, attend, 0, unroll=UNROLL)
+    def attend_chip(q):
+        attend(q * 2)
+        attend(q * 2 + 1)
+
+    a, b = pos[:2]
+
+    def late():
+        def there(u, _):
+            attend_chip(line_order(u, a, na) * 2 + b)
+
+            @pl.when(u < na - 1)
+            def _():
+                attend_chip(line_order(u, a, na) * 2 + 1 - b)
+
+            return 0
+
+        lax.fori_loop(0, na, there, 0)
+
+    gather_loop(pos, count, buf, gsems, on_chip, hook, late)
+    early = half * 5 // 8
+    gu_rows.start(1, 0, early)
+    attend_chip(line_order(na - 1, a, na) * 2 + 1 - b)
     packed[...] = stats[...].astype(BF)
     exchange_start(n_shard, packed, got, xs, xr)
     gu_rows.start(1, early, half)
+    gu_rows.forward(0, 1, half)
 
     def out_cols(n, _):
         lo = rows_of(n, 256)

time: 590 us -> 596 us (1.010)
  no operation moved by 1% of the time
where the time goes in v9:
time: 596 us; the launch traced here: 593 us
  Pallas kernels  575 us (96%)
  other arithmetic  14.4 us (2%)
    pallas_call x4, Pallas kernels, call(): pl.pallas_call(kernel, name=name, out_shape=[jax.ShapeDtypeStruct(shape,...  575 us

profile of v9, /device:TPU:0, one launch (start us, length us, event | category | flops | bytes accessed | tf_op | source)
XLA Modules:
  0.0 593.3 jit_solution(189429562288155738)
XLA Ops:
  0.6 0.7 convert_bitcast_fusion
  1.3 0.7 bitcast_convert_fusion
  2.0 0.7 bitcast_convert_fusion.2
  2.7 0.6 stack.43.aux_ref
  3.3 162.7 %attn.1 = (bf16[2048,2048]{1,0:T(8,128)(2,1)}, bf16[2048,384]{1,0:T(8,128)(2,1)}, bf16[2048,1024]{1,0:T(8,128)(2,1)}, f32[16,8,128]{2,1,0:T(8,128)}, f32[2,2048]...) custom-call(bf16[128,2048]{1,0:T(8,128)(2,1)} %x_ref.1, ...), custom_call_target="tpu_custom_call" | custom-call | tf_op jit(solution)/shard_map/attn/pallas_call | solution.py:618
  165.9 110.3 %mlp.1 = (bf16[2048,2048]{1,0:T(8,128)(2,1)}, bf16[2048,1024]{1,0:T(8,128)(2,1)}, bf16[2048,512]{1,0:T(8,128)(2,1)}, bf16[128,2048]{1,0:T(8,128)(2,1)}, bf16[128,2048]{1,0:T(8,128)(2,1)}, /*index=5*/f32[1,2048]{1,0:T(1,128)}) custom-call(bf16[128,2048]{1,0:T(8,128)(2,1)} %get-tuple-element.40.x_ref, bf16[2048,1024]{1,0:T(8,128)(2,1)} %get-tuple-element.41.wg_ref, ...), custom_call_target="tpu_custom_call" | custom-call | tf_op jit(solution)/shard_map/mlp/pallas_call | solution.py:618
  276.3 124.5 %mlp_back.1 = (bf16[1024,1024]{1,0:T(8,128)(2,1)}, bf16[512,2048]{1,0:T(8,128)(2,1)}, f32[128,2048]{1,0:T(8,128)}, bf16[128,2048]{1,0:T(8,128)(2,1)}, f32[16,8,128]{2,1,0:T(8,128)}) custom-call(bf16[128,2048]{1,0:T(8,128)(2,1)} %get-tuple-element.45.x_ref, bf16[2048,1024]{1,0:T(8,128)(2,1)} %get-tuple-element.46.gu_ref, ...), custom_call_target="tpu_custom_call" | custom-call | tf_op jit(solution)/shard_map/mlp_back/pallas_call | solution.py:618
  400.8 0.0 copy-start.3
  400.8 177.3 %attn_back.1 = (bf16[128,16384]{1,0:T(8,128)(2,1)}, bf16[512,2048]{1,0:T(8,128)(2,1)}, bf16[128,2048]{1,0:T(8,128)(2,1)}, bf16[128,6144]{1,0:T(8,128)(2,1)}, f32[8,128]{1,0:T(8,128)}, /*index=5*/f32[128,2048]{1,0:T(8,128)}) custom-call(bf16[128,2048]{1,0:T(8,128)(2,1)} %get-tuple-element.53.x_ref, bf16[2048,2048]{1,0:T(8,128)(2,1)} %get-tuple-element.54.tok_ref, ...), custom_call_target="tpu_custom_call" | custom-call | tf_op jit(solution)/shard_map/attn_back/pallas_call | solution.py:618
  578.1 0.0 copy-start.6
  578.1 0.0 copy-start.4
  578.1 0.0 copy-done.3
  578.1 0.0 copy-start.2
  578.1 2.5 add.3
  580.6 0.0 copy-done.6
  580.6 0.5 slice_bitcast_fusion
  581.1 0.0 copy-done.4
  581.1 1.1 convert_element_type.21
  582.2 0.0 copy-done.2
  582.2 0.0 copy-start.1
  582.2 2.0 convert_element_type.20
  584.2 0.3 copy-done.1
  584.5 0.0 copy-start
  584.5 2.7 convert_element_type.23
  587.2 1.0 copy-done
  588.2 0.0 copy-start.5
  588.2 4.2 convert_element_type.22
  592.5 0.0 copy-done.5
  592.5 0.8 copy.23
  (2 shorter events, 0.0 us)
Async XLA Ops:
  400.8 177.4 %copy-start.3 = (f32[128,2048]{1,0:T(8,128)S(1)}, f32[128,2048]{1,0:T(8,128)}, u32[]{:S(2)}) copy-start(f32[128,2048]{1,0:T(8,128)} %get-tuple-element.52) | copy-start | bytes 3145732
  578.1 2.5 copy-start.6
  578.1 3.0 copy-start.4
  578.1 4.1 copy-start.2
  582.2 2.3 copy-start.1
  584.5 3.7 copy-start
  588.2 4.2 copy-start.5
